TPU v7x, 32 devices: a whole 2x2x4 slice. The times are simulated.
32 devices in a mesh: visit: 4 (over z), bulk: 8 (over y, x, core).
Axes of the slice: x: 2, y: 2, z: 4, core: 2. Of those that a mesh axis runs over, the one named last changes fastest.
Arguments:
- piece_flux: float32 [4, 8, 8, 128, 128], P('visit', 'bulk'), may hold values from -6 to 6
- piece_ivar: float32 [4, 8, 8, 128, 128], P('visit', 'bulk'), may hold values from 0.5 to 8
- warp_rows: float32 [4, 8, 8, 128, 128], P('visit', 'bulk'), may hold values from 0 to 1, as said below
- warp_cols: float32 [4, 8, 8, 128, 128], P('visit', 'bulk'), may hold values from 0 to 1, as said below
- piece_owner: int32 [4, 8, 8, 1], P('visit', 'bulk'), may hold values from 0 to 7; in each aligned block of 8 rows (0 to 7, 8 to 15, ..., all dimensions but the last counted through in order) at most 2 rows name the same one
- piece_slot: int32 [4, 8, 8], P('visit', 'bulk'), may hold values from 0 to 15
- piece_extent: int32 [4, 8, 8, 2], P('visit', 'bulk'), may hold values from 64 to 128
- basis: float32 [4, 128, 128], replicated, may hold values from -0.046875 to 0.046875
- coeffs: float32 [4, 4], P('visit'), may hold values from -4 to 4
Outputs:
- coadd: float32 [2048, 1024], P('bulk', 'visit')
- weight_map: float32 [2048, 1024], P('bulk', 'visit')
Inputs may be any that keep to these rules, and one draw needn't show every extreme that they name: `piece_owner`: among the pieces on one device, no owner is named by more than 2 pieces, a bound that some block reaches. `warp_rows`: entries are nonnegative and each row sums to one. `warp_cols`: entries are nonnegative and each row sums to one.
All inputs are finite; a program needn't handle non-finite values.
Results may differ from a plain program's by a relative error of at most 0.0003.
Values sent between devices are 32-bit elements; how exact they have to be, the bound alone decides.
No kernel may reach another device: no remote copies, remote signals or barrier semaphores. Data moves between devices by JAX's collectives and lax.ppermute only.
A program may use at most 128 MiB of HBM per device.

v0:
```python
import functools
import math

import jax
import jax.numpy as jnp
import numpy as np
from jax import lax
from jax.experimental import pallas as pl
from jax.experimental.pallas import tpu as pltpu
from jax.sharding import PartitionSpec as P


HALO = 64
BR = 2
BC = 8
CAP = 2
LANES = 128
META = 8


F32 = jnp.float32
BF16 = jnp.bfloat16
VMEM = pl.BlockSpec(memory_space=pltpu.VMEM)
SMEM = pl.BlockSpec(memory_space=pltpu.SMEM)


def split(value):
    high = value.astype(BF16)
    low = (value - high.astype(F32)).astype(BF16)
    return high, low


def data(value, axis):
    high, low = split(value)
    return jnp.concatenate([high, low, high], axis)


def weights(value, axis):
    high, low = split(value)
    return jnp.concatenate([high, high, low], axis)


def table(value, axis):
    value = np.asarray(value, np.float32)
    high = value.astype(jnp.bfloat16)
    low = (value - high.astype(np.float32)).astype(jnp.bfloat16)
    return np.concatenate([high, high, low], axis)


def dot(a, b, dims=((1,), (0,))):
    return lax.dot_general(a, b, (dims, ((), ())), preferred_element_type=F32)


@functools.lru_cache
def make_tables(rows_dev, taps):
    length = rows_dev + taps - 1
    freqs = (length + 1) // 2
    k = np.arange(freqs)[:, None]

    def wave(first, second, period):
        return 2.0 * math.pi * ((first * second) % period) / period

    n = np.arange(rows_dev + 2 * HALO)[None, :] - 1
    theta = wave(k, n, length)
    used = n >= 0
    row_fwd = np.concatenate([np.cos(theta) * used, -np.sin(theta) * used], 0)
    theta = wave(k, np.arange(taps)[None, :], length)
    row_ker = np.concatenate([np.cos(theta), -np.sin(theta)], 0)
    period = 2 * taps
    n = np.arange(taps)[:, None]
    f = np.arange(taps)[None, :]
    col_fwd = []
    col_inv = []
    for odd in (0, 1):
        theta = wave(n, 2 * f + odd, period)
        c, s = np.cos(theta), np.sin(theta)
        col_fwd.append(np.block([[c, -s], [s, c]]))
        c, s = c.T, s.T
        sign = -1.0 if odd else 1.0
        col_inv.append(sign * np.block([[c, s], [-s, c]]))
    p = np.arange(rows_dev)[:, None] + taps - 1
    theta = wave(p, k.T, length)
    weight = np.where(k.T == 0, 1.0, 2.0) / (length * period)
    row_inv = np.concatenate([weight * np.cos(theta), -weight * np.sin(theta)], 1)
    return (
        table(row_fwd, 1),
        table(row_ker, 1),
        np.stack([table(t, 0) for t in col_fwd]),
        np.stack([table(t, 0) for t in col_inv]),
        table(row_inv, 1),
    )


def partner(me, other):
    return jnp.bitwise_xor(me, other)


OWNER, SLOT, ROWS, COLS, ME, ORDER = range(6)


def places(info, pieces):
    for q in range(pieces):
        own = info[OWNER, q]
        rank = jnp.int32(0)
        for earlier in range(q):
            rank = rank + (info[OWNER, earlier] == own).astype(jnp.int32)
        yield q, partner(info[ME, 0], own), own, rank, info[SLOT, q]


def masked(info, ivar, q):
    shape = ivar.shape[3:]
    row_at = lax.broadcasted_iota(jnp.int32, shape, 0)
    col_at = lax.broadcasted_iota(jnp.int32, shape, 1)
    valid = (row_at < info[ROWS, q]) & (col_at < info[COLS, q])
    return jnp.where(valid, ivar[0, 0, q], 0.0)


def warp(plane, rows, cols):
    mid = dot(data(plane, 1), weights(cols, 1), ((1,), (1,)))
    return dot(weights(rows, 1), data(mid, 0))


def run(copies):
    for copy in copies:
        copy.start()
    for copy in copies:
        copy.wait()


def warp_weight_body(info, ivar, rows, cols, *rest):
    pieces, side, _ = ivar.shape[2:]
    *outs, send, sems = rest
    for d in range(len(outs)):
        for rank in range(CAP):
            send[d, rank, side:, :] = jnp.full((META, side), -1.0, F32)
    for q, to, _, rank, at in places(info, pieces):
        send[to, rank, :side, :] = warp(masked(info, ivar, q), rows[0, 0, q], cols[0, 0, q])
        send[to, rank, side:, :] = jnp.full((META, side), at.astype(F32), F32)
    run([pltpu.make_async_copy(send.at[d], out, sems.at[d]) for d, out in enumerate(outs)])


def warp_flux_body(info, flux, ivar, rows, cols, *rest):
    pieces, side, _ = ivar.shape[2:]
    half = side // 2
    *outs, inner, send, send_inner, sems = rest
    for q, to, own, rank, at in places(info, pieces):
        first = (at // BC) * half
        maps = jnp.concatenate([rows[0, 0, q, pl.ds(first, half), :], rows[0, 0, q, pl.ds(half - first, half), :]], 0)
        done = warp(masked(info, ivar, q) * flux[0, 0, q], maps, cols[0, 0, q])
        send[to, rank] = done[:half]
        send_inner[own * CAP + rank] = done[half:]
    copies = [pltpu.make_async_copy(send.at[d], out, sems.at[d]) for d, out in enumerate(outs)]
    run(copies + [pltpu.make_async_copy(send_inner, inner, sems.at[len(outs)])])


def weight_body(info, *rest):
    *rest, slot_out, acc = rest
    count = slot_out.shape[0] // CAP
    got, out = rest[:count], rest[count:]
    side = acc.shape[1]
    spare = acc.shape[0] - 1
    per_tile = out[0].shape[0]
    slots = []
    for d in range(count):
        for rank in range(CAP):
            at = jnp.max(got[d][rank, side:, :]).astype(jnp.int32)
            slots.append(jnp.where(at < 0, spare, at))
    acc[...] = jnp.zeros(acc.shape, F32)
    for n, at in enumerate(slots):
        d, rank = divmod(n, CAP)
        slot_out[partner(info[ME, 0], d) * CAP + rank] = at
        acc[at] += got[d][rank, :side, :]
    for k in range(len(out)):
        for c in range(per_tile):
            for r in range(BR):
                out[k][c, r * side : (r + 1) * side, :] = acc[r * BC + info[ORDER, k] * per_tile + c]


def outer_body(info, slot, *rest):
    *rest, top, bottom, acc = rest
    count = slot.shape[0] // CAP
    got, tiles = rest[:count], rest[count:]
    half = acc.shape[1]
    per_tile = tiles[0].shape[0]
    acc[...] = jnp.zeros(acc.shape, F32)
    for d in range(count):
        for rank in range(CAP):
            acc[slot[partner(info[ME, 0], d) * CAP + rank]] += got[d][rank]
    for k, tile in enumerate(tiles):
        for c in range(per_tile):
            to = info[ORDER, k] * per_tile + c
            top[to] = acc[to] / jnp.maximum(tile[c, :half, :], 1.0)
            bottom[to] = acc[BC + to] / jnp.maximum(tile[c, -half:, :], 1.0)


def inner_body(info, slot, got, *rest):
    *tiles, image, acc = rest
    half = acc.shape[1]
    per_tile = tiles[0].shape[0]
    acc[...] = jnp.zeros(acc.shape, F32)
    for n in range(slot.shape[0]):
        acc[slot[n]] += got[n]
    for k, tile in enumerate(tiles):
        for c in range(per_tile):
            to = info[ORDER, k] * per_tile + c
            image[to, :half, :] = acc[to] / jnp.maximum(tile[c, half : 2 * half, :], 1.0)
            image[to, half:, :] = acc[BC + to] / jnp.maximum(tile[c, 2 * half : 3 * half, :], 1.0)


def beside(stacked):
    n = stacked.shape[0] // 2
    return jnp.concatenate([stacked[:n], stacked[n:]], 1)


def spectrum_body(coeffs, basis, row_ker, col_fwd, out):
    kernel = coeffs[0, 0] * basis[0]
    for k in range(1, basis.shape[0]):
        kernel = kernel + coeffs[0, k] * basis[k]
    lines = data(beside(dot(row_ker[...], data(kernel, 0))), 1)
    for odd in (0, 1):
        out[odd] = dot(lines, col_fwd[odd])


def conv_body(first, info, above, top, image, bottom, below, spec, row_fwd, col_fwd, col_inv, row_inv, *rest):
    *rest, lines = rest
    count = len(rest) // 2
    weight, out = rest[:count], rest[count:]
    taps = image.shape[2]
    per_tile = weight[0].shape[0]

    def column(c):
        return jnp.concatenate([above[c], top[c], image[c], bottom[c], below[c]], 0)

    def shifted(u):
        if isinstance(u, int):
            gap = jnp.zeros((above.shape[1] * 6, HALO), F32)
            left = column(u - 1)[:, taps - HALO :] if u > 0 else gap
            right = column(u)[:, :HALO] if u < BC else gap
            return jnp.concatenate([left, right], 1)
        left = column(jnp.maximum(u - 1, 0))[:, taps - HALO :]
        right = column(jnp.minimum(u, BC - 1))[:, :HALO]
        left = jnp.where(u > 0, left, 0.0)
        right = jnp.where(u < BC, right, 0.0)
        return jnp.concatenate([left, right], 1)

    one_tile = lines.shape[0] == per_tile + 1
    base = info[ORDER, first] * per_tile if one_tile else 0
    for u in range(0, lines.shape[0], 2):
        n = min(2, lines.shape[0] - u)
        ext = jnp.concatenate([shifted(base + u + i) for i in range(n)], 1)
        got = dot(row_fwd[...], data(ext, 0))
        for i in range(n):
            lines[u + i] = got[:, i * taps : (i + 1) * taps]
    for k in range(count):
        start = 0 if one_tile else info[ORDER, first + k] * per_tile
        one = [lines[start + c] for c in range(per_tile)]
        two = [lines[start + c + 1] for c in range(per_tile)]
        freqs = one[0].shape[0] // 2
        total = []
        for odd in (0, 1):
            mixed = [beside(a - b if odd else a + b) for a, b in zip(one, two)]
            freq = dot(data(jnp.concatenate(mixed, 0), 1), col_fwd[odd])
            kr = jnp.concatenate([spec[odd, :, :taps]] * per_tile, 0)
            ki = jnp.concatenate([spec[odd, :, taps:]] * per_tile, 0)
            zr, zi = freq[:, :taps], freq[:, taps:]
            prod = jnp.concatenate([zr * kr - zi * ki, zr * ki + zi * kr], 1)
            total.append(dot(data(prod, 1), col_inv[odd]))
        wave = total[0] + total[1]
        parts = [wave[c * freqs : (c + 1) * freqs] for c in range(per_tile)]
        cols = [jnp.concatenate([p[:, :taps], p[:, taps:]], 0) for p in parts]
        done = dot(row_inv[...], data(jnp.concatenate(cols, 1), 0))
        for c in range(per_tile):
            out[k][c] = done[:, c * taps : (c + 1) * taps] * weight[k][c]


def total_body(*refs):
    parts, out = refs[:-1], refs[-1]
    side = parts[0].shape[2]
    for c in range(parts[0].shape[0]):
        out[:, c * side : (c + 1) * side] = functools.reduce(jnp.add, [p[c] for p in parts])


def ratio_body(*refs):
    parts, weight, out = refs[:-2], refs[-2], refs[-1]
    side = parts[0].shape[2]
    for c in range(parts[0].shape[0]):
        cols = slice(c * side, (c + 1) * side)
        out[:, cols] = functools.reduce(jnp.add, [p[c] for p in parts]) / jnp.maximum(weight[:, cols], 1.0)


LINE = ((3, 2, 1, 0), (3, 0, 2, 1), (0, 3, 1, 2), (0, 1, 2, 3))


def send_order(count):
    if count == 4:
        return np.array(LINE, np.int32)
    return np.array([list(range(count))] * count, np.int32)


class VisitSum:
    def __init__(self, count):
        self.count = count
        self.sent = []
        self.tiles = []

    def send(self, tile, *routes):
        self.sent += [lax.ppermute(tile, "visit", route) for route in routes]

    def push(self, *tiles):
        for tile in tiles:
            k = len(self.tiles)
            self.tiles.append(tile)
            if self.count == 4:
                if k == 0:
                    self.send(tile, [(0, 1), (3, 2)])
                elif k == 1:
                    self.send(tile, [(0, 2), (1, 0), (2, 3), (3, 1)])
                elif k == 2:
                    self.send(tile, [(0, 1), (1, 2)], [(2, 1), (3, 2)])

    def parts(self):
        if self.count != 4:
            return [lax.psum_scatter(jnp.stack(self.tiles), "visit", scatter_dimension=0, tiled=False)]
        self.send(self.tiles[0] + self.sent[0], [(1, 3), (2, 0)])
        return [self.tiles[3], *self.sent[1:]]


def coadd_patches(piece_flux, piece_ivar, warp_rows, warp_cols, piece_owner, piece_slot, piece_extent, basis, coeffs):
    owners = lax.axis_size("bulk")
    visits = lax.axis_size("visit")
    pieces, side = piece_flux.shape[2:4]
    assert side == LANES and side == 2 * HALO and owners & (owners - 1) == 0
    half = side // 2
    rows_dev = BR * side
    per_tile = BC // visits
    cap = owners * CAP
    row_fwd, row_ker, col_fwd, col_inv, row_inv = [jnp.asarray(t) for t in make_tables(rows_dev, side)]
    freqs = row_fwd.shape[0] // 2
    width = max(pieces, visits)

    def line(values):
        return jnp.pad(values, (0, width - values.shape[0]))

    me = lax.axis_index("bulk").astype(jnp.int32)
    order = jnp.asarray(send_order(visits))[lax.axis_index("visit")]
    info = jnp.stack(
        [
            line(piece_owner[0, 0, :, 0]),
            line(piece_slot[0, 0]),
            line(piece_extent[0, 0, :, 0]),
            line(piece_extent[0, 0, :, 1]),
            jnp.full((width,), me),
            line(order),
        ]
    )

    def arr(*shape):
        return jax.ShapeDtypeStruct(shape, F32)

    hbm = pl.BlockSpec(memory_space=pl.ANY)

    def exchange(sent):
        got = [sent[0]]
        for d in range(1, owners):
            got.append(lax.ppermute(sent[d], "bulk", [(i, i ^ d) for i in range(owners)]))
        return got

    sent_weight = pl.pallas_call(
        warp_weight_body,
        out_shape=[arr(CAP, side + META, side)] * owners,
        in_specs=[SMEM] + [VMEM] * 3,
        out_specs=[hbm] * owners,
        scratch_shapes=[pltpu.VMEM((owners, CAP, side + META, side), F32), pltpu.SemaphoreType.DMA((owners,))],
        name="warp_weight",
    )(info, piece_ivar, warp_rows, warp_cols)
    got_weight = exchange(sent_weight)
    *sent_outer, sent_inner = pl.pallas_call(
        warp_flux_body,
        out_shape=[arr(CAP, half, side)] * owners + [arr(cap, half, side)],
        in_specs=[SMEM] + [VMEM] * 4,
        out_specs=[hbm] * (owners + 1),
        scratch_shapes=[
            pltpu.VMEM((owners, CAP, half, side), F32),
            pltpu.VMEM((cap, half, side), F32),
            pltpu.SemaphoreType.DMA((owners + 1,)),
        ],
        name="warp_flux",
    )(info, piece_flux, piece_ivar, warp_rows, warp_cols)
    got_outer = exchange(sent_outer)
    got_inner = lax.all_to_all(sent_inner, "bulk", split_axis=0, concat_axis=0, tiled=True)
    spec = pl.pallas_call(
        spectrum_body,
        out_shape=arr(2, freqs, 2 * side),
        in_specs=[SMEM] + [VMEM] * 3,
        out_specs=VMEM,
        name="spectrum",
    )(coeffs, basis, row_ker, col_fwd)
    tile = arr(per_tile, rows_dev, side)
    *ivar, slots = pl.pallas_call(
        weight_body,
        out_shape=[tile] * visits + [jax.ShapeDtypeStruct((cap,), jnp.int32)],
        in_specs=[SMEM] + [VMEM] * owners,
        out_specs=[VMEM] * visits + [SMEM],
        scratch_shapes=[pltpu.VMEM((BR * BC + 1, side, side), F32)],
        name="weights",
    )(info, *got_weight)
    weight_sum = VisitSum(visits)
    weight_sum.push(*ivar)
    scratch = [pltpu.VMEM((BR * BC + 1, half, side), F32)]
    top, bottom = pl.pallas_call(
        outer_body,
        out_shape=[arr(BC, half, side)] * 2,
        in_specs=[SMEM] * 2 + [VMEM] * (owners + visits),
        out_specs=[VMEM] * 2,
        scratch_shapes=scratch,
        name="outer",
    )(info, slots, *got_outer, *ivar)
    ends = owners - 1
    above = lax.ppermute(bottom, "bulk", [(i, i + 1) for i in range(ends)])
    below = lax.ppermute(top, "bulk", [(i + 1, i) for i in range(ends)])
    image = pl.pallas_call(
        inner_body,
        out_shape=arr(BC, side, side),
        in_specs=[SMEM] * 2 + [VMEM] * (1 + visits),
        out_specs=VMEM,
        scratch_shapes=scratch,
        name="inner",
    )(info, slots, got_inner, *ivar)
    weight_map = pl.pallas_call(
        total_body, out_shape=arr(rows_dev, per_tile * side), name="weight_map"
    )(*weight_sum.parts())

    def convolve(first, count, blocks):
        return pl.pallas_call(
            functools.partial(conv_body, first),
            out_shape=[tile] * count,
            in_specs=[SMEM] + [VMEM] * (10 + count),
            out_specs=[VMEM] * count,
            scratch_shapes=[pltpu.VMEM((blocks, 2 * freqs, side), F32)],
        )(
            info, above, top, image, bottom, below, spec, row_fwd, col_fwd, col_inv, row_inv,
            *ivar[first : first + count],
        )

    image_sum = VisitSum(visits)
    image_sum.push(*convolve(0, 1, per_tile + 1))
    image_sum.push(*convolve(1, visits - 1, BC + 1))
    coadd = pl.pallas_call(
        ratio_body, out_shape=arr(rows_dev, per_tile * side), name="coadd"
    )(*image_sum.parts(), weight_map)
    return (coadd, weight_map)


def solution(mesh):
    placed = (
        P("visit", "bulk", None, None, None),
        P("visit", "bulk", None, None, None),
        P("visit", "bulk", None, None, None),
        P("visit", "bulk", None, None, None),
        P("visit", "bulk", None, None),
        P("visit", "bulk", None),
        P("visit", "bulk", None, None),
        P(),
        P("visit", None),
    )
    return jax.shard_map(
        coadd_patches,
        mesh=mesh,
        in_specs=placed,
        out_specs=(P("bulk", "visit"), P("bulk", "visit")),
        check_vma=False,
    )
```

profile of v0, /device:TPU:0, one launch (start us, length us, event | category | flops | bytes accessed | tf_op | source)
XLA Modules:
  0.0 111.0 jit_solution(7628742505141596091)
XLA Ops:
  3.3 4.2 %warp_weight.1 = (f32[2,136,128]{2,1,0:T(8,128)}, f32[2,136,128]{2,1,0:T(8,128)}, f32[2,136,128]{2,1,0:T(8,128)}, f32[2,136,128]{2,1,0:T(8,128)}, f32[2,136,128]...) custom-call(s32[6,8]{1,0:T(8,128)} %stack.23.info, ...), custom_call_target="tpu_custom_call" | custom-call | tf_op jit(solution)/shard_map/warp_weight/pallas_call | solution.py:368
  8.0 2.6 %collective-permute-start.1 = (f32[2,136,128]{2,1,0:T(8,128)}, f32[2,136,128]{2,1,0:T(8,128)S(1)}, u32[]{:S(2)}, u32[]{:S(2)}) collective-permute-start(f32[2,136,128]{2,1,0:T(8,128)} %get-tuple-element.31), channel_id=1, source_target_pairs={{0,2},{1,3},{2,0},{3,1},{4,6},{5,7},{6,4},{7,5},{8,10},{9,11},{10,... | collective-permute-start | bytes 417800 | tf_op jit(solution)/shard_map/ppermute | solution.py:365
  10.6 4.3 %warp_flux.1 = (f32[2,64,128]{2,1,0:T(8,128)}, f32[2,64,128]{2,1,0:T(8,128)}, f32[2,64,128]{2,1,0:T(8,128)}, f32[2,64,128]{2,1,0:T(8,128)}, f32[2,64,128]{2,1,0:...) custom-call(s32[6,8]{1,0:T(8,128)} %stack.23.info, ...), custom_call_target="tpu_custom_call" | custom-call | tf_op jit(solution)/shard_map/warp_flux/pallas_call | solution.py:377
  18.5 1.9 %collective-permute-done.8.rest_2_ = f32[2,64,128]{2,1,0:T(8,128)S(1)} collective-permute-done((f32[2,64,128]{2,1,0:T(8,128)}, f32[2,64,128]{2,1,0:T(8,128)S(1)}, u32[]{:S(2)}, u32[]{:S(2)}) %collective-permute-start.8) | collective-permute-done | bytes 65568 | tf_op jit(solution)/shard_map/ppermute | solution.py:365
  21.4 3.0 %collective-permute-start.6 = (f32[2,136,128]{2,1,0:T(8,128)S(1)}, f32[2,136,128]{2,1,0:T(8,128)S(1)}, u32[]{:S(2)}, u32[]{:S(2)}) collective-permute-start(f32[2,136,128]{2,1,0:T(8,128)S(1)} %copy-done.32), channel_id=1, source_target_pairs={{0,7},{1,6},{2,5},{3,4},{4,3},{5,2},{6,1},{7,0},{8,15},{9,14},{10,... | collective-permute-start | bytes 417800 | tf_op jit(solution)/shard_map/ppermute | solution.py:365
  24.5 3.6 %all-to-all-start = ((f32[16,64,128]{2,1,0:T(8,128)}), f32[16,64,128]{2,1,0:T(8,128)S(1)}, u32[]{:S(2)}, u32[]{:S(2)}) async-start(f32[16,64,128]{2,1,0:T(8,128)} %get-tuple-element.52), calls=%async_computation | async-start | bytes 1048576 | tf_op jit(solution)/shard_map/all_to_all | solution.py:390
  32.8 1.9 %collective-permute-start.12 = (f32[2,64,128]{2,1,0:T(8,128)S(1)}, f32[2,64,128]{2,1,0:T(8,128)S(1)}, u32[]{:S(2)}, u32[]{:S(2)}) collective-permute-start(f32[2,64,128]{2,1,0:T(8,128)S(1)} %copy-done.38), channel_id=1, source_target_pairs={{0,6},{1,7},{2,4},{3,5},{4,2},{5,3},{6,0},{7,1},{8,14},{9,15},{10,... | collective-permute-start | bytes 196616 | tf_op jit(solution)/shard_map/ppermute | solution.py:365
  34.7 1.9 %collective-permute-start.13 = (f32[2,64,128]{2,1,0:T(8,128)S(1)}, f32[2,64,128]{2,1,0:T(8,128)S(1)}, u32[]{:S(2)}, u32[]{:S(2)}) collective-permute-start(f32[2,64,128]{2,1,0:T(8,128)S(1)} %copy-done.37), channel_id=1, source_target_pairs={{0,7},{1,6},{2,5},{3,4},{4,3},{5,2},{6,1},{7,0},{8,15},{9,14},{10,... | collective-permute-start | bytes 196616 | tf_op jit(solution)/shard_map/ppermute | solution.py:365
  36.7 2.6 %weights.1 = (f32[2,256,128]{2,1,0:T(8,128)}, f32[2,256,128]{2,1,0:T(8,128)}, f32[2,256,128]{2,1,0:T(8,128)}, f32[2,256,128]{2,1,0:T(8,128)}, s32[16]{0:T(128)}) custom-call(s32[6,8]{1,0:T(8,128)} %stack.23.info, f32[2,136,128]{2,1,0:T(8,128)} %get-tuple-element.29.rest_0_, f32[2,136,128]{2,1,0:T(8,128)} %copy-done.14, f32[2,136,128]{2,1,0:T(8,128)} %copy-done.15, ...), custom_call_target="tpu_custom_call" | custom-call | tf_op jit(solution)/shard_map/weights/pallas_call | solution.py:399
  39.3 2.9 %collective-permute-done.10.rest_4_ = f32[2,64,128]{2,1,0:T(8,128)S(1)} collective-permute-done((f32[2,64,128]{2,1,0:T(8,128)S(1)}, f32[2,64,128]{2,1,0:T(8,128)S(1)}, u32[]{:S(2)}, u32[]{:S(2)}) %collective-permute-start.10) | collective-permute-done | bytes 65568 | tf_op jit(solution)/shard_map/ppermute | solution.py:365
  44.2 2.4 %outer.1 = (f32[8,64,128]{2,1,0:T(8,128)}, f32[8,64,128]{2,1,0:T(8,128)}) custom-call(s32[6,8]{1,0:T(8,128)} %stack.23.info, s32[16]{0:T(128)} %get-tuple-element.37.slot, f32[2,64,128]{2,1,0:T(8,128)} %get-tuple-element.38.rest_0_, f32[2,64,128]{2,1,0:T(8,128)} %copy-done.21, f32[2,64,128]{2,1,0:T(8,128)} %copy-done.22, f32[2,64,128]{2,1,0:T(8,128)} %copy-done.23, ...), custom_call_target="tpu_custom_call" | custom-call | tf_op jit(solution)/shard_map/outer/pallas_call | solution.py:410
  46.6 2.0 %collective-permute-start.14 = (f32[8,64,128]{2,1,0:T(8,128)}, f32[8,64,128]{2,1,0:T(8,128)S(1)}, u32[]{:S(2)}, u32[]{:S(2)}) collective-permute-start(f32[8,64,128]{2,1,0:T(8,128)} %get-tuple-element.50.bottom), channel_id=1, source_target_pairs={{0,1},{1,2},{2,3},{3,4},{4,5},{5,6},{6,7},{8,9},{9,10},{10,11},{11... | collective-permute-start | bytes 786440 | tf_op jit(solution)/shard_map/ppermute | solution.py:419
  49.9 2.6 %spectrum.1.spec = f32[2,192,256]{2,1,0:T(8,128)} custom-call(f32[1,4]{1,0:T(1,128)} %coeffs.1, f32[4,128,128]{2,1,0:T(8,128)} %basis.1, bf16[384,384]{1,0:T(8,128)(2,1)} %constant.25.clone.row_ker, bf16[2,768,256]{2,1,0:T(8,128)(2,1)} %constant.26.clone.col_fwd), custom_call_target="tpu_custom_call" | custom-call | tf_op jit(solution)/shard_map/spectrum/pallas_call | solution.py:391
  52.5 3.5 %collective-permute-start.24 = (f32[2,256,128]{2,1,0:T(8,128)}, f32[2,256,128]{2,1,0:T(8,128)S(1)}, u32[]{:S(2)}, u32[]{:S(2)}) collective-permute-start(f32[2,256,128]{2,1,0:T(8,128)} %get-tuple-element.46.rest_8_.rest_0_), channel_id=1, source_target_pairs={{0,8},{24,16},{1,9},{25,17},{2,10},{26,18},{3,11},{27,19},{4,12},{... | collective-permute-start | bytes 786440 | tf_op jit(solution)/shard_map/ppermute | solution.py:307
  56.8 2.3 %inner.1.image = f32[8,128,128]{2,1,0:T(8,128)} custom-call(s32[6,8]{1,0:T(8,128)} %stack.23.info, s32[16]{0:T(128)} %get-tuple-element.37.slot, f32[16,64,128]{2,1,0:T(8,128)} %copy-done.2, f32[2,256,128]{2,1,0:T(8,128)} %get-tuple-element.46.rest_8_.rest_0_, f32[2,256,128]{2,1,0:T(8,128)} %get-tuple-element.47.rest_9_.rest_1_.rest_0_, ...), custom_call_target="tpu_custom_call" | custom-call | tf_op jit(solution)/shard_map/inner/pallas_call | solution.py:421
  60.6 5.6 %shard_map.159 = f32[2,256,128]{2,1,0:T(8,128)} custom-call(s32[6,8]{1,0:T(8,128)} %stack.23.info, f32[8,64,128]{2,1,0:T(8,128)} %copy-done.3, f32[8,64,128]{2,1,0:T(8,128)} %get-tuple-element.51.top, f32[8,128,128]{2,1,0:T(8,128)} %inner.1.image, f32[8,64,128]{2,1,0:T(8,128)} %get-tuple-element.50.bottom, f32[8,64,128]{2,1,0:T(8,128)} %copy-done.4, ...), custom_call_target="tpu_custom_call" | custom-call | tf_op jit(solution)/shard_map/pallas_call | solution.py:434
  68.6 4.2 %collective-permute-start.22 = (f32[2,256,128]{2,1,0:T(8,128)S(1)}, f32[2,256,128]{2,1,0:T(8,128)S(1)}, u32[]{:S(2)}, u32[]{:S(2)}) collective-permute-start(f32[2,256,128]{2,1,0:T(8,128)S(1)} %copy-done), channel_id=1, source_target_pairs={{0,8},{8,16},{1,9},{9,17},{2,10},{10,18},{3,11},{11,19},{4,12},{12... | collective-permute-start | bytes 786440 | tf_op jit(solution)/shard_map/ppermute | solution.py:307
  75.4 9.7 %shard_map.158 = (f32[2,256,128]{2,1,0:T(8,128)}, f32[2,256,128]{2,1,0:T(8,128)}, f32[2,256,128]{2,1,0:T(8,128)}) custom-call(s32[6,8]{1,0:T(8,128)} %stack.23.info, f32[8,64,128]{2,1,0:T(8,128)} %copy-done.3, f32[8,64,128]{2,1,0:T(8,128)} %get-tuple-element.51.top, f32[8,128,128]{2,1,0:T(8,128)} %inner.1.image, f32[8,64,128]{2,1,0:T(8,128)} %get-tuple-element.50.bottom, ...), custom_call_target="tpu_custom_call" | custom-call | tf_op jit(solution)/shard_map/pallas_call | solution.py:434
  85.1 3.6 %collective-permute-start.16 = (f32[2,256,128]{2,1,0:T(8,128)}, f32[2,256,128]{2,1,0:T(8,128)S(1)}, u32[]{:S(2)}, u32[]{:S(2)}) collective-permute-start(f32[2,256,128]{2,1,0:T(8,128)} %get-tuple-element.54), channel_id=1, source_target_pairs={{0,16},{8,0},{16,24},{24,8},{1,17},{9,1},{17,25},{25,9},{2,18},{10... | collective-permute-start | bytes 786440 | tf_op jit(solution)/shard_map/ppermute | solution.py:307
  89.5 2.8 %collective-permute-start.17 = (f32[2,256,128]{2,1,0:T(8,128)S(1)}, f32[2,256,128]{2,1,0:T(8,128)S(1)}, u32[]{:S(2)}, u32[]{:S(2)}) collective-permute-start(f32[2,256,128]{2,1,0:T(8,128)S(1)} %copy-done.31), channel_id=1, source_target_pairs={{0,8},{8,16},{1,9},{9,17},{2,10},{10,18},{3,11},{11,19},{4,12},{12... | collective-permute-start | bytes 786440 | tf_op jit(solution)/shard_map/ppermute | solution.py:307
  94.4 2.0 %weight_map.1.refs_5_ = f32[256,256]{1,0:T(8,128)} custom-call(f32[2,256,128]{2,1,0:T(8,128)} %get-tuple-element.49.rest_11_.rest_3_.rest_2_.refs_0_, f32[2,256,128]{2,1,0:T(8,128)} %copy-done.10, f32[2,256,128]{2,1,0:T(8,128)} %copy-done.12, f32[2,256,128]{2,1,0:T(8,128)} %copy-done.11, f32[2,256,128]{2,1,0:T(8,128)} %copy-done.13), custom_call_target="tpu_custom_call" | custom-call | tf_op jit(solution)/shard_map/weight_map/pallas_call | solution.py:429
  96.5 3.8 %collective-permute-done.17.refs_2_ = f32[2,256,128]{2,1,0:T(8,128)S(1)} collective-permute-done((f32[2,256,128]{2,1,0:T(8,128)S(1)}, f32[2,256,128]{2,1,0:T(8,128)S(1)}, u32[]{:S(2)}, u32[]{:S(2)}) %collective-permute-start.17) | collective-permute-done | bytes 262176 | tf_op jit(solution)/shard_map/ppermute | solution.py:307
  100.3 7.9 %collective-permute-done.20.refs_4_ = f32[2,256,128]{2,1,0:T(8,128)S(1)} collective-permute-done((f32[2,256,128]{2,1,0:T(8,128)S(1)}, f32[2,256,128]{2,1,0:T(8,128)S(1)}, u32[]{:S(2)}, u32[]{:S(2)}) %collective-permute-start.20) | collective-permute-done | bytes 262176 | tf_op jit(solution)/shard_map/ppermute | solution.py:307
  108.9 2.1 %coadd.1 = f32[256,256]{1,0:T(8,128)} custom-call(f32[2,256,128]{2,1,0:T(8,128)} %get-tuple-element.53.refs_0_, f32[2,256,128]{2,1,0:T(8,128)} %copy-done.6, f32[2,256,128]{2,1,0:T(8,128)} %copy-done.8, f32[2,256,128]{2,1,0:T(8,128)} %copy-done.7, f32[2,256,128]{2,1,0:T(8,128)} %copy-done.9, f32[256,256]{1,0:T(8,128)} %weight_map.1.refs_5_), custom_call_target="tpu_custom_call" | custom-call | tf_op jit(solution)/shard_map/coadd/pallas_call | solution.py:448
  (131 shorter events, 26.3 us)
Async XLA Ops:
  7.5 12.9 %collective-permute-start = (f32[2,136,128]{2,1,0:T(8,128)}, f32[2,136,128]{2,1,0:T(8,128)S(1)}, u32[]{:S(2)}, u32[]{:S(2)}) collective-permute-start(f32[2,136,128]{2,1,0:T(8,128)} %get-tuple-element.30), channel_id=1, source_target_pairs={{0,1},{1,0},{2,3},{3,2},{4,5},{5,4},{6,7},{7,6},{8,9},{9,8},{10,11... | collective-permute-start | bytes 417800 | tf_op jit(solution)/shard_map/ppermute | solution.py:365
  8.0 13.3 %collective-permute-start.1 = (f32[2,136,128]{2,1,0:T(8,128)}, f32[2,136,128]{2,1,0:T(8,128)S(1)}, u32[]{:S(2)}, u32[]{:S(2)}) collective-permute-start(f32[2,136,128]{2,1,0:T(8,128)} %get-tuple-element.31), channel_id=1, source_target_pairs={{0,2},{1,3},{2,0},{3,1},{4,6},{5,7},{6,4},{7,5},{8,10},{9,11},{10,... | collective-permute-start | bytes 417800 | tf_op jit(solution)/shard_map/ppermute | solution.py:365
  15.7 12.5 %collective-permute-start.2 = (f32[2,136,128]{2,1,0:T(8,128)S(1)}, f32[2,136,128]{2,1,0:T(8,128)S(1)}, u32[]{:S(2)}, u32[]{:S(2)}) collective-permute-start(f32[2,136,128]{2,1,0:T(8,128)S(1)} %copy-done.36), channel_id=1, source_target_pairs={{0,3},{1,2},{2,1},{3,0},{4,7},{5,6},{6,5},{7,4},{8,11},{9,10},{10,... | collective-permute-start | bytes 417800 | tf_op jit(solution)/shard_map/ppermute | solution.py:365
  16.9 13.0 %collective-permute-start.3 = (f32[2,136,128]{2,1,0:T(8,128)S(1)}, f32[2,136,128]{2,1,0:T(8,128)S(1)}, u32[]{:S(2)}, u32[]{:S(2)}) collective-permute-start(f32[2,136,128]{2,1,0:T(8,128)S(1)} %copy-done.35), channel_id=1, source_target_pairs={{0,4},{1,5},{2,6},{3,7},{4,0},{5,1},{6,2},{7,3},{8,12},{9,13},{10,... | collective-permute-start | bytes 417800 | tf_op jit(solution)/shard_map/ppermute | solution.py:365
  20.4 11.9 %collective-permute-start.4 = (f32[2,136,128]{2,1,0:T(8,128)S(1)}, f32[2,136,128]{2,1,0:T(8,128)S(1)}, u32[]{:S(2)}, u32[]{:S(2)}) collective-permute-start(f32[2,136,128]{2,1,0:T(8,128)S(1)} %copy-done.34), channel_id=1, source_target_pairs={{0,5},{1,4},{2,7},{3,6},{4,1},{5,0},{6,3},{7,2},{8,13},{9,12},{10,... | collective-permute-start | bytes 417800 | tf_op jit(solution)/shard_map/ppermute | solution.py:365
  20.4 12.4 %collective-permute-start.5 = (f32[2,136,128]{2,1,0:T(8,128)S(1)}, f32[2,136,128]{2,1,0:T(8,128)S(1)}, u32[]{:S(2)}, u32[]{:S(2)}) collective-permute-start(f32[2,136,128]{2,1,0:T(8,128)S(1)} %copy-done.33), channel_id=1, source_target_pairs={{0,6},{1,7},{2,4},{3,5},{4,2},{5,3},{6,0},{7,1},{8,14},{9,15},{10,... | collective-permute-start | bytes 417800 | tf_op jit(solution)/shard_map/ppermute | solution.py:365
  21.4 13.3 %collective-permute-start.6 = (f32[2,136,128]{2,1,0:T(8,128)S(1)}, f32[2,136,128]{2,1,0:T(8,128)S(1)}, u32[]{:S(2)}, u32[]{:S(2)}) collective-permute-start(f32[2,136,128]{2,1,0:T(8,128)S(1)} %copy-done.32), channel_id=1, source_target_pairs={{0,7},{1,6},{2,5},{3,4},{4,3},{5,2},{6,1},{7,0},{8,15},{9,14},{10,... | collective-permute-start | bytes 417800 | tf_op jit(solution)/shard_map/ppermute | solution.py:365
  24.5 31.6 %all-to-all-start = ((f32[16,64,128]{2,1,0:T(8,128)}), f32[16,64,128]{2,1,0:T(8,128)S(1)}, u32[]{:S(2)}, u32[]{:S(2)}) async-start(f32[16,64,128]{2,1,0:T(8,128)} %get-tuple-element.52), calls=%async_computation | async-start | bytes 1048576 | tf_op jit(solution)/shard_map/all_to_all | solution.py:390
  28.1 11.1 %collective-permute-start.9 = (f32[2,64,128]{2,1,0:T(8,128)S(1)}, f32[2,64,128]{2,1,0:T(8,128)S(1)}, u32[]{:S(2)}, u32[]{:S(2)}) collective-permute-start(f32[2,64,128]{2,1,0:T(8,128)S(1)} %copy-done.41), channel_id=1, source_target_pairs={{0,3},{1,2},{2,1},{3,0},{4,7},{5,6},{6,5},{7,4},{8,11},{9,10},{10,... | collective-permute-start | bytes 196616 | tf_op jit(solution)/shard_map/ppermute | solution.py:365
  29.9 12.4 %collective-permute-start.10 = (f32[2,64,128]{2,1,0:T(8,128)S(1)}, f32[2,64,128]{2,1,0:T(8,128)S(1)}, u32[]{:S(2)}, u32[]{:S(2)}) collective-permute-start(f32[2,64,128]{2,1,0:T(8,128)S(1)} %copy-done.40), channel_id=1, source_target_pairs={{0,4},{1,5},{2,6},{3,7},{4,0},{5,1},{6,2},{7,3},{8,12},{9,13},{10,... | collective-permute-start | bytes 196616 | tf_op jit(solution)/shard_map/ppermute | solution.py:365
  32.3 11.2 %collective-permute-start.11 = (f32[2,64,128]{2,1,0:T(8,128)S(1)}, f32[2,64,128]{2,1,0:T(8,128)S(1)}, u32[]{:S(2)}, u32[]{:S(2)}) collective-permute-start(f32[2,64,128]{2,1,0:T(8,128)S(1)} %copy-done.39), channel_id=1, source_target_pairs={{0,5},{1,4},{2,7},{3,6},{4,1},{5,0},{6,3},{7,2},{8,13},{9,12},{10,... | collective-permute-start | bytes 196616 | tf_op jit(solution)/shard_map/ppermute | solution.py:365
  32.8 10.7 %collective-permute-start.12 = (f32[2,64,128]{2,1,0:T(8,128)S(1)}, f32[2,64,128]{2,1,0:T(8,128)S(1)}, u32[]{:S(2)}, u32[]{:S(2)}) collective-permute-start(f32[2,64,128]{2,1,0:T(8,128)S(1)} %copy-done.38), channel_id=1, source_target_pairs={{0,6},{1,7},{2,4},{3,5},{4,2},{5,3},{6,0},{7,1},{8,14},{9,15},{10,... | collective-permute-start | bytes 196616 | tf_op jit(solution)/shard_map/ppermute | solution.py:365
  34.7 8.8 %collective-permute-start.13 = (f32[2,64,128]{2,1,0:T(8,128)S(1)}, f32[2,64,128]{2,1,0:T(8,128)S(1)}, u32[]{:S(2)}, u32[]{:S(2)}) collective-permute-start(f32[2,64,128]{2,1,0:T(8,128)S(1)} %copy-done.37), channel_id=1, source_target_pairs={{0,7},{1,6},{2,5},{3,4},{4,3},{5,2},{6,1},{7,0},{8,15},{9,14},{10,... | collective-permute-start | bytes 196616 | tf_op jit(solution)/shard_map/ppermute | solution.py:365
  46.6 12.6 %collective-permute-start.14 = (f32[8,64,128]{2,1,0:T(8,128)}, f32[8,64,128]{2,1,0:T(8,128)S(1)}, u32[]{:S(2)}, u32[]{:S(2)}) collective-permute-start(f32[8,64,128]{2,1,0:T(8,128)} %get-tuple-element.50.bottom), channel_id=1, source_target_pairs={{0,1},{1,2},{2,3},{3,4},{4,5},{5,6},{6,7},{8,9},{9,10},{10,11},{11... | collective-permute-start | bytes 786440 | tf_op jit(solution)/shard_map/ppermute | solution.py:419
  48.6 10.6 %collective-permute-start.15 = (f32[8,64,128]{2,1,0:T(8,128)}, f32[8,64,128]{2,1,0:T(8,128)S(1)}, u32[]{:S(2)}, u32[]{:S(2)}) collective-permute-start(f32[8,64,128]{2,1,0:T(8,128)} %get-tuple-element.51.top), channel_id=1, source_target_pairs={{1,0},{2,1},{3,2},{4,3},{5,4},{6,5},{7,6},{9,8},{10,9},{11,10},{12... | collective-permute-start | bytes 786440 | tf_op jit(solution)/shard_map/ppermute | solution.py:420
  52.5 20.2 %collective-permute-start.24 = (f32[2,256,128]{2,1,0:T(8,128)}, f32[2,256,128]{2,1,0:T(8,128)S(1)}, u32[]{:S(2)}, u32[]{:S(2)}) collective-permute-start(f32[2,256,128]{2,1,0:T(8,128)} %get-tuple-element.46.rest_8_.rest_0_), channel_id=1, source_target_pairs={{0,8},{24,16},{1,9},{25,17},{2,10},{26,18},{3,11},{27,19},{4,12},{... | collective-permute-start | bytes 786440 | tf_op jit(solution)/shard_map/ppermute | solution.py:307
  66.2 18.9 %collective-permute-start.19 = (f32[2,256,128]{2,1,0:T(8,128)}, f32[2,256,128]{2,1,0:T(8,128)S(1)}, u32[]{:S(2)}, u32[]{:S(2)}) collective-permute-start(f32[2,256,128]{2,1,0:T(8,128)} %shard_map.159), channel_id=1, source_target_pairs={{0,8},{24,16},{1,9},{25,17},{2,10},{26,18},{3,11},{27,19},{4,12},{... | collective-permute-start | bytes 786440 | tf_op jit(solution)/shard_map/ppermute | solution.py:307
  67.5 21.3 %collective-permute-start.21 = (f32[2,256,128]{2,1,0:T(8,128)S(1)}, f32[2,256,128]{2,1,0:T(8,128)S(1)}, u32[]{:S(2)}, u32[]{:S(2)}) collective-permute-start(f32[2,256,128]{2,1,0:T(8,128)S(1)} %copy-done.1), channel_id=1, source_target_pairs={{0,16},{8,0},{16,24},{24,8},{1,17},{9,1},{17,25},{25,9},{2,18},{10... | collective-permute-start | bytes 786440 | tf_op jit(solution)/shard_map/ppermute | solution.py:307
  67.9 21.6 %collective-permute-start.23 = (f32[2,256,128]{2,1,0:T(8,128)S(1)}, f32[2,256,128]{2,1,0:T(8,128)S(1)}, u32[]{:S(2)}, u32[]{:S(2)}) collective-permute-start(f32[2,256,128]{2,1,0:T(8,128)S(1)} %copy-done), channel_id=1, source_target_pairs={{16,8},{24,16},{17,9},{25,17},{18,10},{26,18},{19,11},{27,19},{20,... | collective-permute-start | bytes 786440 | tf_op jit(solution)/shard_map/ppermute | solution.py:307
  68.6 23.8 %collective-permute-start.22 = (f32[2,256,128]{2,1,0:T(8,128)S(1)}, f32[2,256,128]{2,1,0:T(8,128)S(1)}, u32[]{:S(2)}, u32[]{:S(2)}) collective-permute-start(f32[2,256,128]{2,1,0:T(8,128)S(1)} %copy-done), channel_id=1, source_target_pairs={{0,8},{8,16},{1,9},{9,17},{2,10},{10,18},{3,11},{11,19},{4,12},{12... | collective-permute-start | bytes 786440 | tf_op jit(solution)/shard_map/ppermute | solution.py:307
  73.8 19.9 %collective-permute-start.25 = (f32[2,256,128]{2,1,0:T(8,128)S(1)}, f32[2,256,128]{2,1,0:T(8,128)S(1)}, u32[]{:S(2)}, u32[]{:S(2)}) collective-permute-start(f32[2,256,128]{2,1,0:T(8,128)S(1)} %add.13), channel_id=1, source_target_pairs={{8,24},{16,0},{9,25},{17,1},{10,26},{18,2},{11,27},{19,3},{12,28},... | collective-permute-start | bytes 786440 | tf_op jit(solution)/shard_map/ppermute | solution.py:307
  85.1 11.4 %collective-permute-start.16 = (f32[2,256,128]{2,1,0:T(8,128)}, f32[2,256,128]{2,1,0:T(8,128)S(1)}, u32[]{:S(2)}, u32[]{:S(2)}) collective-permute-start(f32[2,256,128]{2,1,0:T(8,128)} %get-tuple-element.54), channel_id=1, source_target_pairs={{0,16},{8,0},{16,24},{24,8},{1,17},{9,1},{17,25},{25,9},{2,18},{10... | collective-permute-start | bytes 786440 | tf_op jit(solution)/shard_map/ppermute | solution.py:307
  89.5 10.8 %collective-permute-start.17 = (f32[2,256,128]{2,1,0:T(8,128)S(1)}, f32[2,256,128]{2,1,0:T(8,128)S(1)}, u32[]{:S(2)}, u32[]{:S(2)}) collective-permute-start(f32[2,256,128]{2,1,0:T(8,128)S(1)} %copy-done.31), channel_id=1, source_target_pairs={{0,8},{8,16},{1,9},{9,17},{2,10},{10,18},{3,11},{11,19},{4,12},{12... | collective-permute-start | bytes 786440 | tf_op jit(solution)/shard_map/ppermute | solution.py:307
  92.4 15.9 %collective-permute-start.20 = (f32[2,256,128]{2,1,0:T(8,128)S(1)}, f32[2,256,128]{2,1,0:T(8,128)S(1)}, u32[]{:S(2)}, u32[]{:S(2)}) collective-permute-start(f32[2,256,128]{2,1,0:T(8,128)S(1)} %add.12), channel_id=1, source_target_pairs={{8,24},{16,0},{9,25},{17,1},{10,26},{18,2},{11,27},{19,3},{12,28},... | collective-permute-start | bytes 786440 | tf_op jit(solution)/shard_map/ppermute | solution.py:307
  (45 other events, 240.0 us)
where the time goes:
time: 112 us; the launch traced here: 111 us
  starting transfers between devices  45.3 us (40%)
  Pallas kernels  37.9 us (34%)
  waiting for transfers between devices  18.8 us (17%)
  local copies, waits for them, and re-layouts  6.95 us (6%)
  between operations  1.13 us (1%)
    ppermute x10, starting transfers between devices, send(): self.sent += [lax.ppermute(tile, 'visit', route) for route in routes]  20.1 us
    ppermute x14, starting transfers between devices, exchange(): lax.ppermute(sent[d], 'bulk', [(i, i ^ d) for i in range(owners)])  18.3 us
    pallas_call x2, Pallas kernels, convolve(): pl.pallas_call(functools.partial(conv_body, first), out_shape=[tile] * co...  15.3 us
    ppermute x10, waiting for transfers between devices, send(): self.sent += [lax.ppermute(tile, 'visit', route) for route in routes]  11.8 us
    ppermute x14, waiting for transfers between devices, exchange(): lax.ppermute(sent[d], 'bulk', [(i, i ^ d) for i in range(owners)])  6.99 us
    unnamed x84, local copies, waits for them, and re-layouts  5.64 us
    pallas_call x1, Pallas kernels, coadd_patches(): pl.pallas_call(warp_flux_body, out_shape=[arr(CAP, half, side)] * owners...  4.32 us
    pallas_call x1, Pallas kernels, coadd_patches(): pl.pallas_call(warp_weight_body, out_shape=[arr(CAP, side + META, side)]...  4.17 us
  transfers between devices with their start and end apart: 27, of which 7 were waited for; matrix products, arithmetic and copies ran while one was open for 1% of the time, Pallas kernels for 28%

commit v1 on v0

--- a/solution.py
+++ b/solution.py
@@ -40,11 +40,14 @@
     return jnp.concatenate([high, high, low], axis)
 
 
-def table(value, axis):
+def table(value):
     value = np.asarray(value, np.float32)
     high = value.astype(jnp.bfloat16)
-    low = (value - high.astype(np.float32)).astype(jnp.bfloat16)
-    return np.concatenate([high, high, low], axis)
+    return np.stack([high, (value - high.astype(np.float32)).astype(jnp.bfloat16)])
+
+
+def fixed(ref, axis):
+    return jnp.concatenate([ref[0], ref[0], ref[1]], axis)
 
 
 def dot(a, b, dims=((1,), (0,))):
@@ -83,11 +86,11 @@
     weight = np.where(k.T == 0, 1.0, 2.0) / (length * period)
     row_inv = np.concatenate([weight * np.cos(theta), -weight * np.sin(theta)], 1)
     return (
-        table(row_fwd, 1),
-        table(row_ker, 1),
-        np.stack([table(t, 0) for t in col_fwd]),
-        np.stack([table(t, 0) for t in col_inv]),
-        table(row_inv, 1),
+        table(row_fwd),
+        table(row_ker),
+        np.stack([table(t) for t in col_fwd]),
+        np.stack([table(t) for t in col_inv]),
+        table(row_inv),
     )
 
 
@@ -139,18 +142,9 @@
     run([pltpu.make_async_copy(send.at[d], out, sems.at[d]) for d, out in enumerate(outs)])
 
 
-def warp_flux_body(info, flux, ivar, rows, cols, *rest):
-    pieces, side, _ = ivar.shape[2:]
-    half = side // 2
-    *outs, inner, send, send_inner, sems = rest
-    for q, to, own, rank, at in places(info, pieces):
-        first = (at // BC) * half
-        maps = jnp.concatenate([rows[0, 0, q, pl.ds(first, half), :], rows[0, 0, q, pl.ds(half - first, half), :]], 0)
-        done = warp(masked(info, ivar, q) * flux[0, 0, q], maps, cols[0, 0, q])
-        send[to, rank] = done[:half]
-        send_inner[own * CAP + rank] = done[half:]
-    copies = [pltpu.make_async_copy(send.at[d], out, sems.at[d]) for d, out in enumerate(outs)]
-    run(copies + [pltpu.make_async_copy(send_inner, inner, sems.at[len(outs)])])
+def warp_flux_body(info, flux, ivar, rows, cols, out):
+    for q, _, own, rank, _ in places(info, ivar.shape[2]):
+        out[own * CAP + rank] = warp(masked(info, ivar, q) * flux[0, 0, q], rows[0, 0, q], cols[0, 0, q])
 
 
 def weight_body(info, *rest):
@@ -176,26 +170,9 @@
                 out[k][c, r * side : (r + 1) * side, :] = acc[r * BC + info[ORDER, k] * per_tile + c]
 
 
-def outer_body(info, slot, *rest):
-    *rest, top, bottom, acc = rest
-    count = slot.shape[0] // CAP
-    got, tiles = rest[:count], rest[count:]
-    half = acc.shape[1]
-    per_tile = tiles[0].shape[0]
-    acc[...] = jnp.zeros(acc.shape, F32)
-    for d in range(count):
-        for rank in range(CAP):
-            acc[slot[partner(info[ME, 0], d) * CAP + rank]] += got[d][rank]
-    for k, tile in enumerate(tiles):
-        for c in range(per_tile):
-            to = info[ORDER, k] * per_tile + c
-            top[to] = acc[to] / jnp.maximum(tile[c, :half, :], 1.0)
-            bottom[to] = acc[BC + to] / jnp.maximum(tile[c, -half:, :], 1.0)
-
-
-def inner_body(info, slot, got, *rest):
-    *tiles, image, acc = rest
-    half = acc.shape[1]
+def image_body(info, slot, got, *rest):
+    *tiles, image, top, bottom, acc = rest
+    side = acc.shape[1]
     per_tile = tiles[0].shape[0]
     acc[...] = jnp.zeros(acc.shape, F32)
     for n in range(slot.shape[0]):
@@ -203,8 +180,11 @@
     for k, tile in enumerate(tiles):
         for c in range(per_tile):
             to = info[ORDER, k] * per_tile + c
-            image[to, :half, :] = acc[to] / jnp.maximum(tile[c, half : 2 * half, :], 1.0)
-            image[to, half:, :] = acc[BC + to] / jnp.maximum(tile[c, 2 * half : 3 * half, :], 1.0)
+            for r in range(BR):
+                rows = slice(r * side, (r + 1) * side)
+                image[to, rows, :] = acc[r * BC + to] / jnp.maximum(tile[c, rows, :], 1.0)
+            top[to] = image[to, :HALO, :]
+            bottom[to] = image[to, -HALO:, :]
 
 
 def beside(stacked):
@@ -216,12 +196,12 @@
     kernel = coeffs[0, 0] * basis[0]
     for k in range(1, basis.shape[0]):
         kernel = kernel + coeffs[0, k] * basis[k]
-    lines = data(beside(dot(row_ker[...], data(kernel, 0))), 1)
+    lines = data(beside(dot(fixed(row_ker, 1), data(kernel, 0))), 1)
     for odd in (0, 1):
-        out[odd] = dot(lines, col_fwd[odd])
-
-
-def conv_body(first, info, above, top, image, bottom, below, spec, row_fwd, col_fwd, col_inv, row_inv, *rest):
+        out[odd] = dot(lines, fixed(col_fwd.at[odd], 0))
+
+
+def conv_body(first, info, above, image, below, spec, row_fwd, col_fwd, col_inv, row_inv, *rest):
     *rest, lines = rest
     count = len(rest) // 2
     weight, out = rest[:count], rest[count:]
@@ -229,11 +209,11 @@
     per_tile = weight[0].shape[0]
 
     def column(c):
-        return jnp.concatenate([above[c], top[c], image[c], bottom[c], below[c]], 0)
+        return jnp.concatenate([above[c], image[c], below[c]], 0)
 
     def shifted(u):
         if isinstance(u, int):
-            gap = jnp.zeros((above.shape[1] * 6, HALO), F32)
+            gap = jnp.zeros((image.shape[1] + 2 * HALO, HALO), F32)
             left = column(u - 1)[:, taps - HALO :] if u > 0 else gap
             right = column(u)[:, :HALO] if u < BC else gap
             return jnp.concatenate([left, right], 1)
@@ -243,12 +223,14 @@
         right = jnp.where(u < BC, right, 0.0)
         return jnp.concatenate([left, right], 1)
 
+    lead = fixed(row_fwd, 1)
+    last = fixed(row_inv, 1)
     one_tile = lines.shape[0] == per_tile + 1
     base = info[ORDER, first] * per_tile if one_tile else 0
     for u in range(0, lines.shape[0], 2):
         n = min(2, lines.shape[0] - u)
         ext = jnp.concatenate([shifted(base + u + i) for i in range(n)], 1)
-        got = dot(row_fwd[...], data(ext, 0))
+        got = dot(lead, data(ext, 0))
         for i in range(n):
             lines[u + i] = got[:, i * taps : (i + 1) * taps]
     for k in range(count):
@@ -259,16 +241,16 @@
         total = []
         for odd in (0, 1):
             mixed = [beside(a - b if odd else a + b) for a, b in zip(one, two)]
-            freq = dot(data(jnp.concatenate(mixed, 0), 1), col_fwd[odd])
+            freq = dot(data(jnp.concatenate(mixed, 0), 1), fixed(col_fwd.at[odd], 0))
             kr = jnp.concatenate([spec[odd, :, :taps]] * per_tile, 0)
             ki = jnp.concatenate([spec[odd, :, taps:]] * per_tile, 0)
             zr, zi = freq[:, :taps], freq[:, taps:]
             prod = jnp.concatenate([zr * kr - zi * ki, zr * ki + zi * kr], 1)
-            total.append(dot(data(prod, 1), col_inv[odd]))
+            total.append(dot(data(prod, 1), fixed(col_inv.at[odd], 0)))
         wave = total[0] + total[1]
         parts = [wave[c * freqs : (c + 1) * freqs] for c in range(per_tile)]
         cols = [jnp.concatenate([p[:, :taps], p[:, taps:]], 0) for p in parts]
-        done = dot(row_inv[...], data(jnp.concatenate(cols, 1), 0))
+        done = dot(last, data(jnp.concatenate(cols, 1), 0))
         for c in range(per_tile):
             out[k][c] = done[:, c * taps : (c + 1) * taps] * weight[k][c]
 
@@ -330,12 +312,11 @@
     visits = lax.axis_size("visit")
     pieces, side = piece_flux.shape[2:4]
     assert side == LANES and side == 2 * HALO and owners & (owners - 1) == 0
-    half = side // 2
     rows_dev = BR * side
     per_tile = BC // visits
     cap = owners * CAP
     row_fwd, row_ker, col_fwd, col_inv, row_inv = [jnp.asarray(t) for t in make_tables(rows_dev, side)]
-    freqs = row_fwd.shape[0] // 2
+    freqs = row_fwd.shape[1] // 2
     width = max(pieces, visits)
 
     def line(values):
@@ -374,20 +355,14 @@
         name="warp_weight",
     )(info, piece_ivar, warp_rows, warp_cols)
     got_weight = exchange(sent_weight)
-    *sent_outer, sent_inner = pl.pallas_call(
+    sent_flux = pl.pallas_call(
         warp_flux_body,
-        out_shape=[arr(CAP, half, side)] * owners + [arr(cap, half, side)],
+        out_shape=arr(cap, side, side),
         in_specs=[SMEM] + [VMEM] * 4,
-        out_specs=[hbm] * (owners + 1),
-        scratch_shapes=[
-            pltpu.VMEM((owners, CAP, half, side), F32),
-            pltpu.VMEM((cap, half, side), F32),
-            pltpu.SemaphoreType.DMA((owners + 1,)),
-        ],
+        out_specs=VMEM,
         name="warp_flux",
     )(info, piece_flux, piece_ivar, warp_rows, warp_cols)
-    got_outer = exchange(sent_outer)
-    got_inner = lax.all_to_all(sent_inner, "bulk", split_axis=0, concat_axis=0, tiled=True)
+    got_flux = lax.all_to_all(sent_flux, "bulk", split_axis=0, concat_axis=0, tiled=True)
     spec = pl.pallas_call(
         spectrum_body,
         out_shape=arr(2, freqs, 2 * side),
@@ -406,26 +381,17 @@
     )(info, *got_weight)
     weight_sum = VisitSum(visits)
     weight_sum.push(*ivar)
-    scratch = [pltpu.VMEM((BR * BC + 1, half, side), F32)]
-    top, bottom = pl.pallas_call(
-        outer_body,
-        out_shape=[arr(BC, half, side)] * 2,
-        in_specs=[SMEM] * 2 + [VMEM] * (owners + visits),
-        out_specs=[VMEM] * 2,
-        scratch_shapes=scratch,
-        name="outer",
-    )(info, slots, *got_outer, *ivar)
+    image, top, bottom = pl.pallas_call(
+        image_body,
+        out_shape=[arr(BC, rows_dev, side)] + [arr(BC, HALO, side)] * 2,
+        in_specs=[SMEM] * 2 + [VMEM] * (1 + visits),
+        out_specs=[VMEM] * 3,
+        scratch_shapes=[pltpu.VMEM((BR * BC + 1, side, side), F32)],
+        name="image",
+    )(info, slots, got_flux, *ivar)
     ends = owners - 1
     above = lax.ppermute(bottom, "bulk", [(i, i + 1) for i in range(ends)])
     below = lax.ppermute(top, "bulk", [(i + 1, i) for i in range(ends)])
-    image = pl.pallas_call(
-        inner_body,
-        out_shape=arr(BC, side, side),
-        in_specs=[SMEM] * 2 + [VMEM] * (1 + visits),
-        out_specs=VMEM,
-        scratch_shapes=scratch,
-        name="inner",
-    )(info, slots, got_inner, *ivar)
     weight_map = pl.pallas_call(
         total_body, out_shape=arr(rows_dev, per_tile * side), name="weight_map"
     )(*weight_sum.parts())
@@ -434,11 +400,11 @@
         return pl.pallas_call(
             functools.partial(conv_body, first),
             out_shape=[tile] * count,
-            in_specs=[SMEM] + [VMEM] * (10 + count),
+            in_specs=[SMEM] + [VMEM] * (8 + count),
             out_specs=[VMEM] * count,
             scratch_shapes=[pltpu.VMEM((blocks, 2 * freqs, side), F32)],
         )(
-            info, above, top, image, bottom, below, spec, row_fwd, col_fwd, col_inv, row_inv,
+            info, above, image, below, spec, row_fwd, col_fwd, col_inv, row_inv,
             *ivar[first : first + count],
         )
 

time: 112 us -> 113 us (level)
  waiting for transfers between devices: 18.8 us -> 29.6 us
  starting transfers between devices: 45.3 us -> 37.9 us
  Pallas kernels: 37.9 us -> 35.5 us
    ppermute x14 -> x7, starting transfers between devices: 18.3 us -> 6.63 us  [exchange(): lax.ppermute(sent[d], 'bulk', [(i, i ^ d) for i in range(owners)])]
    ppermute x14 -> x7, waiting for transfers between devices: 6.99 us -> 15.9 us  [exchange(): lax.ppermute(sent[d], 'bulk', [(i, i ^ d) for i in range(owners)])]
    ppermute x10, starting transfers between devices: 20.1 us -> 22.4 us  [send(): self.sent += [lax.ppermute(tile, 'visit', route) for route in routes]]
    ppermute x10, waiting for transfers between devices: 11.8 us -> 13.6 us  [send(): self.sent += [lax.ppermute(tile, 'visit', route) for route in routes]]
    pallas_call x3 -> x2, Pallas kernels: 9.06 us -> 7.26 us  [the longest x1 4.26 us: coadd_patches(): pl.pallas_call(warp_flux_body, out_shape=arr(cap, side, side), in_specs=[...]
    all_to_all x1, starting transfers between devices: 3.64 us -> 5.2 us  [coadd_patches(): lax.all_to_all(sent_flux, 'bulk', split_axis=0, concat_axis=0, tiled=True)]
    unnamed x84 -> x52, local copies, waits for them, and re-layouts: 5.64 us -> 5.19 us
  transfers between devices with their start and end apart: 27 -> 20, of which waited for: 7 -> 6; matrix products, arithmetic and copies ran while one was open for 1% -> 1% of each run, Pallas kernels for 28% -> 23%
where the time goes in v1:
time: 113 us; the launch traced here: 111 us
  starting transfers between devices  37.9 us (34%)
  Pallas kernels  35.5 us (31%)
  waiting for transfers between devices  29.6 us (26%)
  local copies, waits for them, and re-layouts  6.49 us (6%)
    ppermute x10, starting transfers between devices, send(): self.sent += [lax.ppermute(tile, 'visit', route) for route in routes]  22.4 us
    ppermute x7, waiting for transfers between devices, exchange(): lax.ppermute(sent[d], 'bulk', [(i, i ^ d) for i in range(owners)])  15.9 us
    pallas_call x2, Pallas kernels, convolve(): pl.pallas_call(functools.partial(conv_body, first), out_shape=[tile] * co...  14.8 us
    ppermute x10, waiting for transfers between devices, send(): self.sent += [lax.ppermute(tile, 'visit', route) for route in routes]  13.6 us
    ppermute x7, starting transfers between devices, exchange(): lax.ppermute(sent[d], 'bulk', [(i, i ^ d) for i in range(owners)])  6.63 us
    all_to_all x1, starting transfers between devices, coadd_patches(): lax.all_to_all(sent_flux, 'bulk', split_axis=0, concat_axis=0, tiled=True)  5.2 us
    unnamed x52, local copies, waits for them, and re-layouts  5.19 us
    pallas_call x1, Pallas kernels, coadd_patches(): pl.pallas_call(warp_flux_body, out_shape=arr(cap, side, side), in_specs=[...  4.26 us
  transfers between devices with their start and end apart: 20, of which 6 were waited for; matrix products, arithmetic and copies ran while one was open for 1% of the time, Pallas kernels for 23%

profile of v1, /device:TPU:0, one launch (start us, length us, event | category | flops | bytes accessed | tf_op | source)
XLA Modules:
  0.0 111.4 jit_solution(15019846262260985021)
XLA Ops:
  3.3 4.3 %warp_flux.1 = f32[16,128,128]{2,1,0:T(8,128)} custom-call(s32[6,8]{1,0:T(8,128)} %stack.23.info, f32[1,1,8,128,128]{4,3,2,1,0:T(8,128)} %flux.1, f32[1,1,8,128,128]{4,3,2,1,0:T(8,128)} %ivar.3, f32[1,1,8,128,128]{4,3,2,1,0:T(8,128)} %rows.3, f32[1,1,8,128,128]{4,3,2,1,0:T(8,128)} %cols.3), custom_call_target="tpu_custom_call" | custom-call | tf_op jit(solution)/shard_map/warp_flux/pallas_call | solution.py:358
  7.5 5.2 %all-to-all-start = ((f32[16,128,128]{2,1,0:T(8,128)}), f32[16,128,128]{2,1,0:T(8,128)S(1)}, u32[]{:S(2)}, u32[]{:S(2)}) async-start(f32[16,128,128]{2,1,0:T(8,128)} %warp_flux.1), calls=%async_computation | async-start | bytes 2097152 | tf_op jit(solution)/shard_map/all_to_all | solution.py:365
  12.7 4.2 %warp_weight.1 = (f32[2,136,128]{2,1,0:T(8,128)}, f32[2,136,128]{2,1,0:T(8,128)}, f32[2,136,128]{2,1,0:T(8,128)}, f32[2,136,128]{2,1,0:T(8,128)}, f32[2,136,128]...) custom-call(s32[6,8]{1,0:T(8,128)} %stack.23.info, ...), custom_call_target="tpu_custom_call" | custom-call | tf_op jit(solution)/shard_map/warp_weight/pallas_call | solution.py:349
  17.5 1.6 %collective-permute-start.1 = (f32[2,136,128]{2,1,0:T(8,128)}, f32[2,136,128]{2,1,0:T(8,128)S(1)}, u32[]{:S(2)}, u32[]{:S(2)}) collective-permute-start(f32[2,136,128]{2,1,0:T(8,128)} %get-tuple-element.23), channel_id=1, source_target_pairs={{0,2},{1,3},{2,0},{3,1},{4,6},{5,7},{6,4},{7,5},{8,10},{9,11},{10,... | collective-permute-start | bytes 417800 | tf_op jit(solution)/shard_map/ppermute | solution.py:346
  19.1 1.7 %collective-permute-start.3 = (f32[2,136,128]{2,1,0:T(8,128)}, f32[2,136,128]{2,1,0:T(8,128)S(1)}, u32[]{:S(2)}, u32[]{:S(2)}) collective-permute-start(f32[2,136,128]{2,1,0:T(8,128)} %get-tuple-element.25), channel_id=1, source_target_pairs={{0,4},{1,5},{2,6},{3,7},{4,0},{5,1},{6,2},{7,3},{8,12},{9,13},{10,... | collective-permute-start | bytes 417800 | tf_op jit(solution)/shard_map/ppermute | solution.py:346
  21.0 2.5 %collective-permute-start.5 = (f32[2,136,128]{2,1,0:T(8,128)}, f32[2,136,128]{2,1,0:T(8,128)S(1)}, u32[]{:S(2)}, u32[]{:S(2)}) collective-permute-start(f32[2,136,128]{2,1,0:T(8,128)} %get-tuple-element.27), channel_id=1, source_target_pairs={{0,6},{1,7},{2,4},{3,5},{4,2},{5,3},{6,0},{7,1},{8,14},{9,15},{10,... | collective-permute-start | bytes 417800 | tf_op jit(solution)/shard_map/ppermute | solution.py:346
  23.5 7.3 %collective-permute-done.1.rest_2_ = f32[2,136,128]{2,1,0:T(8,128)S(1)} collective-permute-done((f32[2,136,128]{2,1,0:T(8,128)}, f32[2,136,128]{2,1,0:T(8,128)S(1)}, u32[]{:S(2)}, u32[]{:S(2)}) %collective-permute-start.1) | collective-permute-done | bytes 139296 | tf_op jit(solution)/shard_map/ppermute | solution.py:346
  30.9 1.8 %collective-permute-done.2.rest_3_ = f32[2,136,128]{2,1,0:T(8,128)S(1)} collective-permute-done((f32[2,136,128]{2,1,0:T(8,128)}, f32[2,136,128]{2,1,0:T(8,128)S(1)}, u32[]{:S(2)}, u32[]{:S(2)}) %collective-permute-start.2) | collective-permute-done | bytes 139296 | tf_op jit(solution)/shard_map/ppermute | solution.py:346
  32.7 5.0 %collective-permute-done.5.rest_6_ = f32[2,136,128]{2,1,0:T(8,128)S(1)} collective-permute-done((f32[2,136,128]{2,1,0:T(8,128)}, f32[2,136,128]{2,1,0:T(8,128)S(1)}, u32[]{:S(2)}, u32[]{:S(2)}) %collective-permute-start.5) | collective-permute-done | bytes 139296 | tf_op jit(solution)/shard_map/ppermute | solution.py:346
  37.7 1.8 %collective-permute-done.6.rest_7_ = f32[2,136,128]{2,1,0:T(8,128)S(1)} collective-permute-done((f32[2,136,128]{2,1,0:T(8,128)}, f32[2,136,128]{2,1,0:T(8,128)S(1)}, u32[]{:S(2)}, u32[]{:S(2)}) %collective-permute-start.6) | collective-permute-done | bytes 139296 | tf_op jit(solution)/shard_map/ppermute | solution.py:346
  40.2 2.6 %weights.1 = (f32[2,256,128]{2,1,0:T(8,128)}, f32[2,256,128]{2,1,0:T(8,128)}, f32[2,256,128]{2,1,0:T(8,128)}, f32[2,256,128]{2,1,0:T(8,128)}, s32[16]{0:T(128)}) custom-call(s32[6,8]{1,0:T(8,128)} %stack.23.info, f32[2,136,128]{2,1,0:T(8,128)} %get-tuple-element.21.rest_0_, f32[2,136,128]{2,1,0:T(8,128)} %copy-done.14, f32[2,136,128]{2,1,0:T(8,128)} %copy-done.15, ...), custom_call_target="tpu_custom_call" | custom-call | tf_op jit(solution)/shard_map/weights/pallas_call | solution.py:374
  43.8 3.0 %image.1 = (f32[8,256,128]{2,1,0:T(8,128)}, f32[8,64,128]{2,1,0:T(8,128)}, f32[8,64,128]{2,1,0:T(8,128)}) custom-call(s32[6,8]{1,0:T(8,128)} %stack.23.info, s32[16]{0:T(128)} %get-tuple-element.29.slot, f32[16,128,128]{2,1,0:T(8,128)} %copy-done, f32[2,256,128]{2,1,0:T(8,128)} %get-tuple-element.30.rest_0_, ...), custom_call_target="tpu_custom_call" | custom-call | tf_op jit(solution)/shard_map/image/pallas_call | solution.py:384
  46.8 2.3 %collective-permute-start.7 = (f32[8,64,128]{2,1,0:T(8,128)}, f32[8,64,128]{2,1,0:T(8,128)S(1)}, u32[]{:S(2)}, u32[]{:S(2)}) collective-permute-start(f32[8,64,128]{2,1,0:T(8,128)} %get-tuple-element.34), channel_id=1, source_target_pairs={{0,1},{1,2},{2,3},{3,4},{4,5},{5,6},{6,7},{8,9},{9,10},{10,11},{11... | collective-permute-start | bytes 786440 | tf_op jit(solution)/shard_map/ppermute | solution.py:393
  50.4 2.5 %spectrum.1.spec = f32[2,192,256]{2,1,0:T(8,128)} custom-call(f32[1,4]{1,0:T(1,128)} %coeffs.1, f32[4,128,128]{2,1,0:T(8,128)} %basis.1, bf16[2,384,128]{2,1,0:T(8,128)(2,1)} %constant.25.clone.row_ker, bf16[2,2,256,256]{3,2,1,0:T(8,128)(2,1)} %constant.26.clone.col_fwd), custom_call_target="tpu_custom_call" | custom-call | tf_op jit(solution)/shard_map/spectrum/pallas_call | solution.py:366
  52.9 3.5 %collective-permute-start.17 = (f32[2,256,128]{2,1,0:T(8,128)}, f32[2,256,128]{2,1,0:T(8,128)S(1)}, u32[]{:S(2)}, u32[]{:S(2)}) collective-permute-start(f32[2,256,128]{2,1,0:T(8,128)} %get-tuple-element.30.rest_0_), channel_id=1, source_target_pairs={{0,8},{24,16},{1,9},{25,17},{2,10},{26,18},{3,11},{27,19},{4,12},{... | collective-permute-start | bytes 786440 | tf_op jit(solution)/shard_map/ppermute | solution.py:289
  57.2 5.3 %shard_map.159 = f32[2,256,128]{2,1,0:T(8,128)} custom-call(s32[6,8]{1,0:T(8,128)} %stack.23.info, f32[8,64,128]{2,1,0:T(8,128)} %copy-done.4, f32[8,256,128]{2,1,0:T(8,128)} %get-tuple-element.35.image, f32[8,64,128]{2,1,0:T(8,128)} %copy-done.5, f32[2,192,256]{2,1,0:T(8,128)} %spectrum.1.spec, bf16[2,384,384]{2,1,0:T(8,128)(2,1)} %constant.24.clone.row_fwd, ...), custom_call_target="tpu_custom_call" | custom-call | tf_op jit(solution)/shard_map/pallas_call | solution.py:400
  64.3 3.6 %collective-permute-start.15 = (f32[2,256,128]{2,1,0:T(8,128)S(1)}, f32[2,256,128]{2,1,0:T(8,128)S(1)}, u32[]{:S(2)}, u32[]{:S(2)}) collective-permute-start(f32[2,256,128]{2,1,0:T(8,128)S(1)} %copy-done.2), channel_id=1, source_target_pairs={{0,8},{8,16},{1,9},{9,17},{2,10},{10,18},{3,11},{11,19},{4,12},{12... | collective-permute-start | bytes 786440 | tf_op jit(solution)/shard_map/ppermute | solution.py:289
  71.0 9.4 %shard_map.158 = (f32[2,256,128]{2,1,0:T(8,128)}, f32[2,256,128]{2,1,0:T(8,128)}, f32[2,256,128]{2,1,0:T(8,128)}) custom-call(s32[6,8]{1,0:T(8,128)} %stack.23.info, f32[8,64,128]{2,1,0:T(8,128)} %copy-done.4, f32[8,256,128]{2,1,0:T(8,128)} %get-tuple-element.35.image, f32[8,64,128]{2,1,0:T(8,128)} %copy-done.5, f32[2,192,256]{2,1,0:T(8,128)} %spectrum.1.spec, ...), custom_call_target="tpu_custom_call" | custom-call | tf_op jit(solution)/shard_map/pallas_call | solution.py:400
  80.5 6.3 %collective-permute-start.10 = (f32[2,256,128]{2,1,0:T(8,128)}, f32[2,256,128]{2,1,0:T(8,128)S(1)}, u32[]{:S(2)}, u32[]{:S(2)}) collective-permute-start(f32[2,256,128]{2,1,0:T(8,128)} %get-tuple-element.39), channel_id=1, source_target_pairs={{0,8},{8,16},{1,9},{9,17},{2,10},{10,18},{3,11},{11,19},{4,12},{12... | collective-permute-start | bytes 786440 | tf_op jit(solution)/shard_map/ppermute | solution.py:289
  87.6 3.3 %collective-permute-start.9 = (f32[2,256,128]{2,1,0:T(8,128)S(1)}, f32[2,256,128]{2,1,0:T(8,128)S(1)}, u32[]{:S(2)}, u32[]{:S(2)}) collective-permute-start(f32[2,256,128]{2,1,0:T(8,128)S(1)} %copy-done.24), channel_id=1, source_target_pairs={{0,16},{8,0},{16,24},{24,8},{1,17},{9,1},{17,25},{25,9},{2,18},{10... | collective-permute-start | bytes 786440 | tf_op jit(solution)/shard_map/ppermute | solution.py:289
  92.9 2.0 %weight_map.1.refs_5_ = f32[256,256]{1,0:T(8,128)} custom-call(f32[2,256,128]{2,1,0:T(8,128)} %get-tuple-element.33.rest_3_.rest_2_.refs_0_, f32[2,256,128]{2,1,0:T(8,128)} %copy-done.10, f32[2,256,128]{2,1,0:T(8,128)} %copy-done.11, f32[2,256,128]{2,1,0:T(8,128)} %copy-done.12, f32[2,256,128]{2,1,0:T(8,128)} %copy-done.13), custom_call_target="tpu_custom_call" | custom-call | tf_op jit(solution)/shard_map/weight_map/pallas_call | solution.py:395
  95.0 3.5 %collective-permute-done.9.refs_1_ = f32[2,256,128]{2,1,0:T(8,128)S(1)} collective-permute-done((f32[2,256,128]{2,1,0:T(8,128)S(1)}, f32[2,256,128]{2,1,0:T(8,128)S(1)}, u32[]{:S(2)}, u32[]{:S(2)}) %collective-permute-start.9) | collective-permute-done | bytes 262176 | tf_op jit(solution)/shard_map/ppermute | solution.py:289
  98.5 10.1 %collective-permute-done.13.refs_4_ = f32[2,256,128]{2,1,0:T(8,128)S(1)} collective-permute-done((f32[2,256,128]{2,1,0:T(8,128)S(1)}, f32[2,256,128]{2,1,0:T(8,128)S(1)}, u32[]{:S(2)}, u32[]{:S(2)}) %collective-permute-start.13) | collective-permute-done | bytes 262176 | tf_op jit(solution)/shard_map/ppermute | solution.py:289
  109.3 2.1 %coadd.1 = f32[256,256]{1,0:T(8,128)} custom-call(f32[2,256,128]{2,1,0:T(8,128)} %get-tuple-element.37.refs_0_, f32[2,256,128]{2,1,0:T(8,128)} %copy-done.8, f32[2,256,128]{2,1,0:T(8,128)} %copy-done.6, f32[2,256,128]{2,1,0:T(8,128)} %copy-done.7, f32[2,256,128]{2,1,0:T(8,128)} %copy-done.9, f32[256,256]{1,0:T(8,128)} %weight_map.1.refs_5_), custom_call_target="tpu_custom_call" | custom-call | tf_op jit(solution)/shard_map/coadd/pallas_call | solution.py:414
  (84 shorter events, 15.3 us)
Async XLA Ops:
  7.5 35.2 %all-to-all-start = ((f32[16,128,128]{2,1,0:T(8,128)}), f32[16,128,128]{2,1,0:T(8,128)S(1)}, u32[]{:S(2)}, u32[]{:S(2)}) async-start(f32[16,128,128]{2,1,0:T(8,128)} %warp_flux.1), calls=%async_computation | async-start | bytes 2097152 | tf_op jit(solution)/shard_map/all_to_all | solution.py:365
  16.9 4.1 %collective-permute-start = (f32[2,136,128]{2,1,0:T(8,128)}, f32[2,136,128]{2,1,0:T(8,128)S(1)}, u32[]{:S(2)}, u32[]{:S(2)}) collective-permute-start(f32[2,136,128]{2,1,0:T(8,128)} %get-tuple-element.22), channel_id=1, source_target_pairs={{0,1},{1,0},{2,3},{3,2},{4,5},{5,4},{6,7},{7,6},{8,9},{9,8},{10,11... | collective-permute-start | bytes 417800 | tf_op jit(solution)/shard_map/ppermute | solution.py:346
  17.5 13.3 %collective-permute-start.1 = (f32[2,136,128]{2,1,0:T(8,128)}, f32[2,136,128]{2,1,0:T(8,128)S(1)}, u32[]{:S(2)}, u32[]{:S(2)}) collective-permute-start(f32[2,136,128]{2,1,0:T(8,128)} %get-tuple-element.23), channel_id=1, source_target_pairs={{0,2},{1,3},{2,0},{3,1},{4,6},{5,7},{6,4},{7,5},{8,10},{9,11},{10,... | collective-permute-start | bytes 417800 | tf_op jit(solution)/shard_map/ppermute | solution.py:346
  19.1 13.5 %collective-permute-start.2 = (f32[2,136,128]{2,1,0:T(8,128)}, f32[2,136,128]{2,1,0:T(8,128)S(1)}, u32[]{:S(2)}, u32[]{:S(2)}) collective-permute-start(f32[2,136,128]{2,1,0:T(8,128)} %get-tuple-element.24), channel_id=1, source_target_pairs={{0,3},{1,2},{2,1},{3,0},{4,7},{5,6},{6,5},{7,4},{8,11},{9,10},{10,... | collective-permute-start | bytes 417800 | tf_op jit(solution)/shard_map/ppermute | solution.py:346
  19.1 13.5 %collective-permute-start.3 = (f32[2,136,128]{2,1,0:T(8,128)}, f32[2,136,128]{2,1,0:T(8,128)S(1)}, u32[]{:S(2)}, u32[]{:S(2)}) collective-permute-start(f32[2,136,128]{2,1,0:T(8,128)} %get-tuple-element.25), channel_id=1, source_target_pairs={{0,4},{1,5},{2,6},{3,7},{4,0},{5,1},{6,2},{7,3},{8,12},{9,13},{10,... | collective-permute-start | bytes 417800 | tf_op jit(solution)/shard_map/ppermute | solution.py:346
  20.9 11.8 %collective-permute-start.4 = (f32[2,136,128]{2,1,0:T(8,128)}, f32[2,136,128]{2,1,0:T(8,128)S(1)}, u32[]{:S(2)}, u32[]{:S(2)}) collective-permute-start(f32[2,136,128]{2,1,0:T(8,128)} %get-tuple-element.26), channel_id=1, source_target_pairs={{0,5},{1,4},{2,7},{3,6},{4,1},{5,0},{6,3},{7,2},{8,13},{9,12},{10,... | collective-permute-start | bytes 417800 | tf_op jit(solution)/shard_map/ppermute | solution.py:346
  21.0 18.6 %copy-start.14 = (f32[2,136,128]{2,1,0:T(8,128)}, f32[2,136,128]{2,1,0:T(8,128)S(1)}, u32[]{:S(2)}) copy-start(f32[2,136,128]{2,1,0:T(8,128)S(1)} %collective-permute-done.rest_1_) | copy-start | bytes 417796
  21.0 16.7 %collective-permute-start.5 = (f32[2,136,128]{2,1,0:T(8,128)}, f32[2,136,128]{2,1,0:T(8,128)S(1)}, u32[]{:S(2)}, u32[]{:S(2)}) collective-permute-start(f32[2,136,128]{2,1,0:T(8,128)} %get-tuple-element.27), channel_id=1, source_target_pairs={{0,6},{1,7},{2,4},{3,5},{4,2},{5,3},{6,0},{7,1},{8,14},{9,15},{10,... | collective-permute-start | bytes 417800 | tf_op jit(solution)/shard_map/ppermute | solution.py:346
  30.8 8.7 %collective-permute-start.6 = (f32[2,136,128]{2,1,0:T(8,128)}, f32[2,136,128]{2,1,0:T(8,128)S(1)}, u32[]{:S(2)}, u32[]{:S(2)}) collective-permute-start(f32[2,136,128]{2,1,0:T(8,128)} %get-tuple-element.28), channel_id=1, source_target_pairs={{0,7},{1,6},{2,5},{3,4},{4,3},{5,2},{6,1},{7,0},{8,15},{9,14},{10,... | collective-permute-start | bytes 417800 | tf_op jit(solution)/shard_map/ppermute | solution.py:346
  46.8 9.7 %collective-permute-start.7 = (f32[8,64,128]{2,1,0:T(8,128)}, f32[8,64,128]{2,1,0:T(8,128)S(1)}, u32[]{:S(2)}, u32[]{:S(2)}) collective-permute-start(f32[8,64,128]{2,1,0:T(8,128)} %get-tuple-element.34), channel_id=1, source_target_pairs={{0,1},{1,2},{2,3},{3,4},{4,5},{5,6},{6,7},{8,9},{9,10},{10,11},{11... | collective-permute-start | bytes 786440 | tf_op jit(solution)/shard_map/ppermute | solution.py:393
  49.1 7.4 %collective-permute-start.8 = (f32[8,64,128]{2,1,0:T(8,128)}, f32[8,64,128]{2,1,0:T(8,128)S(1)}, u32[]{:S(2)}, u32[]{:S(2)}) collective-permute-start(f32[8,64,128]{2,1,0:T(8,128)} %get-tuple-element.36), channel_id=1, source_target_pairs={{1,0},{2,1},{3,2},{4,3},{5,4},{6,5},{7,6},{9,8},{10,9},{11,10},{12... | collective-permute-start | bytes 786440 | tf_op jit(solution)/shard_map/ppermute | solution.py:394
  52.9 15.6 %collective-permute-start.17 = (f32[2,256,128]{2,1,0:T(8,128)}, f32[2,256,128]{2,1,0:T(8,128)S(1)}, u32[]{:S(2)}, u32[]{:S(2)}) collective-permute-start(f32[2,256,128]{2,1,0:T(8,128)} %get-tuple-element.30.rest_0_), channel_id=1, source_target_pairs={{0,8},{24,16},{1,9},{25,17},{2,10},{26,18},{3,11},{27,19},{4,12},{... | collective-permute-start | bytes 786440 | tf_op jit(solution)/shard_map/ppermute | solution.py:289
  62.6 17.8 %collective-permute-start.12 = (f32[2,256,128]{2,1,0:T(8,128)}, f32[2,256,128]{2,1,0:T(8,128)S(1)}, u32[]{:S(2)}, u32[]{:S(2)}) collective-permute-start(f32[2,256,128]{2,1,0:T(8,128)} %shard_map.159), channel_id=1, source_target_pairs={{0,8},{24,16},{1,9},{25,17},{2,10},{26,18},{3,11},{27,19},{4,12},{... | collective-permute-start | bytes 786440 | tf_op jit(solution)/shard_map/ppermute | solution.py:289
  63.9 22.9 %collective-permute-start.14 = (f32[2,256,128]{2,1,0:T(8,128)S(1)}, f32[2,256,128]{2,1,0:T(8,128)S(1)}, u32[]{:S(2)}, u32[]{:S(2)}) collective-permute-start(f32[2,256,128]{2,1,0:T(8,128)S(1)} %copy-done.3), channel_id=1, source_target_pairs={{0,16},{8,0},{16,24},{24,8},{1,17},{9,1},{17,25},{25,9},{2,18},{10... | collective-permute-start | bytes 786440 | tf_op jit(solution)/shard_map/ppermute | solution.py:289
  64.3 23.2 %collective-permute-start.15 = (f32[2,256,128]{2,1,0:T(8,128)S(1)}, f32[2,256,128]{2,1,0:T(8,128)S(1)}, u32[]{:S(2)}, u32[]{:S(2)}) collective-permute-start(f32[2,256,128]{2,1,0:T(8,128)S(1)} %copy-done.2), channel_id=1, source_target_pairs={{0,8},{8,16},{1,9},{9,17},{2,10},{10,18},{3,11},{11,19},{4,12},{12... | collective-permute-start | bytes 786440 | tf_op jit(solution)/shard_map/ppermute | solution.py:289
  67.9 23.0 %collective-permute-start.16 = (f32[2,256,128]{2,1,0:T(8,128)S(1)}, f32[2,256,128]{2,1,0:T(8,128)S(1)}, u32[]{:S(2)}, u32[]{:S(2)}) collective-permute-start(f32[2,256,128]{2,1,0:T(8,128)S(1)} %copy-done.2), channel_id=1, source_target_pairs={{16,8},{24,16},{17,9},{25,17},{18,10},{26,18},{19,11},{27,19},{20,... | collective-permute-start | bytes 786440 | tf_op jit(solution)/shard_map/ppermute | solution.py:289
  69.6 17.2 %copy-start.1 = (f32[2,256,128]{2,1,0:T(8,128)S(1)}, f32[2,256,128]{2,1,0:T(8,128)}, u32[]{:S(2)}) copy-start(f32[2,256,128]{2,1,0:T(8,128)} %shard_map.159) | copy-start | bytes 786436
  69.6 22.6 %collective-permute-start.18 = (f32[2,256,128]{2,1,0:T(8,128)S(1)}, f32[2,256,128]{2,1,0:T(8,128)S(1)}, u32[]{:S(2)}, u32[]{:S(2)}) collective-permute-start(f32[2,256,128]{2,1,0:T(8,128)S(1)} %add.13), channel_id=1, source_target_pairs={{8,24},{16,0},{9,25},{17,1},{10,26},{18,2},{11,27},{19,3},{12,28},... | collective-permute-start | bytes 786440 | tf_op jit(solution)/shard_map/ppermute | solution.py:289
  80.5 14.5 %collective-permute-start.10 = (f32[2,256,128]{2,1,0:T(8,128)}, f32[2,256,128]{2,1,0:T(8,128)S(1)}, u32[]{:S(2)}, u32[]{:S(2)}) collective-permute-start(f32[2,256,128]{2,1,0:T(8,128)} %get-tuple-element.39), channel_id=1, source_target_pairs={{0,8},{8,16},{1,9},{9,17},{2,10},{10,18},{3,11},{11,19},{4,12},{12... | collective-permute-start | bytes 786440 | tf_op jit(solution)/shard_map/ppermute | solution.py:289
  86.9 8.1 %collective-permute-start.11 = (f32[2,256,128]{2,1,0:T(8,128)S(1)}, f32[2,256,128]{2,1,0:T(8,128)S(1)}, u32[]{:S(2)}, u32[]{:S(2)}) collective-permute-start(f32[2,256,128]{2,1,0:T(8,128)S(1)} %copy-done.25), channel_id=1, source_target_pairs={{16,8},{24,16},{17,9},{25,17},{18,10},{26,18},{19,11},{27,19},{20,... | collective-permute-start | bytes 786440 | tf_op jit(solution)/shard_map/ppermute | solution.py:289
  87.6 10.9 %collective-permute-start.9 = (f32[2,256,128]{2,1,0:T(8,128)S(1)}, f32[2,256,128]{2,1,0:T(8,128)S(1)}, u32[]{:S(2)}, u32[]{:S(2)}) collective-permute-start(f32[2,256,128]{2,1,0:T(8,128)S(1)} %copy-done.24), channel_id=1, source_target_pairs={{0,16},{8,0},{16,24},{24,8},{1,17},{9,1},{17,25},{25,9},{2,18},{10... | collective-permute-start | bytes 786440 | tf_op jit(solution)/shard_map/ppermute | solution.py:289
  90.9 17.7 %collective-permute-start.13 = (f32[2,256,128]{2,1,0:T(8,128)S(1)}, f32[2,256,128]{2,1,0:T(8,128)S(1)}, u32[]{:S(2)}, u32[]{:S(2)}) collective-permute-start(f32[2,256,128]{2,1,0:T(8,128)S(1)} %add.12), channel_id=1, source_target_pairs={{8,24},{16,0},{9,25},{17,1},{10,26},{18,2},{11,27},{19,3},{12,28},... | collective-permute-start | bytes 786440 | tf_op jit(solution)/shard_map/ppermute | solution.py:289
  95.0 13.6 %copy-start.6 = (f32[2,256,128]{2,1,0:T(8,128)}, f32[2,256,128]{2,1,0:T(8,128)S(1)}, u32[]{:S(2)}) copy-start(f32[2,256,128]{2,1,0:T(8,128)S(1)} %collective-permute-done.10.refs_2_) | copy-start | bytes 786436
  95.0 13.6 %copy-start.7 = (f32[2,256,128]{2,1,0:T(8,128)}, f32[2,256,128]{2,1,0:T(8,128)S(1)}, u32[]{:S(2)}) copy-start(f32[2,256,128]{2,1,0:T(8,128)S(1)} %collective-permute-done.11.refs_3_) | copy-start | bytes 786436
  (22 other events, 86.5 us)

commit v2 on v1

--- a/solution.py
+++ b/solution.py
@@ -15,6 +15,7 @@
 BC = 8
 CAP = 2
 LANES = 128
+VMEM_BYTES = 12 * 2**20
 META = 8
 
 
@@ -335,6 +336,8 @@
         ]
     )
 
+    params = pltpu.CompilerParams(vmem_limit_bytes=VMEM_BYTES)
+
     def arr(*shape):
         return jax.ShapeDtypeStruct(shape, F32)
 
@@ -352,6 +355,7 @@
         in_specs=[SMEM] + [VMEM] * 3,
         out_specs=[hbm] * owners,
         scratch_shapes=[pltpu.VMEM((owners, CAP, side + META, side), F32), pltpu.SemaphoreType.DMA((owners,))],
+        compiler_params=params,
         name="warp_weight",
     )(info, piece_ivar, warp_rows, warp_cols)
     got_weight = exchange(sent_weight)
@@ -360,6 +364,7 @@
         out_shape=arr(cap, side, side),
         in_specs=[SMEM] + [VMEM] * 4,
         out_specs=VMEM,
+        compiler_params=params,
         name="warp_flux",
     )(info, piece_flux, piece_ivar, warp_rows, warp_cols)
     got_flux = lax.all_to_all(sent_flux, "bulk", split_axis=0, concat_axis=0, tiled=True)
@@ -368,6 +373,7 @@
         out_shape=arr(2, freqs, 2 * side),
         in_specs=[SMEM] + [VMEM] * 3,
         out_specs=VMEM,
+        compiler_params=params,
         name="spectrum",
     )(coeffs, basis, row_ker, col_fwd)
     tile = arr(per_tile, rows_dev, side)
@@ -377,6 +383,7 @@
         in_specs=[SMEM] + [VMEM] * owners,
         out_specs=[VMEM] * visits + [SMEM],
         scratch_shapes=[pltpu.VMEM((BR * BC + 1, side, side), F32)],
+        compiler_params=params,
         name="weights",
     )(info, *got_weight)
     weight_sum = VisitSum(visits)
@@ -387,13 +394,14 @@
         in_specs=[SMEM] * 2 + [VMEM] * (1 + visits),
         out_specs=[VMEM] * 3,
         scratch_shapes=[pltpu.VMEM((BR * BC + 1, side, side), F32)],
+        compiler_params=params,
         name="image",
     )(info, slots, got_flux, *ivar)
     ends = owners - 1
     above = lax.ppermute(bottom, "bulk", [(i, i + 1) for i in range(ends)])
     below = lax.ppermute(top, "bulk", [(i + 1, i) for i in range(ends)])
     weight_map = pl.pallas_call(
-        total_body, out_shape=arr(rows_dev, per_tile * side), name="weight_map"
+        total_body, out_shape=arr(rows_dev, per_tile * side), compiler_params=params, name="weight_map"
     )(*weight_sum.parts())
 
     def convolve(first, count, blocks):
@@ -403,6 +411,7 @@
             in_specs=[SMEM] + [VMEM] * (8 + count),
             out_specs=[VMEM] * count,
             scratch_shapes=[pltpu.VMEM((blocks, 2 * freqs, side), F32)],
+            compiler_params=params,
         )(
             info, above, image, below, spec, row_fwd, col_fwd, col_inv, row_inv,
             *ivar[first : first + count],
@@ -412,7 +421,7 @@
     image_sum.push(*convolve(0, 1, per_tile + 1))
     image_sum.push(*convolve(1, visits - 1, BC + 1))
     coadd = pl.pallas_call(
-        ratio_body, out_shape=arr(rows_dev, per_tile * side), name="coadd"
+        ratio_body, out_shape=arr(rows_dev, per_tile * side), compiler_params=params, name="coadd"
     )(*image_sum.parts(), weight_map)
     return (coadd, weight_map)
 

time: 113 us -> 104 us (0.920)
  the two profiles are of different devices: /device:TPU:0 before, /device:TPU:4 now
where the time goes in v2:
time: 104 us; the launch traced here: 103 us
  starting transfers between devices  39.7 us (38%)
  waiting for transfers between devices  33 us (32%)
  Pallas kernels  22.4 us (22%)
  local copies, waits for them, and re-layouts  7.24 us (7%)
    ppermute x10, starting transfers between devices, send(): self.sent += [lax.ppermute(tile, 'visit', route) for route in routes]  23.6 us
    ppermute x10, waiting for transfers between devices, send(): self.sent += [lax.ppermute(tile, 'visit', route) for route in routes]  16.7 us
    ppermute x7, waiting for transfers between devices, exchange(): lax.ppermute(sent[d], 'bulk', [(i, i ^ d) for i in range(owners)])  16.3 us
    pallas_call x2, Pallas kernels, convolve(): pl.pallas_call(functools.partial(conv_body, first), out_shape=[tile] * co...  10.1 us
    unnamed x36, local copies, waits for them, and re-layouts  6.51 us
    ppermute x7, starting transfers between devices, exchange(): lax.ppermute(sent[d], 'bulk', [(i, i ^ d) for i in range(owners)])  5.14 us
    all_to_all x1, starting transfers between devices, coadd_patches(): lax.all_to_all(sent_flux, 'bulk', split_axis=0, concat_axis=0, tiled=True)  4.36 us
    ppermute x1, starting transfers between devices, coadd_patches(): below = lax.ppermute(top, 'bulk', [(i + 1, i) for i in range(ends)])  4.29 us
  transfers between devices with their start and end apart: 20, of which 7 were waited for; matrix products, arithmetic and copies ran while one was open for 0% of the time, Pallas kernels for 17%

profile of v2, /device:TPU:4, one launch (start us, length us, event | category | flops | bytes accessed | tf_op | source)
XLA Modules:
  0.0 103.3 jit_solution(10928405942293465194)
XLA Ops:
  6.9 3.3 %warp_flux.1 = f32[16,128,128]{2,1,0:T(8,128)} custom-call(s32[6,8]{1,0:T(8,128)S(1)} %stack.23.info, f32[1,1,8,128,128]{4,3,2,1,0:T(8,128)S(1)} %copy-done.11, f32[1,1,8,128,128]{4,3,2,1,0:T(8,128)S(1)} %copy-done.2, f32[1,1,8,128,128]{4,3,2,1,0:T(8,128)S(1)} %copy-done.4, f32[1,1,8,128,128]{4,3,2,1,0:T(8,128)S(1)} %copy-done.6), custom_call_target="tpu_custom_call" | custom-call | tf_op jit(solution)/shard_map/warp_flux/pallas_call | solution.py:362
  10.2 4.4 %all-to-all-start = ((f32[16,128,128]{2,1,0:T(8,128)}), f32[16,128,128]{2,1,0:T(8,128)S(1)}, u32[]{:S(2)}, u32[]{:S(2)}) async-start(f32[16,128,128]{2,1,0:T(8,128)} %warp_flux.1), calls=%async_computation | async-start | bytes 2097152 | tf_op jit(solution)/shard_map/all_to_all | solution.py:370
  14.6 3.9 %warp_weight.1 = (f32[2,136,128]{2,1,0:T(8,128)S(1)}, f32[2,136,128]{2,1,0:T(8,128)S(1)}, f32[2,136,128]{2,1,0:T(8,128)S(1)}, f32[2,136,128]{2,1,0:T(8,128)S(1)}...) custom-call(s32[6,8]{1,0:T(8,128)S(1)} %stack.23.info, ...), custom_call_target="tpu_custom_call" | custom-call | tf_op jit(solution)/shard_map/warp_weight/pallas_call | solution.py:352
  18.6 1.5 %collective-permute-start.1 = (f32[2,136,128]{2,1,0:T(8,128)S(1)}, f32[2,136,128]{2,1,0:T(8,128)S(1)}, u32[]{:S(2)}, u32[]{:S(2)}) collective-permute-start(f32[2,136,128]{2,1,0:T(8,128)S(1)} %get-tuple-element.23), channel_id=1, source_target_pairs={{0,2},{1,3},{2,0},{3,1},{4,6},{5,7},{6,4},{7,5},{8,10},{9,11},{10,... | collective-permute-start | bytes 417800 | tf_op jit(solution)/shard_map/ppermute | solution.py:349
  20.7 1.5 %collective-permute-start.4 = (f32[2,136,128]{2,1,0:T(8,128)S(1)}, f32[2,136,128]{2,1,0:T(8,128)S(1)}, u32[]{:S(2)}, u32[]{:S(2)}) collective-permute-start(f32[2,136,128]{2,1,0:T(8,128)S(1)} %get-tuple-element.26), channel_id=1, source_target_pairs={{0,5},{1,4},{2,7},{3,6},{4,1},{5,0},{6,3},{7,2},{8,13},{9,12},{10,... | collective-permute-start | bytes 417800 | tf_op jit(solution)/shard_map/ppermute | solution.py:349
  22.1 1.5 %collective-permute-start.5 = (f32[2,136,128]{2,1,0:T(8,128)S(1)}, f32[2,136,128]{2,1,0:T(8,128)S(1)}, u32[]{:S(2)}, u32[]{:S(2)}) collective-permute-start(f32[2,136,128]{2,1,0:T(8,128)S(1)} %get-tuple-element.27), channel_id=1, source_target_pairs={{0,6},{1,7},{2,4},{3,5},{4,2},{5,3},{6,0},{7,1},{8,14},{9,15},{10,... | collective-permute-start | bytes 417800 | tf_op jit(solution)/shard_map/ppermute | solution.py:349
  23.6 8.5 %collective-permute-done.1.rest_2_ = f32[2,136,128]{2,1,0:T(8,128)S(1)} collective-permute-done((f32[2,136,128]{2,1,0:T(8,128)S(1)}, f32[2,136,128]{2,1,0:T(8,128)S(1)}, u32[]{:S(2)}, u32[]{:S(2)}) %collective-permute-start.1) | collective-permute-done | bytes 139296 | tf_op jit(solution)/shard_map/ppermute | solution.py:349
  32.1 1.8 %collective-permute-done.2.rest_3_ = f32[2,136,128]{2,1,0:T(8,128)S(1)} collective-permute-done((f32[2,136,128]{2,1,0:T(8,128)S(1)}, f32[2,136,128]{2,1,0:T(8,128)S(1)}, u32[]{:S(2)}, u32[]{:S(2)}) %collective-permute-start.2) | collective-permute-done | bytes 139296 | tf_op jit(solution)/shard_map/ppermute | solution.py:349
  33.9 4.1 %collective-permute-done.5.rest_6_ = f32[2,136,128]{2,1,0:T(8,128)S(1)} collective-permute-done((f32[2,136,128]{2,1,0:T(8,128)S(1)}, f32[2,136,128]{2,1,0:T(8,128)S(1)}, u32[]{:S(2)}, u32[]{:S(2)}) %collective-permute-start.5) | collective-permute-done | bytes 139296 | tf_op jit(solution)/shard_map/ppermute | solution.py:349
  38.1 1.8 %collective-permute-done.6.rest_7_ = f32[2,136,128]{2,1,0:T(8,128)S(1)} collective-permute-done((f32[2,136,128]{2,1,0:T(8,128)S(1)}, f32[2,136,128]{2,1,0:T(8,128)S(1)}, u32[]{:S(2)}, u32[]{:S(2)}) %collective-permute-start.6) | collective-permute-done | bytes 139296 | tf_op jit(solution)/shard_map/ppermute | solution.py:349
  39.9 1.4 %weights.1 = (f32[2,256,128]{2,1,0:T(8,128)S(1)}, f32[2,256,128]{2,1,0:T(8,128)S(1)}, f32[2,256,128]{2,1,0:T(8,128)S(1)}, f32[2,256,128]{2,1,0:T(8,128)S(1)}, s32[16]{0:T(128)S(1)}) custom-call(s32[6,8]{1,0:T(8,128)S(1)} %stack.23.info, f32[2,136,128]{2,1,0:T(8,128)S(1)} %get-tuple-element.21.rest_0_, f32[2,136,128]{2,1,0:T(8,128)S(1)} %collective-permute-done.rest_1_, ...), custom_call_target="tpu_custom_call" | custom-call | tf_op jit(solution)/shard_map/weights/pallas_call | solution.py:380
  42.4 2.3 %collective-permute-start.7 = (f32[8,64,128]{2,1,0:T(8,128)S(1)}, f32[8,64,128]{2,1,0:T(8,128)S(1)}, u32[]{:S(2)}, u32[]{:S(2)}) collective-permute-start(f32[8,64,128]{2,1,0:T(8,128)S(1)} %get-tuple-element.34), channel_id=1, source_target_pairs={{0,1},{1,2},{2,3},{3,4},{4,5},{5,6},{6,7},{8,9},{9,10},{10,11},{11... | collective-permute-start | bytes 786440 | tf_op jit(solution)/shard_map/ppermute | solution.py:401
  44.7 4.3 %collective-permute-start.8 = (f32[8,64,128]{2,1,0:T(8,128)S(1)}, f32[8,64,128]{2,1,0:T(8,128)S(1)}, u32[]{:S(2)}, u32[]{:S(2)}) collective-permute-start(f32[8,64,128]{2,1,0:T(8,128)S(1)} %get-tuple-element.36), channel_id=1, source_target_pairs={{1,0},{2,1},{3,2},{4,3},{5,4},{6,5},{7,6},{9,8},{10,9},{11,10},{12... | collective-permute-start | bytes 786440 | tf_op jit(solution)/shard_map/ppermute | solution.py:402
  50.1 3.5 %collective-permute-start.17 = (f32[2,256,128]{2,1,0:T(8,128)S(1)}, f32[2,256,128]{2,1,0:T(8,128)S(1)}, u32[]{:S(2)}, u32[]{:S(2)}) collective-permute-start(f32[2,256,128]{2,1,0:T(8,128)S(1)} %get-tuple-element.30.rest_0_), channel_id=1, source_target_pairs={{0,8},{24,16},{1,9},{25,17},{2,10},{26,18},{3,11},{27,19},{4,12},{... | collective-permute-start | bytes 786440 | tf_op jit(solution)/shard_map/ppermute | solution.py:290
  53.7 3.0 %shard_map.159 = f32[2,256,128]{2,1,0:T(8,128)S(1)} custom-call(s32[6,8]{1,0:T(8,128)S(1)} %stack.23.info, f32[8,64,128]{2,1,0:T(8,128)S(1)} %collective-permute-done.7.above, f32[8,256,128]{2,1,0:T(8,128)S(1)} %get-tuple-element.35.image, f32[8,64,128]{2,1,0:T(8,128)S(1)} %collective-permute-done.8.below, f32[2,192,256]{2,1,0:T(8,128)S(1)} %spectrum.1.spec, ...), custom_call_target="tpu_custom_call" | custom-call | tf_op jit(solution)/shard_map/pallas_call | solution.py:408
  56.7 2.7 %collective-permute-start.12 = (f32[2,256,128]{2,1,0:T(8,128)S(1)}, f32[2,256,128]{2,1,0:T(8,128)S(1)}, u32[]{:S(2)}, u32[]{:S(2)}) collective-permute-start(f32[2,256,128]{2,1,0:T(8,128)S(1)} %shard_map.159), channel_id=1, source_target_pairs={{0,8},{24,16},{1,9},{25,17},{2,10},{26,18},{3,11},{27,19},{4,12},{... | collective-permute-start | bytes 786440 | tf_op jit(solution)/shard_map/ppermute | solution.py:290
  59.8 3.5 %collective-permute-start.15 = (f32[2,256,128]{2,1,0:T(8,128)S(1)}, f32[2,256,128]{2,1,0:T(8,128)S(1)}, u32[]{:S(2)}, u32[]{:S(2)}) collective-permute-start(f32[2,256,128]{2,1,0:T(8,128)S(1)} %get-tuple-element.32.rest_2_.rest_1_), channel_id=1, source_target_pairs={{0,8},{8,16},{1,9},{9,17},{2,10},{10,18},{3,11},{11,19},{4,12},{12... | collective-permute-start | bytes 786440 | tf_op jit(solution)/shard_map/ppermute | solution.py:290
  64.1 1.3 %collective-permute-start.18 = (f32[2,256,128]{2,1,0:T(8,128)S(1)}, f32[2,256,128]{2,1,0:T(8,128)S(1)}, u32[]{:S(2)}, u32[]{:S(2)}) collective-permute-start(f32[2,256,128]{2,1,0:T(8,128)S(1)} %add.13), channel_id=1, source_target_pairs={{8,24},{16,0},{9,25},{17,1},{10,26},{18,2},{11,27},{19,3},{12,28},... | collective-permute-start | bytes 786440 | tf_op jit(solution)/shard_map/ppermute | solution.py:290
  65.4 7.1 %shard_map.158 = (f32[2,256,128]{2,1,0:T(8,128)S(1)}, f32[2,256,128]{2,1,0:T(8,128)S(1)}, f32[2,256,128]{2,1,0:T(8,128)S(1)}) custom-call(s32[6,8]{1,0:T(8,128)S(1)} %stack.23.info, f32[8,64,128]{2,1,0:T(8,128)S(1)} %collective-permute-done.7.above, f32[8,256,128]{2,1,0:T(8,128)S(1)} %get-tuple-element.35.image, ...), custom_call_target="tpu_custom_call" | custom-call | tf_op jit(solution)/shard_map/pallas_call | solution.py:408
  72.5 6.2 %collective-permute-start.10 = (f32[2,256,128]{2,1,0:T(8,128)S(1)}, f32[2,256,128]{2,1,0:T(8,128)S(1)}, u32[]{:S(2)}, u32[]{:S(2)}) collective-permute-start(f32[2,256,128]{2,1,0:T(8,128)S(1)} %get-tuple-element.39), channel_id=1, source_target_pairs={{0,8},{8,16},{1,9},{9,17},{2,10},{10,18},{3,11},{11,19},{4,12},{12... | collective-permute-start | bytes 786440 | tf_op jit(solution)/shard_map/ppermute | solution.py:290
  79.5 3.3 %collective-permute-start.9 = (f32[2,256,128]{2,1,0:T(8,128)S(1)}, f32[2,256,128]{2,1,0:T(8,128)S(1)}, u32[]{:S(2)}, u32[]{:S(2)}) collective-permute-start(f32[2,256,128]{2,1,0:T(8,128)S(1)} %get-tuple-element.38), channel_id=1, source_target_pairs={{0,16},{8,0},{16,24},{24,8},{1,17},{9,1},{17,25},{25,9},{2,18},{10... | collective-permute-start | bytes 786440 | tf_op jit(solution)/shard_map/ppermute | solution.py:290
  84.1 1.5 %collective-permute-done.18.refs_4_ = f32[2,256,128]{2,1,0:T(8,128)S(1)} collective-permute-done((f32[2,256,128]{2,1,0:T(8,128)S(1)}, f32[2,256,128]{2,1,0:T(8,128)S(1)}, u32[]{:S(2)}, u32[]{:S(2)}) %collective-permute-start.18) | collective-permute-done | bytes 262176 | tf_op jit(solution)/shard_map/ppermute | solution.py:290
  86.4 3.9 %collective-permute-done.9.refs_1_ = f32[2,256,128]{2,1,0:T(8,128)S(1)} collective-permute-done((f32[2,256,128]{2,1,0:T(8,128)S(1)}, f32[2,256,128]{2,1,0:T(8,128)S(1)}, u32[]{:S(2)}, u32[]{:S(2)}) %collective-permute-start.9) | collective-permute-done | bytes 262176 | tf_op jit(solution)/shard_map/ppermute | solution.py:290
  90.3 11.3 %collective-permute-done.13.refs_4_ = f32[2,256,128]{2,1,0:T(8,128)S(1)} collective-permute-done((f32[2,256,128]{2,1,0:T(8,128)S(1)}, f32[2,256,128]{2,1,0:T(8,128)S(1)}, u32[]{:S(2)}, u32[]{:S(2)}) %collective-permute-start.13) | collective-permute-done | bytes 262176 | tf_op jit(solution)/shard_map/ppermute | solution.py:290
  (68 shorter events, 14.8 us)
Async XLA Ops:
  10.2 31.1 %all-to-all-start = ((f32[16,128,128]{2,1,0:T(8,128)}), f32[16,128,128]{2,1,0:T(8,128)S(1)}, u32[]{:S(2)}, u32[]{:S(2)}) async-start(f32[16,128,128]{2,1,0:T(8,128)} %warp_flux.1), calls=%async_computation | async-start | bytes 2097152 | tf_op jit(solution)/shard_map/all_to_all | solution.py:370
  18.5 3.7 %collective-permute-start = (f32[2,136,128]{2,1,0:T(8,128)S(1)}, f32[2,136,128]{2,1,0:T(8,128)S(1)}, u32[]{:S(2)}, u32[]{:S(2)}) collective-permute-start(f32[2,136,128]{2,1,0:T(8,128)S(1)} %get-tuple-element.22), channel_id=1, source_target_pairs={{0,1},{1,0},{2,3},{3,2},{4,5},{5,4},{6,7},{7,6},{8,9},{9,8},{10,11... | collective-permute-start | bytes 417800 | tf_op jit(solution)/shard_map/ppermute | solution.py:349
  18.6 13.5 %collective-permute-start.1 = (f32[2,136,128]{2,1,0:T(8,128)S(1)}, f32[2,136,128]{2,1,0:T(8,128)S(1)}, u32[]{:S(2)}, u32[]{:S(2)}) collective-permute-start(f32[2,136,128]{2,1,0:T(8,128)S(1)} %get-tuple-element.23), channel_id=1, source_target_pairs={{0,2},{1,3},{2,0},{3,1},{4,6},{5,7},{6,4},{7,5},{8,10},{9,11},{10,... | collective-permute-start | bytes 417800 | tf_op jit(solution)/shard_map/ppermute | solution.py:349
  20.1 13.8 %collective-permute-start.2 = (f32[2,136,128]{2,1,0:T(8,128)S(1)}, f32[2,136,128]{2,1,0:T(8,128)S(1)}, u32[]{:S(2)}, u32[]{:S(2)}) collective-permute-start(f32[2,136,128]{2,1,0:T(8,128)S(1)} %get-tuple-element.24), channel_id=1, source_target_pairs={{0,3},{1,2},{2,1},{3,0},{4,7},{5,6},{6,5},{7,4},{8,11},{9,10},{10,... | collective-permute-start | bytes 417800 | tf_op jit(solution)/shard_map/ppermute | solution.py:349
  20.4 13.5 %collective-permute-start.3 = (f32[2,136,128]{2,1,0:T(8,128)S(1)}, f32[2,136,128]{2,1,0:T(8,128)S(1)}, u32[]{:S(2)}, u32[]{:S(2)}) collective-permute-start(f32[2,136,128]{2,1,0:T(8,128)S(1)} %get-tuple-element.25), channel_id=1, source_target_pairs={{0,4},{1,5},{2,6},{3,7},{4,0},{5,1},{6,2},{7,3},{8,12},{9,13},{10,... | collective-permute-start | bytes 417800 | tf_op jit(solution)/shard_map/ppermute | solution.py:349
  20.7 13.3 %collective-permute-start.4 = (f32[2,136,128]{2,1,0:T(8,128)S(1)}, f32[2,136,128]{2,1,0:T(8,128)S(1)}, u32[]{:S(2)}, u32[]{:S(2)}) collective-permute-start(f32[2,136,128]{2,1,0:T(8,128)S(1)} %get-tuple-element.26), channel_id=1, source_target_pairs={{0,5},{1,4},{2,7},{3,6},{4,1},{5,0},{6,3},{7,2},{8,13},{9,12},{10,... | collective-permute-start | bytes 417800 | tf_op jit(solution)/shard_map/ppermute | solution.py:349
  22.1 15.9 %collective-permute-start.5 = (f32[2,136,128]{2,1,0:T(8,128)S(1)}, f32[2,136,128]{2,1,0:T(8,128)S(1)}, u32[]{:S(2)}, u32[]{:S(2)}) collective-permute-start(f32[2,136,128]{2,1,0:T(8,128)S(1)} %get-tuple-element.27), channel_id=1, source_target_pairs={{0,6},{1,7},{2,4},{3,5},{4,2},{5,3},{6,0},{7,1},{8,14},{9,15},{10,... | collective-permute-start | bytes 417800 | tf_op jit(solution)/shard_map/ppermute | solution.py:349
  32.1 7.8 %collective-permute-start.6 = (f32[2,136,128]{2,1,0:T(8,128)S(1)}, f32[2,136,128]{2,1,0:T(8,128)S(1)}, u32[]{:S(2)}, u32[]{:S(2)}) collective-permute-start(f32[2,136,128]{2,1,0:T(8,128)S(1)} %get-tuple-element.28), channel_id=1, source_target_pairs={{0,7},{1,6},{2,5},{3,4},{4,3},{5,2},{6,1},{7,0},{8,15},{9,14},{10,... | collective-permute-start | bytes 417800 | tf_op jit(solution)/shard_map/ppermute | solution.py:349
  41.3 7.7 %copy-start = (bf16[2,2,256,256]{3,2,1,0:T(8,128)(2,1)S(1)}, bf16[2,2,256,256]{3,2,1,0:T(8,128)(2,1)}, u32[]{:S(2)}) copy-start(bf16[2,2,256,256]{3,2,1,0:T(8,128)(2,1)} %constant.26.clone.col_fwd) | copy-start | bytes 1572868
  41.4 12.3 %copy-start.9 = (bf16[2,256,384]{2,1,0:T(8,128)(2,1)S(1)}, bf16[2,256,384]{2,1,0:T(8,128)(2,1)}, u32[]{:S(2)}) copy-start(bf16[2,256,384]{2,1,0:T(8,128)(2,1)} %constant.28.clone.row_inv) | copy-start | bytes 1179652
  42.4 11.3 %collective-permute-start.7 = (f32[8,64,128]{2,1,0:T(8,128)S(1)}, f32[8,64,128]{2,1,0:T(8,128)S(1)}, u32[]{:S(2)}, u32[]{:S(2)}) collective-permute-start(f32[8,64,128]{2,1,0:T(8,128)S(1)} %get-tuple-element.34), channel_id=1, source_target_pairs={{0,1},{1,2},{2,3},{3,4},{4,5},{5,6},{6,7},{8,9},{9,10},{10,11},{11... | collective-permute-start | bytes 786440 | tf_op jit(solution)/shard_map/ppermute | solution.py:401
  44.7 9.0 %copy-start.1 = (bf16[2,384,384]{2,1,0:T(8,128)(2,1)S(1)}, bf16[2,384,384]{2,1,0:T(8,128)(2,1)}, u32[]{:S(2)}) copy-start(bf16[2,384,384]{2,1,0:T(8,128)(2,1)} %constant.24.clone.row_fwd) | copy-start | bytes 1769476
  44.7 9.0 %copy-start.8 = (bf16[2,2,256,256]{3,2,1,0:T(8,128)(2,1)S(1)}, bf16[2,2,256,256]{3,2,1,0:T(8,128)(2,1)}, u32[]{:S(2)}) copy-start(bf16[2,2,256,256]{3,2,1,0:T(8,128)(2,1)} %constant.27.clone.col_inv) | copy-start | bytes 1572868
  44.7 8.9 %collective-permute-start.8 = (f32[8,64,128]{2,1,0:T(8,128)S(1)}, f32[8,64,128]{2,1,0:T(8,128)S(1)}, u32[]{:S(2)}, u32[]{:S(2)}) collective-permute-start(f32[8,64,128]{2,1,0:T(8,128)S(1)} %get-tuple-element.36), channel_id=1, source_target_pairs={{1,0},{2,1},{3,2},{4,3},{5,4},{6,5},{7,6},{9,8},{10,9},{11,10},{12... | collective-permute-start | bytes 786440 | tf_op jit(solution)/shard_map/ppermute | solution.py:402
  50.1 13.9 %collective-permute-start.17 = (f32[2,256,128]{2,1,0:T(8,128)S(1)}, f32[2,256,128]{2,1,0:T(8,128)S(1)}, u32[]{:S(2)}, u32[]{:S(2)}) collective-permute-start(f32[2,256,128]{2,1,0:T(8,128)S(1)} %get-tuple-element.30.rest_0_), channel_id=1, source_target_pairs={{0,8},{24,16},{1,9},{25,17},{2,10},{26,18},{3,11},{27,19},{4,12},{... | collective-permute-start | bytes 786440 | tf_op jit(solution)/shard_map/ppermute | solution.py:290
  56.7 15.8 %collective-permute-start.12 = (f32[2,256,128]{2,1,0:T(8,128)S(1)}, f32[2,256,128]{2,1,0:T(8,128)S(1)}, u32[]{:S(2)}, u32[]{:S(2)}) collective-permute-start(f32[2,256,128]{2,1,0:T(8,128)S(1)} %shard_map.159), channel_id=1, source_target_pairs={{0,8},{24,16},{1,9},{25,17},{2,10},{26,18},{3,11},{27,19},{4,12},{... | collective-permute-start | bytes 786440 | tf_op jit(solution)/shard_map/ppermute | solution.py:290
  59.4 19.4 %collective-permute-start.14 = (f32[2,256,128]{2,1,0:T(8,128)S(1)}, f32[2,256,128]{2,1,0:T(8,128)S(1)}, u32[]{:S(2)}, u32[]{:S(2)}) collective-permute-start(f32[2,256,128]{2,1,0:T(8,128)S(1)} %get-tuple-element.31.rest_1_.rest_0_), channel_id=1, source_target_pairs={{0,16},{8,0},{16,24},{24,8},{1,17},{9,1},{17,25},{25,9},{2,18},{10... | collective-permute-start | bytes 786440 | tf_op jit(solution)/shard_map/ppermute | solution.py:290
  59.8 19.6 %collective-permute-start.15 = (f32[2,256,128]{2,1,0:T(8,128)S(1)}, f32[2,256,128]{2,1,0:T(8,128)S(1)}, u32[]{:S(2)}, u32[]{:S(2)}) collective-permute-start(f32[2,256,128]{2,1,0:T(8,128)S(1)} %get-tuple-element.32.rest_2_.rest_1_), channel_id=1, source_target_pairs={{0,8},{8,16},{1,9},{9,17},{2,10},{10,18},{3,11},{11,19},{4,12},{12... | collective-permute-start | bytes 786440 | tf_op jit(solution)/shard_map/ppermute | solution.py:290
  63.4 19.4 %collective-permute-start.16 = (f32[2,256,128]{2,1,0:T(8,128)S(1)}, f32[2,256,128]{2,1,0:T(8,128)S(1)}, u32[]{:S(2)}, u32[]{:S(2)}) collective-permute-start(f32[2,256,128]{2,1,0:T(8,128)S(1)} %get-tuple-element.32.rest_2_.rest_1_), channel_id=1, source_target_pairs={{16,8},{24,16},{17,9},{25,17},{18,10},{26,18},{19,11},{27,19},{20,... | collective-permute-start | bytes 786440 | tf_op jit(solution)/shard_map/ppermute | solution.py:290
  64.1 21.4 %collective-permute-start.18 = (f32[2,256,128]{2,1,0:T(8,128)S(1)}, f32[2,256,128]{2,1,0:T(8,128)S(1)}, u32[]{:S(2)}, u32[]{:S(2)}) collective-permute-start(f32[2,256,128]{2,1,0:T(8,128)S(1)} %add.13), channel_id=1, source_target_pairs={{8,24},{16,0},{9,25},{17,1},{10,26},{18,2},{11,27},{19,3},{12,28},... | collective-permute-start | bytes 786440 | tf_op jit(solution)/shard_map/ppermute | solution.py:290
  72.5 13.8 %collective-permute-start.10 = (f32[2,256,128]{2,1,0:T(8,128)S(1)}, f32[2,256,128]{2,1,0:T(8,128)S(1)}, u32[]{:S(2)}, u32[]{:S(2)}) collective-permute-start(f32[2,256,128]{2,1,0:T(8,128)S(1)} %get-tuple-element.39), channel_id=1, source_target_pairs={{0,8},{8,16},{1,9},{9,17},{2,10},{10,18},{3,11},{11,19},{4,12},{12... | collective-permute-start | bytes 786440 | tf_op jit(solution)/shard_map/ppermute | solution.py:290
  78.8 7.6 %collective-permute-start.11 = (f32[2,256,128]{2,1,0:T(8,128)S(1)}, f32[2,256,128]{2,1,0:T(8,128)S(1)}, u32[]{:S(2)}, u32[]{:S(2)}) collective-permute-start(f32[2,256,128]{2,1,0:T(8,128)S(1)} %get-tuple-element.39), channel_id=1, source_target_pairs={{16,8},{24,16},{17,9},{25,17},{18,10},{26,18},{19,11},{27,19},{20,... | collective-permute-start | bytes 786440 | tf_op jit(solution)/shard_map/ppermute | solution.py:290
  79.5 10.8 %collective-permute-start.9 = (f32[2,256,128]{2,1,0:T(8,128)S(1)}, f32[2,256,128]{2,1,0:T(8,128)S(1)}, u32[]{:S(2)}, u32[]{:S(2)}) collective-permute-start(f32[2,256,128]{2,1,0:T(8,128)S(1)} %get-tuple-element.38), channel_id=1, source_target_pairs={{0,16},{8,0},{16,24},{24,8},{1,17},{9,1},{17,25},{25,9},{2,18},{10... | collective-permute-start | bytes 786440 | tf_op jit(solution)/shard_map/ppermute | solution.py:290
  82.8 18.8 %collective-permute-start.13 = (f32[2,256,128]{2,1,0:T(8,128)S(1)}, f32[2,256,128]{2,1,0:T(8,128)S(1)}, u32[]{:S(2)}, u32[]{:S(2)}) collective-permute-start(f32[2,256,128]{2,1,0:T(8,128)S(1)} %add.12), channel_id=1, source_target_pairs={{8,24},{16,0},{9,25},{17,1},{10,26},{18,2},{11,27},{19,3},{12,28},... | collective-permute-start | bytes 786440 | tf_op jit(solution)/shard_map/ppermute | solution.py:290
  (14 other events, 42.2 us)

commit v3 on v2

--- a/solution.py
+++ b/solution.py
@@ -271,7 +271,7 @@
         out[:, cols] = functools.reduce(jnp.add, [p[c] for p in parts]) / jnp.maximum(weight[:, cols], 1.0)
 
 
-LINE = ((3, 2, 1, 0), (3, 0, 2, 1), (0, 3, 1, 2), (0, 1, 2, 3))
+LINE = ((3, 2, 1, 0), (2, 3, 0, 1), (1, 0, 3, 2), (0, 1, 2, 3))
 
 
 def send_order(count):
@@ -293,18 +293,19 @@
         for tile in tiles:
             k = len(self.tiles)
             self.tiles.append(tile)
-            if self.count == 4:
-                if k == 0:
-                    self.send(tile, [(0, 1), (3, 2)])
-                elif k == 1:
-                    self.send(tile, [(0, 2), (1, 0), (2, 3), (3, 1)])
-                elif k == 2:
-                    self.send(tile, [(0, 1), (1, 2)], [(2, 1), (3, 2)])
+            if self.count != 4:
+                continue
+            if k == 0:
+                self.send(tile, [(0, 1), (3, 2)])
+                self.send(tile, [(1, 2), (2, 1)])
+            elif k == 1:
+                self.send(tile + self.sent[0], [(0, 2), (1, 3), (2, 0), (3, 1)])
+            elif k == 2:
+                self.send(tile, [(0, 1), (1, 0), (2, 3), (3, 2)])
 
     def parts(self):
         if self.count != 4:
             return [lax.psum_scatter(jnp.stack(self.tiles), "visit", scatter_dimension=0, tiled=False)]
-        self.send(self.tiles[0] + self.sent[0], [(1, 3), (2, 0)])
         return [self.tiles[3], *self.sent[1:]]
 
 

time: 104 us -> 98.9 us (0.951)
  starting transfers between devices: 39.7 us -> 30.8 us
  waiting for transfers between devices: 33 us -> 37 us
    ppermute x10 -> x8, starting transfers between devices: 23.6 us -> 14.7 us  [send(): self.sent += [lax.ppermute(tile, 'visit', route) for route in routes]]
    ppermute x10 -> x8, waiting for transfers between devices: 16.7 us -> 20.7 us  [send(): self.sent += [lax.ppermute(tile, 'visit', route) for route in routes]]
  transfers between devices with their start and end apart: 20 -> 18, of which waited for: 7 -> 7; matrix products, arithmetic and copies ran while one was open for 0% -> 0% of each run, Pallas kernels for 17% -> 18%
where the time goes in v3:
time: 98.9 us; the launch traced here: 98.3 us
  waiting for transfers between devices  37 us (37%)
  starting transfers between devices  30.8 us (31%)
  Pallas kernels  22.3 us (23%)
  local copies, waits for them, and re-layouts  7.21 us (7%)
    ppermute x8, waiting for transfers between devices, send(): self.sent += [lax.ppermute(tile, 'visit', route) for route in routes]  20.7 us
    ppermute x7, waiting for transfers between devices, exchange(): lax.ppermute(sent[d], 'bulk', [(i, i ^ d) for i in range(owners)])  16.3 us
    ppermute x8, starting transfers between devices, send(): self.sent += [lax.ppermute(tile, 'visit', route) for route in routes]  14.7 us
    pallas_call x2, Pallas kernels, convolve(): pl.pallas_call(functools.partial(conv_body, first), out_shape=[tile] * co...  10.1 us
    unnamed x36, local copies, waits for them, and re-layouts  6.48 us
    ppermute x7, starting transfers between devices, exchange(): lax.ppermute(sent[d], 'bulk', [(i, i ^ d) for i in range(owners)])  5.14 us
    all_to_all x1, starting transfers between devices, coadd_patches(): lax.all_to_all(sent_flux, 'bulk', split_axis=0, concat_axis=0, tiled=True)  4.36 us
    ppermute x1, starting transfers between devices, coadd_patches(): below = lax.ppermute(top, 'bulk', [(i + 1, i) for i in range(ends)])  4.29 us
  transfers between devices with their start and end apart: 18, of which 7 were waited for; matrix products, arithmetic and copies ran while one was open for 0% of the time, Pallas kernels for 18%

profile of v3, /device:TPU:4, one launch (start us, length us, event | category | flops | bytes accessed | tf_op | source)
XLA Modules:
  0.0 98.3 jit_solution(8590021272773609348)
XLA Ops:
  4.8 1.0 %copy-done.6 = f32[1,1,8,128,128]{4,3,2,1,0:T(8,128)S(1)} copy-done((f32[1,1,8,128,128]{4,3,2,1,0:T(8,128)S(1)}, f32[1,1,8,128,128]{4,3,2,1,0:T(8,128)}, u32[]{:S(2)}) %copy-start.6) | copy-done | bytes 524312
  6.9 3.3 %warp_flux.1 = f32[16,128,128]{2,1,0:T(8,128)} custom-call(s32[6,8]{1,0:T(8,128)S(1)} %stack.23.info, f32[1,1,8,128,128]{4,3,2,1,0:T(8,128)S(1)} %copy-done.11, f32[1,1,8,128,128]{4,3,2,1,0:T(8,128)S(1)} %copy-done.2, f32[1,1,8,128,128]{4,3,2,1,0:T(8,128)S(1)} %copy-done.4, f32[1,1,8,128,128]{4,3,2,1,0:T(8,128)S(1)} %copy-done.6), custom_call_target="tpu_custom_call" | custom-call | tf_op jit(solution)/shard_map/warp_flux/pallas_call | solution.py:363
  10.2 4.4 %all-to-all-start = ((f32[16,128,128]{2,1,0:T(8,128)}), f32[16,128,128]{2,1,0:T(8,128)S(1)}, u32[]{:S(2)}, u32[]{:S(2)}) async-start(f32[16,128,128]{2,1,0:T(8,128)} %warp_flux.1), calls=%async_computation | async-start | bytes 2097152 | tf_op jit(solution)/shard_map/all_to_all | solution.py:371
  14.6 3.9 %warp_weight.1 = (f32[2,136,128]{2,1,0:T(8,128)S(1)}, f32[2,136,128]{2,1,0:T(8,128)S(1)}, f32[2,136,128]{2,1,0:T(8,128)S(1)}, f32[2,136,128]{2,1,0:T(8,128)S(1)}...) custom-call(s32[6,8]{1,0:T(8,128)S(1)} %stack.23.info, ...), custom_call_target="tpu_custom_call" | custom-call | tf_op jit(solution)/shard_map/warp_weight/pallas_call | solution.py:353
  18.6 1.5 %collective-permute-start.1 = (f32[2,136,128]{2,1,0:T(8,128)S(1)}, f32[2,136,128]{2,1,0:T(8,128)S(1)}, u32[]{:S(2)}, u32[]{:S(2)}) collective-permute-start(f32[2,136,128]{2,1,0:T(8,128)S(1)} %get-tuple-element.23), channel_id=1, source_target_pairs={{0,2},{1,3},{2,0},{3,1},{4,6},{5,7},{6,4},{7,5},{8,10},{9,11},{10,... | collective-permute-start | bytes 417800 | tf_op jit(solution)/shard_map/ppermute | solution.py:350
  20.7 1.5 %collective-permute-start.4 = (f32[2,136,128]{2,1,0:T(8,128)S(1)}, f32[2,136,128]{2,1,0:T(8,128)S(1)}, u32[]{:S(2)}, u32[]{:S(2)}) collective-permute-start(f32[2,136,128]{2,1,0:T(8,128)S(1)} %get-tuple-element.26), channel_id=1, source_target_pairs={{0,5},{1,4},{2,7},{3,6},{4,1},{5,0},{6,3},{7,2},{8,13},{9,12},{10,... | collective-permute-start | bytes 417800 | tf_op jit(solution)/shard_map/ppermute | solution.py:350
  22.1 1.5 %collective-permute-start.5 = (f32[2,136,128]{2,1,0:T(8,128)S(1)}, f32[2,136,128]{2,1,0:T(8,128)S(1)}, u32[]{:S(2)}, u32[]{:S(2)}) collective-permute-start(f32[2,136,128]{2,1,0:T(8,128)S(1)} %get-tuple-element.27), channel_id=1, source_target_pairs={{0,6},{1,7},{2,4},{3,5},{4,2},{5,3},{6,0},{7,1},{8,14},{9,15},{10,... | collective-permute-start | bytes 417800 | tf_op jit(solution)/shard_map/ppermute | solution.py:350
  23.6 8.5 %collective-permute-done.1.rest_2_ = f32[2,136,128]{2,1,0:T(8,128)S(1)} collective-permute-done((f32[2,136,128]{2,1,0:T(8,128)S(1)}, f32[2,136,128]{2,1,0:T(8,128)S(1)}, u32[]{:S(2)}, u32[]{:S(2)}) %collective-permute-start.1) | collective-permute-done | bytes 139296 | tf_op jit(solution)/shard_map/ppermute | solution.py:350
  32.1 1.8 %collective-permute-done.2.rest_3_ = f32[2,136,128]{2,1,0:T(8,128)S(1)} collective-permute-done((f32[2,136,128]{2,1,0:T(8,128)S(1)}, f32[2,136,128]{2,1,0:T(8,128)S(1)}, u32[]{:S(2)}, u32[]{:S(2)}) %collective-permute-start.2) | collective-permute-done | bytes 139296 | tf_op jit(solution)/shard_map/ppermute | solution.py:350
  33.9 4.1 %collective-permute-done.5.rest_6_ = f32[2,136,128]{2,1,0:T(8,128)S(1)} collective-permute-done((f32[2,136,128]{2,1,0:T(8,128)S(1)}, f32[2,136,128]{2,1,0:T(8,128)S(1)}, u32[]{:S(2)}, u32[]{:S(2)}) %collective-permute-start.5) | collective-permute-done | bytes 139296 | tf_op jit(solution)/shard_map/ppermute | solution.py:350
  38.0 1.8 %collective-permute-done.6.rest_7_ = f32[2,136,128]{2,1,0:T(8,128)S(1)} collective-permute-done((f32[2,136,128]{2,1,0:T(8,128)S(1)}, f32[2,136,128]{2,1,0:T(8,128)S(1)}, u32[]{:S(2)}, u32[]{:S(2)}) %collective-permute-start.6) | collective-permute-done | bytes 139296 | tf_op jit(solution)/shard_map/ppermute | solution.py:350
  39.9 1.4 %weights.1 = (f32[2,256,128]{2,1,0:T(8,128)S(1)}, f32[2,256,128]{2,1,0:T(8,128)S(1)}, f32[2,256,128]{2,1,0:T(8,128)S(1)}, f32[2,256,128]{2,1,0:T(8,128)S(1)}, s32[16]{0:T(128)S(1)}) custom-call(s32[6,8]{1,0:T(8,128)S(1)} %stack.23.info, f32[2,136,128]{2,1,0:T(8,128)S(1)} %get-tuple-element.21.rest_0_, f32[2,136,128]{2,1,0:T(8,128)S(1)} %collective-permute-done.rest_1_, ...), custom_call_target="tpu_custom_call" | custom-call | tf_op jit(solution)/shard_map/weights/pallas_call | solution.py:381
  42.4 2.3 %collective-permute-start.7 = (f32[8,64,128]{2,1,0:T(8,128)S(1)}, f32[8,64,128]{2,1,0:T(8,128)S(1)}, u32[]{:S(2)}, u32[]{:S(2)}) collective-permute-start(f32[8,64,128]{2,1,0:T(8,128)S(1)} %get-tuple-element.34), channel_id=1, source_target_pairs={{0,1},{1,2},{2,3},{3,4},{4,5},{5,6},{6,7},{8,9},{9,10},{10,11},{11... | collective-permute-start | bytes 786440 | tf_op jit(solution)/shard_map/ppermute | solution.py:402
  44.7 4.3 %collective-permute-start.8 = (f32[8,64,128]{2,1,0:T(8,128)S(1)}, f32[8,64,128]{2,1,0:T(8,128)S(1)}, u32[]{:S(2)}, u32[]{:S(2)}) collective-permute-start(f32[8,64,128]{2,1,0:T(8,128)S(1)} %get-tuple-element.36), channel_id=1, source_target_pairs={{1,0},{2,1},{3,2},{4,3},{5,4},{6,5},{7,6},{9,8},{10,9},{11,10},{12... | collective-permute-start | bytes 786440 | tf_op jit(solution)/shard_map/ppermute | solution.py:403
  49.0 1.1 %spectrum.1.spec = f32[2,192,256]{2,1,0:T(8,128)S(1)} custom-call(f32[1,4]{1,0:T(1,128)S(1)} %copy-done.14, f32[4,128,128]{2,1,0:T(8,128)S(1)} %copy-done.12, bf16[2,384,128]{2,1,0:T(8,128)(2,1)S(1)} %copy-done.13, bf16[2,2,256,256]{3,2,1,0:T(8,128)(2,1)S(1)} %copy-done), custom_call_target="tpu_custom_call" | custom-call | tf_op jit(solution)/shard_map/spectrum/pallas_call | solution.py:372
  50.1 3.5 %collective-permute-start.14 = (f32[2,256,128]{2,1,0:T(8,128)S(1)}, f32[2,256,128]{2,1,0:T(8,128)S(1)}, u32[]{:S(2)}, u32[]{:S(2)}) collective-permute-start(f32[2,256,128]{2,1,0:T(8,128)S(1)} %get-tuple-element.30.rest_0_), channel_id=1, source_target_pairs={{0,8},{24,16},{1,9},{25,17},{2,10},{26,18},{3,11},{27,19},{4,12},{... | collective-permute-start | bytes 786440 | tf_op jit(solution)/shard_map/ppermute | solution.py:290
  53.7 3.0 %shard_map.159 = f32[2,256,128]{2,1,0:T(8,128)S(1)} custom-call(s32[6,8]{1,0:T(8,128)S(1)} %stack.23.info, f32[8,64,128]{2,1,0:T(8,128)S(1)} %collective-permute-done.7.above, f32[8,256,128]{2,1,0:T(8,128)S(1)} %get-tuple-element.35.image, f32[8,64,128]{2,1,0:T(8,128)S(1)} %collective-permute-done.8.below, f32[2,192,256]{2,1,0:T(8,128)S(1)} %spectrum.1.spec, ...), custom_call_target="tpu_custom_call" | custom-call | tf_op jit(solution)/shard_map/pallas_call | solution.py:409
  56.7 2.7 %collective-permute-start.10 = (f32[2,256,128]{2,1,0:T(8,128)S(1)}, f32[2,256,128]{2,1,0:T(8,128)S(1)}, u32[]{:S(2)}, u32[]{:S(2)}) collective-permute-start(f32[2,256,128]{2,1,0:T(8,128)S(1)} %shard_map.159), channel_id=1, source_target_pairs={{0,8},{24,16},{1,9},{25,17},{2,10},{26,18},{3,11},{27,19},{4,12},{... | collective-permute-start | bytes 786440 | tf_op jit(solution)/shard_map/ppermute | solution.py:290
  60.1 2.2 %collective-permute-start.16 = (f32[2,256,128]{2,1,0:T(8,128)S(1)}, f32[2,256,128]{2,1,0:T(8,128)S(1)}, u32[]{:S(2)}, u32[]{:S(2)}) collective-permute-start(f32[2,256,128]{2,1,0:T(8,128)S(1)} %get-tuple-element.32.rest_2_.rest_1_), channel_id=1, source_target_pairs={{0,8},{8,0},{16,24},{24,16},{1,9},{9,1},{17,25},{25,17},{2,10},{10... | collective-permute-start | bytes 786440 | tf_op jit(solution)/shard_map/ppermute | solution.py:290
  64.0 7.1 %shard_map.158 = (f32[2,256,128]{2,1,0:T(8,128)S(1)}, f32[2,256,128]{2,1,0:T(8,128)S(1)}, f32[2,256,128]{2,1,0:T(8,128)S(1)}) custom-call(s32[6,8]{1,0:T(8,128)S(1)} %stack.23.info, f32[8,64,128]{2,1,0:T(8,128)S(1)} %collective-permute-done.7.above, f32[8,256,128]{2,1,0:T(8,128)S(1)} %get-tuple-element.35.image, ...), custom_call_target="tpu_custom_call" | custom-call | tf_op jit(solution)/shard_map/pallas_call | solution.py:409
  71.1 3.9 %collective-permute-start.12 = (f32[2,256,128]{2,1,0:T(8,128)S(1)}, f32[2,256,128]{2,1,0:T(8,128)S(1)}, u32[]{:S(2)}, u32[]{:S(2)}) collective-permute-start(f32[2,256,128]{2,1,0:T(8,128)S(1)} %get-tuple-element.39), channel_id=1, source_target_pairs={{0,8},{8,0},{16,24},{24,16},{1,9},{9,1},{17,25},{25,17},{2,10},{10... | collective-permute-start | bytes 786440 | tf_op jit(solution)/shard_map/ppermute | solution.py:290
  75.1 5.4 %collective-permute-done.15.refs_2_ = f32[2,256,128]{2,1,0:T(8,128)S(1)} collective-permute-done((f32[2,256,128]{2,1,0:T(8,128)S(1)}, f32[2,256,128]{2,1,0:T(8,128)S(1)}, u32[]{:S(2)}, u32[]{:S(2)}) %collective-permute-start.15) | collective-permute-done | bytes 262176 | tf_op jit(solution)/shard_map/ppermute | solution.py:290
  81.3 1.6 %collective-permute-done.12.refs_3_ = f32[2,256,128]{2,1,0:T(8,128)S(1)} collective-permute-done((f32[2,256,128]{2,1,0:T(8,128)S(1)}, f32[2,256,128]{2,1,0:T(8,128)S(1)}, u32[]{:S(2)}, u32[]{:S(2)}) %collective-permute-start.12) | collective-permute-done | bytes 262176 | tf_op jit(solution)/shard_map/ppermute | solution.py:290
  83.0 13.6 %collective-permute-done.11.refs_2_ = f32[2,256,128]{2,1,0:T(8,128)S(1)} collective-permute-done((f32[2,256,128]{2,1,0:T(8,128)S(1)}, f32[2,256,128]{2,1,0:T(8,128)S(1)}, u32[]{:S(2)}, u32[]{:S(2)}) %collective-permute-start.11) | collective-permute-done | bytes 262176 | tf_op jit(solution)/shard_map/ppermute | solution.py:290
  (64 shorter events, 11.9 us)
Async XLA Ops:
  10.2 31.1 %all-to-all-start = ((f32[16,128,128]{2,1,0:T(8,128)}), f32[16,128,128]{2,1,0:T(8,128)S(1)}, u32[]{:S(2)}, u32[]{:S(2)}) async-start(f32[16,128,128]{2,1,0:T(8,128)} %warp_flux.1), calls=%async_computation | async-start | bytes 2097152 | tf_op jit(solution)/shard_map/all_to_all | solution.py:371
  18.4 3.7 %collective-permute-start = (f32[2,136,128]{2,1,0:T(8,128)S(1)}, f32[2,136,128]{2,1,0:T(8,128)S(1)}, u32[]{:S(2)}, u32[]{:S(2)}) collective-permute-start(f32[2,136,128]{2,1,0:T(8,128)S(1)} %get-tuple-element.22), channel_id=1, source_target_pairs={{0,1},{1,0},{2,3},{3,2},{4,5},{5,4},{6,7},{7,6},{8,9},{9,8},{10,11... | collective-permute-start | bytes 417800 | tf_op jit(solution)/shard_map/ppermute | solution.py:350
  18.6 13.5 %collective-permute-start.1 = (f32[2,136,128]{2,1,0:T(8,128)S(1)}, f32[2,136,128]{2,1,0:T(8,128)S(1)}, u32[]{:S(2)}, u32[]{:S(2)}) collective-permute-start(f32[2,136,128]{2,1,0:T(8,128)S(1)} %get-tuple-element.23), channel_id=1, source_target_pairs={{0,2},{1,3},{2,0},{3,1},{4,6},{5,7},{6,4},{7,5},{8,10},{9,11},{10,... | collective-permute-start | bytes 417800 | tf_op jit(solution)/shard_map/ppermute | solution.py:350
  20.1 13.8 %collective-permute-start.2 = (f32[2,136,128]{2,1,0:T(8,128)S(1)}, f32[2,136,128]{2,1,0:T(8,128)S(1)}, u32[]{:S(2)}, u32[]{:S(2)}) collective-permute-start(f32[2,136,128]{2,1,0:T(8,128)S(1)} %get-tuple-element.24), channel_id=1, source_target_pairs={{0,3},{1,2},{2,1},{3,0},{4,7},{5,6},{6,5},{7,4},{8,11},{9,10},{10,... | collective-permute-start | bytes 417800 | tf_op jit(solution)/shard_map/ppermute | solution.py:350
  20.4 13.5 %collective-permute-start.3 = (f32[2,136,128]{2,1,0:T(8,128)S(1)}, f32[2,136,128]{2,1,0:T(8,128)S(1)}, u32[]{:S(2)}, u32[]{:S(2)}) collective-permute-start(f32[2,136,128]{2,1,0:T(8,128)S(1)} %get-tuple-element.25), channel_id=1, source_target_pairs={{0,4},{1,5},{2,6},{3,7},{4,0},{5,1},{6,2},{7,3},{8,12},{9,13},{10,... | collective-permute-start | bytes 417800 | tf_op jit(solution)/shard_map/ppermute | solution.py:350
  20.7 13.3 %collective-permute-start.4 = (f32[2,136,128]{2,1,0:T(8,128)S(1)}, f32[2,136,128]{2,1,0:T(8,128)S(1)}, u32[]{:S(2)}, u32[]{:S(2)}) collective-permute-start(f32[2,136,128]{2,1,0:T(8,128)S(1)} %get-tuple-element.26), channel_id=1, source_target_pairs={{0,5},{1,4},{2,7},{3,6},{4,1},{5,0},{6,3},{7,2},{8,13},{9,12},{10,... | collective-permute-start | bytes 417800 | tf_op jit(solution)/shard_map/ppermute | solution.py:350
  22.1 15.9 %collective-permute-start.5 = (f32[2,136,128]{2,1,0:T(8,128)S(1)}, f32[2,136,128]{2,1,0:T(8,128)S(1)}, u32[]{:S(2)}, u32[]{:S(2)}) collective-permute-start(f32[2,136,128]{2,1,0:T(8,128)S(1)} %get-tuple-element.27), channel_id=1, source_target_pairs={{0,6},{1,7},{2,4},{3,5},{4,2},{5,3},{6,0},{7,1},{8,14},{9,15},{10,... | collective-permute-start | bytes 417800 | tf_op jit(solution)/shard_map/ppermute | solution.py:350
  32.1 7.8 %collective-permute-start.6 = (f32[2,136,128]{2,1,0:T(8,128)S(1)}, f32[2,136,128]{2,1,0:T(8,128)S(1)}, u32[]{:S(2)}, u32[]{:S(2)}) collective-permute-start(f32[2,136,128]{2,1,0:T(8,128)S(1)} %get-tuple-element.28), channel_id=1, source_target_pairs={{0,7},{1,6},{2,5},{3,4},{4,3},{5,2},{6,1},{7,0},{8,15},{9,14},{10,... | collective-permute-start | bytes 417800 | tf_op jit(solution)/shard_map/ppermute | solution.py:350
  41.3 7.7 %copy-start = (bf16[2,2,256,256]{3,2,1,0:T(8,128)(2,1)S(1)}, bf16[2,2,256,256]{3,2,1,0:T(8,128)(2,1)}, u32[]{:S(2)}) copy-start(bf16[2,2,256,256]{3,2,1,0:T(8,128)(2,1)} %constant.26.clone.col_fwd) | copy-start | bytes 1572868
  41.3 7.7 %copy-start.12 = (f32[4,128,128]{2,1,0:T(8,128)S(1)}, f32[4,128,128]{2,1,0:T(8,128)}, u32[]{:S(2)}) copy-start(f32[4,128,128]{2,1,0:T(8,128)} %basis.1) | copy-start | bytes 786436
  41.3 7.7 %copy-start.13 = (bf16[2,384,128]{2,1,0:T(8,128)(2,1)S(1)}, bf16[2,384,128]{2,1,0:T(8,128)(2,1)}, u32[]{:S(2)}) copy-start(bf16[2,384,128]{2,1,0:T(8,128)(2,1)} %constant.25.clone.row_ker) | copy-start | bytes 589828
  41.4 12.3 %copy-start.9 = (bf16[2,256,384]{2,1,0:T(8,128)(2,1)S(1)}, bf16[2,256,384]{2,1,0:T(8,128)(2,1)}, u32[]{:S(2)}) copy-start(bf16[2,256,384]{2,1,0:T(8,128)(2,1)} %constant.28.clone.row_inv) | copy-start | bytes 1179652
  42.4 11.3 %collective-permute-start.7 = (f32[8,64,128]{2,1,0:T(8,128)S(1)}, f32[8,64,128]{2,1,0:T(8,128)S(1)}, u32[]{:S(2)}, u32[]{:S(2)}) collective-permute-start(f32[8,64,128]{2,1,0:T(8,128)S(1)} %get-tuple-element.34), channel_id=1, source_target_pairs={{0,1},{1,2},{2,3},{3,4},{4,5},{5,6},{6,7},{8,9},{9,10},{10,11},{11... | collective-permute-start | bytes 786440 | tf_op jit(solution)/shard_map/ppermute | solution.py:402
  44.7 9.0 %copy-start.1 = (bf16[2,384,384]{2,1,0:T(8,128)(2,1)S(1)}, bf16[2,384,384]{2,1,0:T(8,128)(2,1)}, u32[]{:S(2)}) copy-start(bf16[2,384,384]{2,1,0:T(8,128)(2,1)} %constant.24.clone.row_fwd) | copy-start | bytes 1769476
  44.7 9.0 %copy-start.8 = (bf16[2,2,256,256]{3,2,1,0:T(8,128)(2,1)S(1)}, bf16[2,2,256,256]{3,2,1,0:T(8,128)(2,1)}, u32[]{:S(2)}) copy-start(bf16[2,2,256,256]{3,2,1,0:T(8,128)(2,1)} %constant.27.clone.col_inv) | copy-start | bytes 1572868
  44.7 8.9 %collective-permute-start.8 = (f32[8,64,128]{2,1,0:T(8,128)S(1)}, f32[8,64,128]{2,1,0:T(8,128)S(1)}, u32[]{:S(2)}, u32[]{:S(2)}) collective-permute-start(f32[8,64,128]{2,1,0:T(8,128)S(1)} %get-tuple-element.36), channel_id=1, source_target_pairs={{1,0},{2,1},{3,2},{4,3},{5,4},{6,5},{7,6},{9,8},{10,9},{11,10},{12... | collective-permute-start | bytes 786440 | tf_op jit(solution)/shard_map/ppermute | solution.py:403
  50.1 12.2 %collective-permute-start.14 = (f32[2,256,128]{2,1,0:T(8,128)S(1)}, f32[2,256,128]{2,1,0:T(8,128)S(1)}, u32[]{:S(2)}, u32[]{:S(2)}) collective-permute-start(f32[2,256,128]{2,1,0:T(8,128)S(1)} %get-tuple-element.30.rest_0_), channel_id=1, source_target_pairs={{0,8},{24,16},{1,9},{25,17},{2,10},{26,18},{3,11},{27,19},{4,12},{... | collective-permute-start | bytes 786440 | tf_op jit(solution)/shard_map/ppermute | solution.py:290
  56.7 14.4 %collective-permute-start.10 = (f32[2,256,128]{2,1,0:T(8,128)S(1)}, f32[2,256,128]{2,1,0:T(8,128)S(1)}, u32[]{:S(2)}, u32[]{:S(2)}) collective-permute-start(f32[2,256,128]{2,1,0:T(8,128)S(1)} %shard_map.159), channel_id=1, source_target_pairs={{0,8},{24,16},{1,9},{25,17},{2,10},{26,18},{3,11},{27,19},{4,12},{... | collective-permute-start | bytes 786440 | tf_op jit(solution)/shard_map/ppermute | solution.py:290
  59.4 15.6 %collective-permute-start.13 = (f32[2,256,128]{2,1,0:T(8,128)S(1)}, f32[2,256,128]{2,1,0:T(8,128)S(1)}, u32[]{:S(2)}, u32[]{:S(2)}) collective-permute-start(f32[2,256,128]{2,1,0:T(8,128)S(1)} %get-tuple-element.30.rest_0_), channel_id=1, source_target_pairs={{8,16},{16,8},{9,17},{17,9},{10,18},{18,10},{11,19},{19,11},{12,20... | collective-permute-start | bytes 786440 | tf_op jit(solution)/shard_map/ppermute | solution.py:290
  60.1 15.0 %collective-permute-start.16 = (f32[2,256,128]{2,1,0:T(8,128)S(1)}, f32[2,256,128]{2,1,0:T(8,128)S(1)}, u32[]{:S(2)}, u32[]{:S(2)}) collective-permute-start(f32[2,256,128]{2,1,0:T(8,128)S(1)} %get-tuple-element.32.rest_2_.rest_1_), channel_id=1, source_target_pairs={{0,8},{8,0},{16,24},{24,16},{1,9},{9,1},{17,25},{25,17},{2,10},{10... | collective-permute-start | bytes 786440 | tf_op jit(solution)/shard_map/ppermute | solution.py:290
  62.4 18.2 %collective-permute-start.15 = (f32[2,256,128]{2,1,0:T(8,128)S(1)}, f32[2,256,128]{2,1,0:T(8,128)S(1)}, u32[]{:S(2)}, u32[]{:S(2)}) collective-permute-start(f32[2,256,128]{2,1,0:T(8,128)S(1)} %add.13), channel_id=1, source_target_pairs={{0,16},{8,24},{16,0},{24,8},{1,17},{9,25},{17,1},{25,9},{2,18},{10... | collective-permute-start | bytes 786440 | tf_op jit(solution)/shard_map/ppermute | solution.py:290
  63.3 18.0 %collective-permute-start.9 = (f32[2,256,128]{2,1,0:T(8,128)S(1)}, f32[2,256,128]{2,1,0:T(8,128)S(1)}, u32[]{:S(2)}, u32[]{:S(2)}) collective-permute-start(f32[2,256,128]{2,1,0:T(8,128)S(1)} %shard_map.159), channel_id=1, source_target_pairs={{8,16},{16,8},{9,17},{17,9},{10,18},{18,10},{11,19},{19,11},{12,20... | collective-permute-start | bytes 786440 | tf_op jit(solution)/shard_map/ppermute | solution.py:290
  71.1 11.9 %collective-permute-start.12 = (f32[2,256,128]{2,1,0:T(8,128)S(1)}, f32[2,256,128]{2,1,0:T(8,128)S(1)}, u32[]{:S(2)}, u32[]{:S(2)}) collective-permute-start(f32[2,256,128]{2,1,0:T(8,128)S(1)} %get-tuple-element.39), channel_id=1, source_target_pairs={{0,8},{8,0},{16,24},{24,16},{1,9},{9,1},{17,25},{25,17},{2,10},{10... | collective-permute-start | bytes 786440 | tf_op jit(solution)/shard_map/ppermute | solution.py:290
  75.0 21.6 %collective-permute-start.11 = (f32[2,256,128]{2,1,0:T(8,128)S(1)}, f32[2,256,128]{2,1,0:T(8,128)S(1)}, u32[]{:S(2)}, u32[]{:S(2)}) collective-permute-start(f32[2,256,128]{2,1,0:T(8,128)S(1)} %add.12), channel_id=1, source_target_pairs={{0,16},{8,24},{16,0},{24,8},{1,17},{9,25},{17,1},{25,9},{2,18},{10... | collective-permute-start | bytes 786440 | tf_op jit(solution)/shard_map/ppermute | solution.py:290
  (12 other events, 26.9 us)

commit v4 on v3

v4 whole, which is shorter than its diff:
```python
import functools
import math

import jax
import jax.numpy as jnp
import numpy as np
from jax import lax
from jax.experimental import pallas as pl
from jax.experimental.pallas import tpu as pltpu
from jax.sharding import PartitionSpec as P


HALO = 64
BR = 2
BC = 8
CAP = 2
LANES = 128
VMEM_BYTES = 12 * 2**20
META = 8


F32 = jnp.float32
BF16 = jnp.bfloat16
VMEM = pl.BlockSpec(memory_space=pltpu.VMEM)
SMEM = pl.BlockSpec(memory_space=pltpu.SMEM)


def split(value):
    high = value.astype(BF16)
    low = (value - high.astype(F32)).astype(BF16)
    return high, low


def data(value, axis):
    high, low = split(value)
    return jnp.concatenate([high, low, high], axis)


def weights(value, axis):
    high, low = split(value)
    return jnp.concatenate([high, high, low], axis)


def table(value):
    value = np.asarray(value, np.float32)
    high = value.astype(jnp.bfloat16)
    return np.stack([high, (value - high.astype(np.float32)).astype(jnp.bfloat16)])


def fixed(ref, axis):
    return jnp.concatenate([ref[0], ref[0], ref[1]], axis)


def dot(a, b, dims=((1,), (0,))):
    return lax.dot_general(a, b, (dims, ((), ())), preferred_element_type=F32)


@functools.lru_cache
def make_tables(rows_dev, taps):
    length = rows_dev + taps - 1
    freqs = (length + 1) // 2
    k = np.arange(freqs)[:, None]

    def wave(first, second, period):
        return 2.0 * math.pi * ((first * second) % period) / period

    n = np.arange(rows_dev + 2 * HALO)[None, :] - 1
    theta = wave(k, n, length)
    used = n >= 0
    row_fwd = np.concatenate([np.cos(theta) * used, -np.sin(theta) * used], 0)
    theta = wave(k, np.arange(taps)[None, :], length)
    row_ker = np.concatenate([np.cos(theta), -np.sin(theta)], 0)
    period = 2 * taps
    n = np.arange(taps)[:, None]
    f = np.arange(taps)[None, :]
    col_fwd = []
    col_inv = []
    for odd in (0, 1):
        theta = wave(n, 2 * f + odd, period)
        c, s = np.cos(theta), np.sin(theta)
        col_fwd.append(np.block([[c, -s], [s, c]]))
        c, s = c.T, s.T
        sign = -1.0 if odd else 1.0
        col_inv.append(sign * np.block([[c, s], [-s, c]]))
    p = np.arange(rows_dev)[:, None] + taps - 1
    theta = wave(p, k.T, length)
    weight = np.where(k.T == 0, 1.0, 2.0) / (length * period)
    row_inv = np.concatenate([weight * np.cos(theta), -weight * np.sin(theta)], 1)
    return (
        table(row_fwd),
        table(row_ker),
        np.stack([table(t) for t in col_fwd]),
        np.stack([table(t) for t in col_inv]),
        table(row_inv),
    )


def partner(me, other):
    return jnp.bitwise_xor(me, other)


def places(ids, owner, slot):
    for q in range(slot.shape[2]):
        own = owner[0, 0, 0, q]
        rank = jnp.int32(0)
        for earlier in range(q):
            rank = rank + (owner[0, 0, 0, earlier] == own).astype(jnp.int32)
        yield q, partner(ids[0], own), own, rank, slot[0, 0, q]


def tile_at(ids, k, tiles):
    if tiles != 4:
        return jnp.int32(k)
    mine = jnp.int32(LINE[-1][k])
    for v in range(tiles - 1):
        mine = jnp.where(ids[1] == v, LINE[v][k], mine)
    return mine


def masked(extent, ivar, q):
    row_at = lax.broadcasted_iota(jnp.int32, ivar.shape, 0)
    col_at = lax.broadcasted_iota(jnp.int32, ivar.shape, 1)
    valid = (row_at < extent[0, 0, 0, q]) & (col_at < extent[0, 0, 1, q])
    return jnp.where(valid, ivar, 0.0)


def warp(plane, rows, cols):
    mid = dot(data(plane, 1), weights(cols, 1), ((1,), (1,)))
    return dot(weights(rows, 1), data(mid, 0))


def fetch(refs, buf, sems):
    copies = [
        [pltpu.make_async_copy(ref.at[0, 0, q], buf.at[i, q], sems.at[i, q]) for i, ref in enumerate(refs)]
        for q in range(buf.shape[1])
    ]
    for piece in copies:
        for copy in piece:
            copy.start()

    def get(q):
        for copy in copies[q]:
            copy.wait()
        return [buf[i, q] for i in range(len(refs))]

    return get


def run(copies):
    for copy in copies:
        copy.start()
    for copy in copies:
        copy.wait()


def warp_weight_body(ids, owner, slot, extent, ivar, rows, cols, *rest):
    side = ivar.shape[3]
    *outs, buf, buf_sems, send, sems = rest
    get = fetch((ivar, rows, cols), buf, buf_sems)
    for d in range(len(outs)):
        for rank in range(CAP):
            send[d, rank, side:, :] = jnp.full((META, side), -1.0, F32)
    for q, to, _, rank, at in places(ids, owner, slot):
        weight, row_map, col_map = get(q)
        send[to, rank, :side, :] = warp(masked(extent, weight, q), row_map, col_map)
        send[to, rank, side:, :] = jnp.full((META, side), at.astype(F32), F32)
    run([pltpu.make_async_copy(send.at[d], out, sems.at[d]) for d, out in enumerate(outs)])


def warp_flux_body(ids, owner, slot, extent, ivar, rows, cols, flux, out, buf, buf_sems):
    get = fetch((ivar, rows, cols, flux), buf, buf_sems)
    for q, _, own, rank, _ in places(ids, owner, slot):
        weight, row_map, col_map, value = get(q)
        out[own * CAP + rank] = warp(masked(extent, weight, q) * value, row_map, col_map)


def weight_body(ids, *rest):
    *rest, slot_out, acc, buf, sems = rest
    count = slot_out.shape[0] // CAP
    got, out = rest[:count], rest[count:]
    copies = [pltpu.make_async_copy(ref, buf.at[d], sems.at[d]) for d, ref in enumerate(got)]
    for copy in copies:
        copy.start()
    side = acc.shape[1]
    spare = acc.shape[0] - 1
    per_tile = out[0].shape[1] // side
    acc[...] = jnp.zeros(acc.shape, F32)
    for copy in copies:
        copy.wait()
    slots = []
    for d in range(count):
        for rank in range(CAP):
            at = jnp.max(buf[d, rank, side:, :]).astype(jnp.int32)
            slots.append(jnp.where(at < 0, spare, at))
    for n, at in enumerate(slots):
        d, rank = divmod(n, CAP)
        slot_out[partner(ids[0], d) * CAP + rank] = at
        acc[at] += buf[d, rank, :side, :]
    for k in range(len(out)):
        for c in range(per_tile):
            for r in range(BR):
                block = acc[r * BC + tile_at(ids, k, len(out)) * per_tile + c]
                out[k][r * side : (r + 1) * side, c * side : (c + 1) * side] = block


def image_body(ids, slot, got, *rest):
    *tiles, image, top, bottom, acc = rest
    side = acc.shape[1]
    per_tile = tiles[0].shape[1] // side
    acc[...] = jnp.zeros(acc.shape, F32)
    for n in range(slot.shape[0]):
        acc[slot[n]] += got[n]
    for k, tile in enumerate(tiles):
        for c in range(per_tile):
            to = tile_at(ids, k, len(tiles)) * per_tile + c
            for r in range(BR):
                rows = slice(r * side, (r + 1) * side)
                weight = tile[rows, c * side : (c + 1) * side]
                image[to, rows, :] = acc[r * BC + to] / jnp.maximum(weight, 1.0)
            top[to] = image[to, :HALO, :]
            bottom[to] = image[to, -HALO:, :]


def beside(stacked):
    n = stacked.shape[0] // 2
    return jnp.concatenate([stacked[:n], stacked[n:]], 1)


def spectrum_body(coeffs, basis, row_ker, col_fwd, out):
    kernel = coeffs[0, 0] * basis[0]
    for k in range(1, basis.shape[0]):
        kernel = kernel + coeffs[0, k] * basis[k]
    lines = data(beside(dot(fixed(row_ker, 1), data(kernel, 0))), 1)
    for odd in (0, 1):
        out[odd] = dot(lines, fixed(col_fwd.at[odd], 0))


def conv_body(first, tiles, ids, above, image, below, spec, row_fwd, col_fwd, col_inv, row_inv, *rest):
    *rest, lines = rest
    count = len(rest) // 2
    weight, out = rest[:count], rest[count:]
    taps = image.shape[2]
    per_tile = out[0].shape[1] // taps
    freqs = spec.shape[1]

    def column(c):
        return jnp.concatenate([above[c], image[c], below[c]], 0)

    lead = fixed(row_fwd, 1)
    last = fixed(row_inv, 1)
    for k in range(count):
        start = tile_at(ids, first + k, tiles) * per_tile
        parts = [column(start + c) for c in range(per_tile)]
        before = jnp.where(start > 0, column(jnp.maximum(start - 1, 0)), 0.0)
        after = jnp.where(start + per_tile < BC, column(jnp.minimum(start + per_tile, BC - 1)), 0.0)
        ext = jnp.concatenate([before[:, taps - HALO :], *parts, after[:, :HALO]], 1)
        lines[...] = dot(lead, data(ext, 0))
        one = [lines[:, c * taps : (c + 1) * taps] for c in range(per_tile + 1)]
        total = []
        for odd in (0, 1):
            mixed = [beside(a - b if odd else a + b) for a, b in zip(one, one[1:])]
            freq = dot(data(jnp.concatenate(mixed, 0), 1), fixed(col_fwd.at[odd], 0))
            kr = jnp.concatenate([spec[odd, :, :taps]] * per_tile, 0)
            ki = jnp.concatenate([spec[odd, :, taps:]] * per_tile, 0)
            zr, zi = freq[:, :taps], freq[:, taps:]
            prod = jnp.concatenate([zr * kr - zi * ki, zr * ki + zi * kr], 1)
            total.append(dot(data(prod, 1), fixed(col_inv.at[odd], 0)))
        wave = total[0] + total[1]
        parts = [wave[c * freqs : (c + 1) * freqs] for c in range(per_tile)]
        cols = [jnp.concatenate([p[:, :taps], p[:, taps:]], 0) for p in parts]
        out[k][...] = dot(last, data(jnp.concatenate(cols, 1), 0)) * weight[k][...]


LINE = ((3, 2, 1, 0), (2, 3, 0, 1), (1, 0, 3, 2), (0, 1, 2, 3))


class VisitSum:
    def __init__(self, count):
        self.count = count
        self.sent = []
        self.tiles = []

    def send(self, tile, *routes):
        self.sent += [lax.ppermute(tile, "visit", route) for route in routes]

    def push(self, *tiles):
        for tile in tiles:
            k = len(self.tiles)
            self.tiles.append(tile)
            if self.count != 4:
                continue
            if k == 0:
                self.send(tile, [(0, 1), (3, 2)])
                self.send(tile, [(1, 2), (2, 1)])
            elif k == 1:
                self.send(tile + self.sent[0], [(0, 2), (1, 3), (2, 0), (3, 1)])
            elif k == 2:
                self.send(tile, [(0, 1), (1, 0), (2, 3), (3, 2)])

    def parts(self):
        if self.count != 4:
            return [lax.psum_scatter(jnp.stack(self.tiles), "visit", scatter_dimension=0, tiled=False)]
        return [self.tiles[3], *self.sent[1:]]


def coadd_patches(piece_flux, piece_ivar, warp_rows, warp_cols, piece_owner, piece_slot, piece_extent, basis, coeffs):
    owners = lax.axis_size("bulk")
    visits = lax.axis_size("visit")
    pieces, side = piece_flux.shape[2:4]
    assert side == LANES and side == 2 * HALO and owners & (owners - 1) == 0
    rows_dev = BR * side
    per_tile = BC // visits
    cap = owners * CAP
    row_fwd, row_ker, col_fwd, col_inv, row_inv = [jnp.asarray(t) for t in make_tables(rows_dev, side)]
    freqs = row_fwd.shape[1] // 2
    ids = jnp.stack([lax.axis_index("bulk"), lax.axis_index("visit")]).astype(jnp.int32)
    facts = (ids, piece_owner.transpose(0, 1, 3, 2), piece_slot, piece_extent.transpose(0, 1, 3, 2))

    params = pltpu.CompilerParams(vmem_limit_bytes=VMEM_BYTES)

    def arr(*shape):
        return jax.ShapeDtypeStruct(shape, F32)

    hbm = pl.BlockSpec(memory_space=pltpu.HBM)

    def piece_buffers(count):
        return [pltpu.VMEM((count, pieces, side, side), F32), pltpu.SemaphoreType.DMA((count, pieces))]

    def exchange(sent):
        got = [sent[0]]
        for d in range(1, owners):
            got.append(lax.ppermute(sent[d], "bulk", [(i, i ^ d) for i in range(owners)]))
        return got

    sent_weight = pl.pallas_call(
        warp_weight_body,
        out_shape=[arr(CAP, side + META, side)] * owners,
        in_specs=[SMEM] * 4 + [hbm] * 3,
        out_specs=[hbm] * owners,
        scratch_shapes=piece_buffers(3)
        + [pltpu.VMEM((owners, CAP, side + META, side), F32), pltpu.SemaphoreType.DMA((owners,))],
        compiler_params=params,
        name="warp_weight",
    )(*facts, piece_ivar, warp_rows, warp_cols)
    got_weight = exchange(sent_weight)
    sent_flux = pl.pallas_call(
        warp_flux_body,
        out_shape=arr(cap, side, side),
        in_specs=[SMEM] * 4 + [hbm] * 4,
        out_specs=VMEM,
        scratch_shapes=piece_buffers(4),
        compiler_params=params,
        name="warp_flux",
    )(*facts, piece_ivar, warp_rows, warp_cols, piece_flux)
    got_flux = lax.all_to_all(sent_flux, "bulk", split_axis=0, concat_axis=0, tiled=True)
    spec = pl.pallas_call(
        spectrum_body,
        out_shape=arr(2, freqs, 2 * side),
        in_specs=[SMEM] + [VMEM] * 3,
        out_specs=VMEM,
        compiler_params=params,
        name="spectrum",
    )(coeffs, basis, row_ker, col_fwd)
    tile = arr(rows_dev, per_tile * side)
    *ivar, slots = pl.pallas_call(
        weight_body,
        out_shape=[tile] * visits + [jax.ShapeDtypeStruct((cap,), jnp.int32)],
        in_specs=[SMEM] + [hbm] * owners,
        out_specs=[VMEM] * visits + [SMEM],
        scratch_shapes=[
            pltpu.VMEM((BR * BC + 1, side, side), F32),
            pltpu.VMEM((owners, CAP, side + META, side), F32),
            pltpu.SemaphoreType.DMA((owners,)),
        ],
        compiler_params=params,
        name="weights",
    )(ids, *got_weight)
    weight_sum = VisitSum(visits)
    weight_sum.push(*ivar)
    image, top, bottom = pl.pallas_call(
        image_body,
        out_shape=[arr(BC, rows_dev, side)] + [arr(BC, HALO, side)] * 2,
        in_specs=[SMEM] * 2 + [VMEM] * (1 + visits),
        out_specs=[VMEM] * 3,
        scratch_shapes=[pltpu.VMEM((BR * BC + 1, side, side), F32)],
        compiler_params=params,
        name="image",
    )(ids, slots, got_flux, *ivar)
    ends = owners - 1
    above = lax.ppermute(bottom, "bulk", [(i, i + 1) for i in range(ends)])
    below = lax.ppermute(top, "bulk", [(i + 1, i) for i in range(ends)])
    weight_map = functools.reduce(jnp.add, weight_sum.parts())

    def convolve(first, count):
        return pl.pallas_call(
            functools.partial(conv_body, first, visits),
            out_shape=[tile] * count,
            in_specs=[SMEM] + [VMEM] * (8 + count),
            out_specs=[VMEM] * count,
            scratch_shapes=[pltpu.VMEM((2 * freqs, (per_tile + 1) * side), F32)],
            compiler_params=params,
        )(ids, above, image, below, spec, row_fwd, col_fwd, col_inv, row_inv, *ivar[first : first + count])

    image_sum = VisitSum(visits)
    image_sum.push(*convolve(0, 1))
    image_sum.push(*convolve(1, visits - 2))
    image_sum.push(*convolve(visits - 1, 1))
    numerator = functools.reduce(jnp.add, image_sum.parts())
    return (numerator / jnp.maximum(weight_map, 1.0), weight_map)


def solution(mesh):
    placed = (
        P("visit", "bulk", None, None, None),
        P("visit", "bulk", None, None, None),
        P("visit", "bulk", None, None, None),
        P("visit", "bulk", None, None, None),
        P("visit", "bulk", None, None),
        P("visit", "bulk", None),
        P("visit", "bulk", None, None),
        P(),
        P("visit", None),
    )
    return jax.shard_map(
        coadd_patches,
        mesh=mesh,
        in_specs=placed,
        out_specs=(P("bulk", "visit"), P("bulk", "visit")),
        check_vma=False,
    )
```

time: 98.9 us -> 105 us (1.062)
  the two profiles are of different devices: /device:TPU:4 before, /device:TPU:3 now
where the time goes in v4:
time: 105 us; the launch traced here: 104 us
  starting transfers between devices  34.4 us (33%)
  waiting for transfers between devices  32.6 us (31%)
  Pallas kernels  30.4 us (29%)
  local copies, waits for them, and re-layouts  4.93 us (5%)
  other arithmetic  1.07 us (1%)
    ppermute x8, waiting for transfers between devices, send(): self.sent += [lax.ppermute(tile, 'visit', route) for route in routes]  20.3 us
    ppermute x8, starting transfers between devices, send(): self.sent += [lax.ppermute(tile, 'visit', route) for route in routes]  16.2 us
    pallas_call x3, Pallas kernels, convolve(): pl.pallas_call(functools.partial(conv_body, first, visits), out_shape=[ti...  10.9 us
    ppermute x7, waiting for transfers between devices, exchange(): lax.ppermute(sent[d], 'bulk', [(i, i ^ d) for i in range(owners)])  9.96 us
    ppermute x7, starting transfers between devices, exchange(): lax.ppermute(sent[d], 'bulk', [(i, i ^ d) for i in range(owners)])  8.43 us
    pallas_call x1, Pallas kernels, coadd_patches(): pl.pallas_call(warp_flux_body, out_shape=arr(cap, side, side), in_specs=[...  7.41 us
    pallas_call x1, Pallas kernels, coadd_patches(): pl.pallas_call(warp_weight_body, out_shape=[arr(CAP, side + META, side)]...  7.18 us
    unnamed x34, local copies, waits for them, and re-layouts  4.93 us
  transfers between devices with their start and end apart: 18, of which 9 were waited for; matrix products, arithmetic and copies ran while one was open for 0% of the time, Pallas kernels for 21%

profile of v4, /device:TPU:3, one launch (start us, length us, event | category | flops | bytes accessed | tf_op | source)
XLA Modules:
  0.0 104.3 jit_solution(584940629347585657)
XLA Ops:
  5.6 7.4 %warp_flux.1 = f32[16,128,128]{2,1,0:T(8,128)} custom-call(s32[2]{0:T(128)S(1)} %pad_add_fusion.ids, s32[1,1,1,8]{3,2,1,0:T(1,128)S(1)} %bitcast.6, s32[1,1,8]{2,1,0:T(1,128)S(1)} %copy-done.15, s32[1,1,2,8]{3,2,1,0:T(2,128)S(1)} %bitcast.4, f32[1,1,8,128,128]{4,3,2,1,0:T(8,128)S(1)} %copy-done.4, f32[1,1,8,128,128]{4,3,2,1,0:T(8,128)S(1)} %copy-done.6, ...), custom_call_target="tpu_custom_call" | custom-call | tf_op jit(solution)/shard_map/warp_flux/pallas_call | solution.py:346
  13.0 4.7 %all-to-all-start = ((f32[16,128,128]{2,1,0:T(8,128)}), f32[16,128,128]{2,1,0:T(8,128)S(1)}, u32[]{:S(2)}, u32[]{:S(2)}) async-start(f32[16,128,128]{2,1,0:T(8,128)} %warp_flux.1), calls=%async_computation | async-start | bytes 2097152 | tf_op jit(solution)/shard_map/all_to_all | solution.py:355
  17.7 7.2 %warp_weight.1 = (f32[2,136,128]{2,1,0:T(8,128)S(1)}, f32[2,136,128]{2,1,0:T(8,128)S(1)}, f32[2,136,128]{2,1,0:T(8,128)S(1)}, f32[2,136,128]{2,1,0:T(8,128)S(1)}...) custom-call(s32[2]{0:T(128)S(1)} %pad_add_fusion.ids, ...), custom_call_target="tpu_custom_call" | custom-call | tf_op jit(solution)/shard_map/warp_weight/pallas_call | solution.py:335
  25.4 1.7 %collective-permute-start.2 = (f32[2,136,128]{2,1,0:T(8,128)S(1)}, f32[2,136,128]{2,1,0:T(8,128)S(1)}, u32[]{:S(2)}, u32[]{:S(2)}) collective-permute-start(f32[2,136,128]{2,1,0:T(8,128)S(1)} %get-tuple-element.23), channel_id=1, source_target_pairs={{0,3},{1,2},{2,1},{3,0},{4,7},{5,6},{6,5},{7,4},{8,11},{9,10},{10,... | collective-permute-start | bytes 417800 | tf_op jit(solution)/shard_map/ppermute | solution.py:332
  27.1 1.2 %collective-permute-start.3 = (f32[2,136,128]{2,1,0:T(8,128)S(1)}, f32[2,136,128]{2,1,0:T(8,128)S(1)}, u32[]{:S(2)}, u32[]{:S(2)}) collective-permute-start(f32[2,136,128]{2,1,0:T(8,128)S(1)} %get-tuple-element.24), channel_id=1, source_target_pairs={{0,4},{1,5},{2,6},{3,7},{4,0},{5,1},{6,2},{7,3},{8,12},{9,13},{10,... | collective-permute-start | bytes 417800 | tf_op jit(solution)/shard_map/ppermute | solution.py:332
  28.9 1.2 %collective-permute-start.5 = (f32[2,136,128]{2,1,0:T(8,128)S(1)}, f32[2,136,128]{2,1,0:T(8,128)S(1)}, u32[]{:S(2)}, u32[]{:S(2)}) collective-permute-start(f32[2,136,128]{2,1,0:T(8,128)S(1)} %get-tuple-element.26), channel_id=1, source_target_pairs={{0,6},{1,7},{2,4},{3,5},{4,2},{5,3},{6,0},{7,1},{8,14},{9,15},{10,... | collective-permute-start | bytes 417800 | tf_op jit(solution)/shard_map/ppermute | solution.py:332
  30.1 3.3 %collective-permute-done.1.rest_2_ = f32[2,136,128]{2,1,0:T(8,128)S(1)} collective-permute-done((f32[2,136,128]{2,1,0:T(8,128)S(1)}, f32[2,136,128]{2,1,0:T(8,128)S(1)}, u32[]{:S(2)}, u32[]{:S(2)}) %collective-permute-start.1) | collective-permute-done | bytes 139296 | tf_op jit(solution)/shard_map/ppermute | solution.py:332
  33.4 3.3 %collective-permute-start.6 = (f32[2,136,128]{2,1,0:T(8,128)S(1)}, f32[2,136,128]{2,1,0:T(8,128)S(1)}, u32[]{:S(2)}, u32[]{:S(2)}) collective-permute-start(f32[2,136,128]{2,1,0:T(8,128)S(1)} %get-tuple-element.27), channel_id=1, source_target_pairs={{0,7},{1,6},{2,5},{3,4},{4,3},{5,2},{6,1},{7,0},{8,15},{9,14},{10,... | collective-permute-start | bytes 417800 | tf_op jit(solution)/shard_map/ppermute | solution.py:332
  37.9 2.1 %collective-permute-done.5.rest_6_ = f32[2,136,128]{2,1,0:T(8,128)S(1)} collective-permute-done((f32[2,136,128]{2,1,0:T(8,128)S(1)}, f32[2,136,128]{2,1,0:T(8,128)S(1)}, u32[]{:S(2)}, u32[]{:S(2)}) %collective-permute-start.5) | collective-permute-done | bytes 139296 | tf_op jit(solution)/shard_map/ppermute | solution.py:332
  40.0 3.3 %collective-permute-done.6.rest_7_ = f32[2,136,128]{2,1,0:T(8,128)S(1)} collective-permute-done((f32[2,136,128]{2,1,0:T(8,128)S(1)}, f32[2,136,128]{2,1,0:T(8,128)S(1)}, u32[]{:S(2)}, u32[]{:S(2)}) %collective-permute-start.6) | collective-permute-done | bytes 139296 | tf_op jit(solution)/shard_map/ppermute | solution.py:332
  43.3 2.9 %weights.1 = (f32[256,256]{1,0:T(8,128)S(1)}, f32[256,256]{1,0:T(8,128)S(1)}, f32[256,256]{1,0:T(8,128)S(1)}, f32[256,256]{1,0:T(8,128)S(1)}, s32[16]{0:T(128)S(1)}) custom-call(s32[2]{0:T(128)S(1)} %pad_add_fusion.ids, f32[2,136,128]{2,1,0:T(8,128)S(1)} %get-tuple-element.20.rest_0_, f32[2,136,128]{2,1,0:T(8,128)S(1)} %collective-permute-done.rest_1_, ...), custom_call_target="tpu_custom_call" | custom-call | tf_op jit(solution)/shard_map/weights/pallas_call | solution.py:365
  47.2 3.0 %collective-permute-start.7 = (f32[8,64,128]{2,1,0:T(8,128)S(1)}, f32[8,64,128]{2,1,0:T(8,128)S(1)}, u32[]{:S(2)}, u32[]{:S(2)}) collective-permute-start(f32[8,64,128]{2,1,0:T(8,128)S(1)} %get-tuple-element.33), channel_id=1, source_target_pairs={{0,1},{1,2},{2,3},{3,4},{4,5},{5,6},{6,7},{8,9},{9,10},{10,11},{11... | collective-permute-start | bytes 786440 | tf_op jit(solution)/shard_map/ppermute | solution.py:390
  50.3 2.1 %collective-permute-start.8 = (f32[8,64,128]{2,1,0:T(8,128)S(1)}, f32[8,64,128]{2,1,0:T(8,128)S(1)}, u32[]{:S(2)}, u32[]{:S(2)}) collective-permute-start(f32[8,64,128]{2,1,0:T(8,128)S(1)} %get-tuple-element.35), channel_id=1, source_target_pairs={{1,0},{2,1},{3,2},{4,3},{5,4},{6,5},{7,6},{9,8},{10,9},{11,10},{12... | collective-permute-start | bytes 786440 | tf_op jit(solution)/shard_map/ppermute | solution.py:391
  53.5 3.2 %collective-permute-start.14 = (f32[256,256]{1,0:T(8,128)S(1)}, f32[256,256]{1,0:T(8,128)S(1)}, u32[]{:S(2)}, u32[]{:S(2)}) collective-permute-start(f32[256,256]{1,0:T(8,128)S(1)} %get-tuple-element.29.rest_0_), channel_id=1, source_target_pairs={{0,8},{24,16},{1,9},{25,17},{2,10},{26,18},{3,11},{27,19},{4,12},{... | collective-permute-start | bytes 786440 | tf_op jit(solution)/shard_map/ppermute | solution.py:284
  56.7 2.3 %collective-permute-done.8.below = f32[8,64,128]{2,1,0:T(8,128)S(1)} collective-permute-done((f32[8,64,128]{2,1,0:T(8,128)S(1)}, f32[8,64,128]{2,1,0:T(8,128)S(1)}, u32[]{:S(2)}, u32[]{:S(2)}) %collective-permute-start.8) | collective-permute-done | bytes 262176 | tf_op jit(solution)/shard_map/ppermute | solution.py:391
  59.0 2.9 %shard_map.150 = f32[256,256]{1,0:T(8,128)S(1)} custom-call(s32[2]{0:T(128)S(1)} %pad_add_fusion.ids, f32[8,64,128]{2,1,0:T(8,128)S(1)} %collective-permute-done.7.above, f32[8,256,128]{2,1,0:T(8,128)S(1)} %get-tuple-element.34.image, f32[8,64,128]{2,1,0:T(8,128)S(1)} %collective-permute-done.8.below, f32[2,192,256]{2,1,0:T(8,128)S(1)} %spectrum.1.spec, ...), custom_call_target="tpu_custom_call" | custom-call | tf_op jit(solution)/shard_map/pallas_call | solution.py:395
  62.0 3.2 %collective-permute-start.10 = (f32[256,256]{1,0:T(8,128)S(1)}, f32[256,256]{1,0:T(8,128)S(1)}, u32[]{:S(2)}, u32[]{:S(2)}) collective-permute-start(f32[256,256]{1,0:T(8,128)S(1)} %shard_map.150), channel_id=1, source_target_pairs={{0,8},{24,16},{1,9},{25,17},{2,10},{26,18},{3,11},{27,19},{4,12},{... | collective-permute-start | bytes 786440 | tf_op jit(solution)/shard_map/ppermute | solution.py:284
  66.0 3.9 %collective-permute-start.15 = (f32[256,256]{1,0:T(8,128)S(1)}, f32[256,256]{1,0:T(8,128)S(1)}, u32[]{:S(2)}, u32[]{:S(2)}) collective-permute-start(f32[256,256]{1,0:T(8,128)S(1)} %add.29), channel_id=1, source_target_pairs={{0,16},{8,24},{16,0},{24,8},{1,17},{9,25},{17,1},{25,9},{2,18},{10... | collective-permute-start | bytes 786440 | tf_op jit(solution)/shard_map/ppermute | solution.py:284
  70.8 5.0 %shard_map.151 = (f32[256,256]{1,0:T(8,128)S(1)}, f32[256,256]{1,0:T(8,128)S(1)}) custom-call(s32[2]{0:T(128)S(1)} %pad_add_fusion.ids, f32[8,64,128]{2,1,0:T(8,128)S(1)} %collective-permute-done.7.above, f32[8,256,128]{2,1,0:T(8,128)S(1)} %get-tuple-element.34.image, f32[8,64,128]{2,1,0:T(8,128)S(1)} %collective-permute-done.8.below, ...), custom_call_target="tpu_custom_call" | custom-call | tf_op jit(solution)/shard_map/pallas_call | solution.py:395
  75.8 1.6 %collective-permute-start.12 = (f32[256,256]{1,0:T(8,128)S(1)}, f32[256,256]{1,0:T(8,128)S(1)}, u32[]{:S(2)}, u32[]{:S(2)}) collective-permute-start(f32[256,256]{1,0:T(8,128)S(1)} %get-tuple-element.37), channel_id=1, source_target_pairs={{0,8},{8,0},{16,24},{24,16},{1,9},{9,1},{17,25},{25,17},{2,10},{10... | collective-permute-start | bytes 786440 | tf_op jit(solution)/shard_map/ppermute | solution.py:284
  77.5 2.6 %collective-permute-start.11 = (f32[256,256]{1,0:T(8,128)S(1)}, f32[256,256]{1,0:T(8,128)S(1)}, u32[]{:S(2)}, u32[]{:S(2)}) collective-permute-start(f32[256,256]{1,0:T(8,128)S(1)} %add.25), channel_id=1, source_target_pairs={{0,16},{8,24},{16,0},{24,8},{1,17},{9,25},{17,1},{25,9},{2,18},{10... | collective-permute-start | bytes 786440 | tf_op jit(solution)/shard_map/ppermute | solution.py:284
  80.1 2.9 %shard_map.149 = f32[256,256]{1,0:T(8,128)S(1)} custom-call(s32[2]{0:T(128)S(1)} %pad_add_fusion.ids, f32[8,64,128]{2,1,0:T(8,128)S(1)} %collective-permute-done.7.above, f32[8,256,128]{2,1,0:T(8,128)S(1)} %get-tuple-element.34.image, f32[8,64,128]{2,1,0:T(8,128)S(1)} %collective-permute-done.8.below, f32[2,192,256]{2,1,0:T(8,128)S(1)} %spectrum.1.spec, ...), custom_call_target="tpu_custom_call" | custom-call | tf_op jit(solution)/shard_map/pallas_call | solution.py:395
  83.1 4.5 %collective-permute-done.15 = f32[256,256]{1,0:T(8,128)S(1)} collective-permute-done((f32[256,256]{1,0:T(8,128)S(1)}, f32[256,256]{1,0:T(8,128)S(1)}, u32[]{:S(2)}, u32[]{:S(2)}) %collective-permute-start.15) | collective-permute-done | bytes 262176 | tf_op jit(solution)/shard_map/ppermute | solution.py:284
  88.2 15.2 %collective-permute-done.11 = f32[256,256]{1,0:T(8,128)S(1)} collective-permute-done((f32[256,256]{1,0:T(8,128)S(1)}, f32[256,256]{1,0:T(8,128)S(1)}, u32[]{:S(2)}, u32[]{:S(2)}) %collective-permute-start.11) | collective-permute-done | bytes 262176 | tf_op jit(solution)/shard_map/ppermute | solution.py:284
  (58 shorter events, 12.4 us)
Async XLA Ops:
  13.0 33.2 %all-to-all-start = ((f32[16,128,128]{2,1,0:T(8,128)}), f32[16,128,128]{2,1,0:T(8,128)S(1)}, u32[]{:S(2)}, u32[]{:S(2)}) async-start(f32[16,128,128]{2,1,0:T(8,128)} %warp_flux.1), calls=%async_computation | async-start | bytes 2097152 | tf_op jit(solution)/shard_map/all_to_all | solution.py:355
  24.9 4.0 %collective-permute-start = (f32[2,136,128]{2,1,0:T(8,128)S(1)}, f32[2,136,128]{2,1,0:T(8,128)S(1)}, u32[]{:S(2)}, u32[]{:S(2)}) collective-permute-start(f32[2,136,128]{2,1,0:T(8,128)S(1)} %get-tuple-element.21), channel_id=1, source_target_pairs={{0,1},{1,0},{2,3},{3,2},{4,5},{5,4},{6,7},{7,6},{8,9},{9,8},{10,11... | collective-permute-start | bytes 417800 | tf_op jit(solution)/shard_map/ppermute | solution.py:332
  25.4 8.0 %collective-permute-start.1 = (f32[2,136,128]{2,1,0:T(8,128)S(1)}, f32[2,136,128]{2,1,0:T(8,128)S(1)}, u32[]{:S(2)}, u32[]{:S(2)}) collective-permute-start(f32[2,136,128]{2,1,0:T(8,128)S(1)} %get-tuple-element.22), channel_id=1, source_target_pairs={{0,2},{1,3},{2,0},{3,1},{4,6},{5,7},{6,4},{7,5},{8,10},{9,11},{10,... | collective-permute-start | bytes 417800 | tf_op jit(solution)/shard_map/ppermute | solution.py:332
  25.4 11.4 %collective-permute-start.2 = (f32[2,136,128]{2,1,0:T(8,128)S(1)}, f32[2,136,128]{2,1,0:T(8,128)S(1)}, u32[]{:S(2)}, u32[]{:S(2)}) collective-permute-start(f32[2,136,128]{2,1,0:T(8,128)S(1)} %get-tuple-element.23), channel_id=1, source_target_pairs={{0,3},{1,2},{2,1},{3,0},{4,7},{5,6},{6,5},{7,4},{8,11},{9,10},{10,... | collective-permute-start | bytes 417800 | tf_op jit(solution)/shard_map/ppermute | solution.py:332
  27.1 9.6 %collective-permute-start.3 = (f32[2,136,128]{2,1,0:T(8,128)S(1)}, f32[2,136,128]{2,1,0:T(8,128)S(1)}, u32[]{:S(2)}, u32[]{:S(2)}) collective-permute-start(f32[2,136,128]{2,1,0:T(8,128)S(1)} %get-tuple-element.24), channel_id=1, source_target_pairs={{0,4},{1,5},{2,6},{3,7},{4,0},{5,1},{6,2},{7,3},{8,12},{9,13},{10,... | collective-permute-start | bytes 417800 | tf_op jit(solution)/shard_map/ppermute | solution.py:332
  28.3 9.6 %collective-permute-start.4 = (f32[2,136,128]{2,1,0:T(8,128)S(1)}, f32[2,136,128]{2,1,0:T(8,128)S(1)}, u32[]{:S(2)}, u32[]{:S(2)}) collective-permute-start(f32[2,136,128]{2,1,0:T(8,128)S(1)} %get-tuple-element.25), channel_id=1, source_target_pairs={{0,5},{1,4},{2,7},{3,6},{4,1},{5,0},{6,3},{7,2},{8,13},{9,12},{10,... | collective-permute-start | bytes 417800 | tf_op jit(solution)/shard_map/ppermute | solution.py:332
  28.9 11.2 %collective-permute-start.5 = (f32[2,136,128]{2,1,0:T(8,128)S(1)}, f32[2,136,128]{2,1,0:T(8,128)S(1)}, u32[]{:S(2)}, u32[]{:S(2)}) collective-permute-start(f32[2,136,128]{2,1,0:T(8,128)S(1)} %get-tuple-element.26), channel_id=1, source_target_pairs={{0,6},{1,7},{2,4},{3,5},{4,2},{5,3},{6,0},{7,1},{8,14},{9,15},{10,... | collective-permute-start | bytes 417800 | tf_op jit(solution)/shard_map/ppermute | solution.py:332
  33.4 9.9 %collective-permute-start.6 = (f32[2,136,128]{2,1,0:T(8,128)S(1)}, f32[2,136,128]{2,1,0:T(8,128)S(1)}, u32[]{:S(2)}, u32[]{:S(2)}) collective-permute-start(f32[2,136,128]{2,1,0:T(8,128)S(1)} %get-tuple-element.27), channel_id=1, source_target_pairs={{0,7},{1,6},{2,5},{3,4},{4,3},{5,2},{6,1},{7,0},{8,15},{9,14},{10,... | collective-permute-start | bytes 417800 | tf_op jit(solution)/shard_map/ppermute | solution.py:332
  46.3 6.1 %copy-start = (bf16[2,2,256,256]{3,2,1,0:T(8,128)(2,1)S(1)}, bf16[2,2,256,256]{3,2,1,0:T(8,128)(2,1)}, u32[]{:S(2)}) copy-start(bf16[2,2,256,256]{3,2,1,0:T(8,128)(2,1)} %constant.22.clone.col_fwd) | copy-start | bytes 1572868
  46.3 6.1 %copy-start.11 = (f32[4,128,128]{2,1,0:T(8,128)S(1)}, f32[4,128,128]{2,1,0:T(8,128)}, u32[]{:S(2)}) copy-start(f32[4,128,128]{2,1,0:T(8,128)} %basis.1) | copy-start | bytes 786436
  46.3 6.1 %copy-start.12 = (bf16[2,384,128]{2,1,0:T(8,128)(2,1)S(1)}, bf16[2,384,128]{2,1,0:T(8,128)(2,1)}, u32[]{:S(2)}) copy-start(bf16[2,384,128]{2,1,0:T(8,128)(2,1)} %constant.21.clone.row_ker) | copy-start | bytes 589828
  46.3 12.7 %copy-start.3 = (bf16[2,256,384]{2,1,0:T(8,128)(2,1)S(1)}, bf16[2,256,384]{2,1,0:T(8,128)(2,1)}, u32[]{:S(2)}) copy-start(bf16[2,256,384]{2,1,0:T(8,128)(2,1)} %constant.24.clone.row_inv) | copy-start | bytes 1179652
  47.2 9.5 %collective-permute-start.7 = (f32[8,64,128]{2,1,0:T(8,128)S(1)}, f32[8,64,128]{2,1,0:T(8,128)S(1)}, u32[]{:S(2)}, u32[]{:S(2)}) collective-permute-start(f32[8,64,128]{2,1,0:T(8,128)S(1)} %get-tuple-element.33), channel_id=1, source_target_pairs={{0,1},{1,2},{2,3},{3,4},{4,5},{5,6},{6,7},{8,9},{9,10},{10,11},{11... | collective-permute-start | bytes 786440 | tf_op jit(solution)/shard_map/ppermute | solution.py:390
  50.3 8.8 %copy-start.1 = (bf16[2,384,384]{2,1,0:T(8,128)(2,1)S(1)}, bf16[2,384,384]{2,1,0:T(8,128)(2,1)}, u32[]{:S(2)}) copy-start(bf16[2,384,384]{2,1,0:T(8,128)(2,1)} %constant.20.clone.row_fwd) | copy-start | bytes 1769476
  50.3 8.7 %copy-start.2 = (bf16[2,2,256,256]{3,2,1,0:T(8,128)(2,1)S(1)}, bf16[2,2,256,256]{3,2,1,0:T(8,128)(2,1)}, u32[]{:S(2)}) copy-start(bf16[2,2,256,256]{3,2,1,0:T(8,128)(2,1)} %constant.23.clone.col_inv) | copy-start | bytes 1572868
  50.3 8.7 %collective-permute-start.8 = (f32[8,64,128]{2,1,0:T(8,128)S(1)}, f32[8,64,128]{2,1,0:T(8,128)S(1)}, u32[]{:S(2)}, u32[]{:S(2)}) collective-permute-start(f32[8,64,128]{2,1,0:T(8,128)S(1)} %get-tuple-element.35), channel_id=1, source_target_pairs={{1,0},{2,1},{3,2},{4,3},{5,4},{6,5},{7,6},{9,8},{10,9},{11,10},{12... | collective-permute-start | bytes 786440 | tf_op jit(solution)/shard_map/ppermute | solution.py:391
  53.5 12.5 %collective-permute-start.14 = (f32[256,256]{1,0:T(8,128)S(1)}, f32[256,256]{1,0:T(8,128)S(1)}, u32[]{:S(2)}, u32[]{:S(2)}) collective-permute-start(f32[256,256]{1,0:T(8,128)S(1)} %get-tuple-element.29.rest_0_), channel_id=1, source_target_pairs={{0,8},{24,16},{1,9},{25,17},{2,10},{26,18},{3,11},{27,19},{4,12},{... | collective-permute-start | bytes 786440 | tf_op jit(solution)/shard_map/ppermute | solution.py:284
  62.0 13.8 %collective-permute-start.10 = (f32[256,256]{1,0:T(8,128)S(1)}, f32[256,256]{1,0:T(8,128)S(1)}, u32[]{:S(2)}, u32[]{:S(2)}) collective-permute-start(f32[256,256]{1,0:T(8,128)S(1)} %shard_map.150), channel_id=1, source_target_pairs={{0,8},{24,16},{1,9},{25,17},{2,10},{26,18},{3,11},{27,19},{4,12},{... | collective-permute-start | bytes 786440 | tf_op jit(solution)/shard_map/ppermute | solution.py:284
  65.2 12.3 %collective-permute-start.16 = (f32[256,256]{1,0:T(8,128)S(1)}, f32[256,256]{1,0:T(8,128)S(1)}, u32[]{:S(2)}, u32[]{:S(2)}) collective-permute-start(f32[256,256]{1,0:T(8,128)S(1)} %get-tuple-element.31.rest_2_.rest_1_), channel_id=1, source_target_pairs={{0,8},{8,0},{16,24},{24,16},{1,9},{9,1},{17,25},{25,17},{2,10},{10... | collective-permute-start | bytes 786440 | tf_op jit(solution)/shard_map/ppermute | solution.py:284
  65.3 17.8 %collective-permute-start.13 = (f32[256,256]{1,0:T(8,128)S(1)}, f32[256,256]{1,0:T(8,128)S(1)}, u32[]{:S(2)}, u32[]{:S(2)}) collective-permute-start(f32[256,256]{1,0:T(8,128)S(1)} %get-tuple-element.29.rest_0_), channel_id=1, source_target_pairs={{8,16},{16,8},{9,17},{17,9},{10,18},{18,10},{11,19},{19,11},{12,20... | collective-permute-start | bytes 786440 | tf_op jit(solution)/shard_map/ppermute | solution.py:284
  66.0 21.6 %collective-permute-start.15 = (f32[256,256]{1,0:T(8,128)S(1)}, f32[256,256]{1,0:T(8,128)S(1)}, u32[]{:S(2)}, u32[]{:S(2)}) collective-permute-start(f32[256,256]{1,0:T(8,128)S(1)} %add.29), channel_id=1, source_target_pairs={{0,16},{8,24},{16,0},{24,8},{1,17},{9,25},{17,1},{25,9},{2,18},{10... | collective-permute-start | bytes 786440 | tf_op jit(solution)/shard_map/ppermute | solution.py:284
  69.9 18.3 %collective-permute-start.9 = (f32[256,256]{1,0:T(8,128)S(1)}, f32[256,256]{1,0:T(8,128)S(1)}, u32[]{:S(2)}, u32[]{:S(2)}) collective-permute-start(f32[256,256]{1,0:T(8,128)S(1)} %shard_map.150), channel_id=1, source_target_pairs={{8,16},{16,8},{9,17},{17,9},{10,18},{18,10},{11,19},{19,11},{12,20... | collective-permute-start | bytes 786440 | tf_op jit(solution)/shard_map/ppermute | solution.py:284
  75.8 12.4 %collective-permute-start.12 = (f32[256,256]{1,0:T(8,128)S(1)}, f32[256,256]{1,0:T(8,128)S(1)}, u32[]{:S(2)}, u32[]{:S(2)}) collective-permute-start(f32[256,256]{1,0:T(8,128)S(1)} %get-tuple-element.37), channel_id=1, source_target_pairs={{0,8},{8,0},{16,24},{24,16},{1,9},{9,1},{17,25},{25,17},{2,10},{10... | collective-permute-start | bytes 786440 | tf_op jit(solution)/shard_map/ppermute | solution.py:284
  77.5 25.9 %collective-permute-start.11 = (f32[256,256]{1,0:T(8,128)S(1)}, f32[256,256]{1,0:T(8,128)S(1)}, u32[]{:S(2)}, u32[]{:S(2)}) collective-permute-start(f32[256,256]{1,0:T(8,128)S(1)} %add.25), channel_id=1, source_target_pairs={{0,16},{8,24},{16,0},{24,8},{1,17},{9,25},{17,1},{25,9},{2,18},{10... | collective-permute-start | bytes 786440 | tf_op jit(solution)/shard_map/ppermute | solution.py:284
  (11 other events, 25.5 us)

commit v5 on v4

--- a/solution.py
+++ b/solution.py
@@ -129,23 +129,6 @@
     return dot(weights(rows, 1), data(mid, 0))
 
 
-def fetch(refs, buf, sems):
-    copies = [
-        [pltpu.make_async_copy(ref.at[0, 0, q], buf.at[i, q], sems.at[i, q]) for i, ref in enumerate(refs)]
-        for q in range(buf.shape[1])
-    ]
-    for piece in copies:
-        for copy in piece:
-            copy.start()
-
-    def get(q):
-        for copy in copies[q]:
-            copy.wait()
-        return [buf[i, q] for i in range(len(refs))]
-
-    return get
-
-
 def run(copies):
     for copy in copies:
         copy.start()
@@ -153,49 +136,52 @@
         copy.wait()
 
 
-def warp_weight_body(ids, owner, slot, extent, ivar, rows, cols, *rest):
+def warp_weight_body(ids, owner, slot, extent, ivar_far, rows_far, cols_far, flux_far, *rest):
+    *outs, ivar, rows, cols, flux, send, sems = rest
     side = ivar.shape[3]
-    *outs, buf, buf_sems, send, sems = rest
-    get = fetch((ivar, rows, cols), buf, buf_sems)
+    later = pltpu.make_async_copy(flux_far, flux, sems.at[3])
+    far = (ivar_far, rows_far, cols_far)
+    copies = [pltpu.make_async_copy(a, b, sems.at[n]) for n, (a, b) in enumerate(zip(far, (ivar, rows, cols)))]
+    for copy in [*copies, later]:
+        copy.start()
     for d in range(len(outs)):
         for rank in range(CAP):
             send[d, rank, side:, :] = jnp.full((META, side), -1.0, F32)
+    for copy in copies:
+        copy.wait()
     for q, to, _, rank, at in places(ids, owner, slot):
-        weight, row_map, col_map = get(q)
-        send[to, rank, :side, :] = warp(masked(extent, weight, q), row_map, col_map)
+        send[to, rank, :side, :] = warp(masked(extent, ivar[0, 0, q], q), rows[0, 0, q], cols[0, 0, q])
         send[to, rank, side:, :] = jnp.full((META, side), at.astype(F32), F32)
-    run([pltpu.make_async_copy(send.at[d], out, sems.at[d]) for d, out in enumerate(outs)])
-
-
-def warp_flux_body(ids, owner, slot, extent, ivar, rows, cols, flux, out, buf, buf_sems):
-    get = fetch((ivar, rows, cols, flux), buf, buf_sems)
+    for d, out in enumerate(outs):
+        out[...] = send[d]
+    later.wait()
+
+
+def warp_flux_body(ids, owner, slot, extent, ivar, rows, cols, flux, out):
     for q, _, own, rank, _ in places(ids, owner, slot):
-        weight, row_map, col_map, value = get(q)
-        out[own * CAP + rank] = warp(masked(extent, weight, q) * value, row_map, col_map)
-
-
-def weight_body(ids, *rest):
+        plane = masked(extent, ivar[0, 0, q], q) * flux[0, 0, q]
+        out[own * CAP + rank] = warp(plane, rows[0, 0, q], cols[0, 0, q])
+
+
+def weight_body(ids, own, *rest):
     *rest, slot_out, acc, buf, sems = rest
     count = slot_out.shape[0] // CAP
-    got, out = rest[:count], rest[count:]
-    copies = [pltpu.make_async_copy(ref, buf.at[d], sems.at[d]) for d, ref in enumerate(got)]
-    for copy in copies:
-        copy.start()
+    far, out = rest[: count - 1], rest[count - 1 :]
+    run([pltpu.make_async_copy(ref, buf.at[d], sems.at[d]) for d, ref in enumerate(far)])
+    got = [own] + [buf.at[d] for d in range(count - 1)]
     side = acc.shape[1]
     spare = acc.shape[0] - 1
     per_tile = out[0].shape[1] // side
     acc[...] = jnp.zeros(acc.shape, F32)
-    for copy in copies:
-        copy.wait()
     slots = []
     for d in range(count):
         for rank in range(CAP):
-            at = jnp.max(buf[d, rank, side:, :]).astype(jnp.int32)
+            at = jnp.max(got[d][rank, side:, :]).astype(jnp.int32)
             slots.append(jnp.where(at < 0, spare, at))
     for n, at in enumerate(slots):
         d, rank = divmod(n, CAP)
         slot_out[partner(ids[0], d) * CAP + rank] = at
-        acc[at] += buf[d, rank, :side, :]
+        acc[at] += got[d][rank, :side, :]
     for k in range(len(out)):
         for c in range(per_tile):
             for r in range(BR):
@@ -306,7 +292,7 @@
 def coadd_patches(piece_flux, piece_ivar, warp_rows, warp_cols, piece_owner, piece_slot, piece_extent, basis, coeffs):
     owners = lax.axis_size("bulk")
     visits = lax.axis_size("visit")
-    pieces, side = piece_flux.shape[2:4]
+    _, side = piece_flux.shape[2:4]
     assert side == LANES and side == 2 * HALO and owners & (owners - 1) == 0
     rows_dev = BR * side
     per_tile = BC // visits
@@ -323,8 +309,8 @@
 
     hbm = pl.BlockSpec(memory_space=pltpu.HBM)
 
-    def piece_buffers(count):
-        return [pltpu.VMEM((count, pieces, side, side), F32), pltpu.SemaphoreType.DMA((count, pieces))]
+    def in_hbm(*arrays):
+        return [pltpu.with_memory_space_constraint(a, pltpu.HBM) for a in arrays]
 
     def exchange(sent):
         got = [sent[0]]
@@ -332,26 +318,24 @@
             got.append(lax.ppermute(sent[d], "bulk", [(i, i ^ d) for i in range(owners)]))
         return got
 
-    sent_weight = pl.pallas_call(
+    *sent_weight, ivar_near, rows_near, cols_near, flux_near = pl.pallas_call(
         warp_weight_body,
-        out_shape=[arr(CAP, side + META, side)] * owners,
-        in_specs=[SMEM] * 4 + [hbm] * 3,
-        out_specs=[hbm] * owners,
-        scratch_shapes=piece_buffers(3)
-        + [pltpu.VMEM((owners, CAP, side + META, side), F32), pltpu.SemaphoreType.DMA((owners,))],
+        out_shape=[arr(CAP, side + META, side)] * owners + [arr(*piece_flux.shape)] * 4,
+        in_specs=[SMEM] * 4 + [hbm] * 4,
+        out_specs=[VMEM] * (owners + 4),
+        scratch_shapes=[pltpu.VMEM((owners, CAP, side + META, side), F32), pltpu.SemaphoreType.DMA((4,))],
         compiler_params=params,
         name="warp_weight",
-    )(*facts, piece_ivar, warp_rows, warp_cols)
+    )(*facts, *in_hbm(piece_ivar, warp_rows, warp_cols, piece_flux))
     got_weight = exchange(sent_weight)
     sent_flux = pl.pallas_call(
         warp_flux_body,
         out_shape=arr(cap, side, side),
-        in_specs=[SMEM] * 4 + [hbm] * 4,
+        in_specs=[SMEM] * 4 + [VMEM] * 4,
         out_specs=VMEM,
-        scratch_shapes=piece_buffers(4),
         compiler_params=params,
         name="warp_flux",
-    )(*facts, piece_ivar, warp_rows, warp_cols, piece_flux)
+    )(*facts, ivar_near, rows_near, cols_near, flux_near)
     got_flux = lax.all_to_all(sent_flux, "bulk", split_axis=0, concat_axis=0, tiled=True)
     spec = pl.pallas_call(
         spectrum_body,
@@ -365,16 +349,16 @@
     *ivar, slots = pl.pallas_call(
         weight_body,
         out_shape=[tile] * visits + [jax.ShapeDtypeStruct((cap,), jnp.int32)],
-        in_specs=[SMEM] + [hbm] * owners,
+        in_specs=[SMEM, VMEM] + [hbm] * (owners - 1),
         out_specs=[VMEM] * visits + [SMEM],
         scratch_shapes=[
             pltpu.VMEM((BR * BC + 1, side, side), F32),
-            pltpu.VMEM((owners, CAP, side + META, side), F32),
-            pltpu.SemaphoreType.DMA((owners,)),
+            pltpu.VMEM((owners - 1, CAP, side + META, side), F32),
+            pltpu.SemaphoreType.DMA((owners - 1,)),
         ],
         compiler_params=params,
         name="weights",
-    )(ids, *got_weight)
+    )(ids, got_weight[0], *in_hbm(*got_weight[1:]))
     weight_sum = VisitSum(visits)
     weight_sum.push(*ivar)
     image, top, bottom = pl.pallas_call(
@@ -389,7 +373,7 @@
     ends = owners - 1
     above = lax.ppermute(bottom, "bulk", [(i, i + 1) for i in range(ends)])
     below = lax.ppermute(top, "bulk", [(i + 1, i) for i in range(ends)])
-    weight_map = functools.reduce(jnp.add, weight_sum.parts())
+    weight_map = lax.optimization_barrier(functools.reduce(jnp.add, weight_sum.parts()))
 
     def convolve(first, count):
         return pl.pallas_call(

time: 105 us -> 97.7 us (0.930)
  the two profiles are of different devices: /device:TPU:3 before, /device:TPU:4 now
where the time goes in v5:
time: 97.7 us; the launch traced here: 97.3 us
  waiting for transfers between devices  40.7 us (42%)
  starting transfers between devices  30.6 us (31%)
  Pallas kernels  22.6 us (23%)
  local copies, waits for them, and re-layouts  1.38 us (1%)
  other arithmetic  1.01 us (1%)
  between operations  0.99 us (1%)
    ppermute x8, waiting for transfers between devices, send(): self.sent += [lax.ppermute(tile, 'visit', route) for route in routes]  20.5 us
    ppermute x7, waiting for transfers between devices, exchange(): lax.ppermute(sent[d], 'bulk', [(i, i ^ d) for i in range(owners)])  20.2 us
    ppermute x8, starting transfers between devices, send(): self.sent += [lax.ppermute(tile, 'visit', route) for route in routes]  14.7 us
    pallas_call x3, Pallas kernels, convolve(): pl.pallas_call(functools.partial(conv_body, first, visits), out_shape=[ti...  10.9 us
    ppermute x7, starting transfers between devices, exchange(): lax.ppermute(sent[d], 'bulk', [(i, i ^ d) for i in range(owners)])  5.07 us
    ppermute x1, starting transfers between devices, coadd_patches(): below = lax.ppermute(top, 'bulk', [(i + 1, i) for i in range(ends)])  4.29 us
    all_to_all x1, starting transfers between devices, coadd_patches(): lax.all_to_all(sent_flux, 'bulk', split_axis=0, concat_axis=0, tiled=True)  4.23 us
    pallas_call x1, Pallas kernels, coadd_patches(): pl.pallas_call(warp_weight_body, out_shape=[arr(CAP, side + META, side)]...  3.78 us
  transfers between devices with their start and end apart: 18, of which 7 were waited for; matrix products, arithmetic and copies ran while one was open for 0% of the time, Pallas kernels for 15%

profile of v5, /device:TPU:4, one launch (start us, length us, event | category | flops | bytes accessed | tf_op | source)
XLA Modules:
  0.0 97.3 jit_solution(9924591684786077538)
XLA Ops:
  1.4 3.8 %warp_weight.1 = (f32[2,136,128]{2,1,0:T(8,128)S(1)}, f32[2,136,128]{2,1,0:T(8,128)S(1)}, f32[2,136,128]{2,1,0:T(8,128)S(1)}, f32[2,136,128]{2,1,0:T(8,128)S(1)}...) custom-call(s32[2]{0:T(128)S(1)} %pad_add_fusion.ids, ...), custom_call_target="tpu_custom_call" | custom-call | tf_op jit(solution)/shard_map/warp_weight/pallas_call | solution.py:321
  5.2 3.3 %warp_flux.1 = f32[16,128,128]{2,1,0:T(8,128)} custom-call(s32[2]{0:T(128)S(1)} %pad_add_fusion.ids, s32[1,1,1,8]{3,2,1,0:T(1,128)S(1)} %bitcast.7, s32[1,1,8]{2,1,0:T(1,128)S(1)} %copy-done.8, s32[1,1,2,8]{3,2,1,0:T(2,128)S(1)} %bitcast.5, f32[1,1,8,128,128]{4,3,2,1,0:T(8,128)S(1)} %get-tuple-element.33.ivar, ...), custom_call_target="tpu_custom_call" | custom-call | tf_op jit(solution)/shard_map/warp_flux/pallas_call | solution.py:331
  8.5 4.2 %all-to-all-start = ((f32[16,128,128]{2,1,0:T(8,128)}), f32[16,128,128]{2,1,0:T(8,128)S(1)}, u32[]{:S(2)}, u32[]{:S(2)}) async-start(f32[16,128,128]{2,1,0:T(8,128)} %warp_flux.1), calls=%async_computation | async-start | bytes 2097152 | tf_op jit(solution)/shard_map/all_to_all | solution.py:339
  12.8 1.5 %collective-permute-start.1 = (f32[2,136,128]{2,1,0:T(8,128)S(1)}, f32[2,136,128]{2,1,0:T(8,128)S(1)}, u32[]{:S(2)}, u32[]{:S(2)}) collective-permute-start(f32[2,136,128]{2,1,0:T(8,128)S(1)} %get-tuple-element.26), channel_id=1, source_target_pairs={{0,2},{1,3},{2,0},{3,1},{4,6},{5,7},{6,4},{7,5},{8,10},{9,11},{10,... | collective-permute-start | bytes 417800 | tf_op jit(solution)/shard_map/ppermute | solution.py:318
  14.9 1.5 %collective-permute-start.4 = (f32[2,136,128]{2,1,0:T(8,128)S(1)}, f32[2,136,128]{2,1,0:T(8,128)S(1)}, u32[]{:S(2)}, u32[]{:S(2)}) collective-permute-start(f32[2,136,128]{2,1,0:T(8,128)S(1)} %get-tuple-element.29), channel_id=1, source_target_pairs={{0,5},{1,4},{2,7},{3,6},{4,1},{5,0},{6,3},{7,2},{8,13},{9,12},{10,... | collective-permute-start | bytes 417800 | tf_op jit(solution)/shard_map/ppermute | solution.py:318
  16.3 1.5 %collective-permute-start.5 = (f32[2,136,128]{2,1,0:T(8,128)S(1)}, f32[2,136,128]{2,1,0:T(8,128)S(1)}, u32[]{:S(2)}, u32[]{:S(2)}) collective-permute-start(f32[2,136,128]{2,1,0:T(8,128)S(1)} %get-tuple-element.30), channel_id=1, source_target_pairs={{0,6},{1,7},{2,4},{3,5},{4,2},{5,3},{6,0},{7,1},{8,14},{9,15},{10,... | collective-permute-start | bytes 417800 | tf_op jit(solution)/shard_map/ppermute | solution.py:318
  17.8 12.4 %collective-permute-done.1.rest_1_ = f32[2,136,128]{2,1,0:T(8,128)S(1)} collective-permute-done((f32[2,136,128]{2,1,0:T(8,128)S(1)}, f32[2,136,128]{2,1,0:T(8,128)S(1)}, u32[]{:S(2)}, u32[]{:S(2)}) %collective-permute-start.1) | collective-permute-done | bytes 139296 | tf_op jit(solution)/shard_map/ppermute | solution.py:318
  30.2 1.8 %collective-permute-done.2.rest_2_ = f32[2,136,128]{2,1,0:T(8,128)S(1)} collective-permute-done((f32[2,136,128]{2,1,0:T(8,128)S(1)}, f32[2,136,128]{2,1,0:T(8,128)S(1)}, u32[]{:S(2)}, u32[]{:S(2)}) %collective-permute-start.2) | collective-permute-done | bytes 139296 | tf_op jit(solution)/shard_map/ppermute | solution.py:318
  32.1 4.1 %collective-permute-done.5.rest_5_ = f32[2,136,128]{2,1,0:T(8,128)S(1)} collective-permute-done((f32[2,136,128]{2,1,0:T(8,128)S(1)}, f32[2,136,128]{2,1,0:T(8,128)S(1)}, u32[]{:S(2)}, u32[]{:S(2)}) %collective-permute-start.5) | collective-permute-done | bytes 139296 | tf_op jit(solution)/shard_map/ppermute | solution.py:318
  36.2 1.8 %collective-permute-done.6.rest_6_ = f32[2,136,128]{2,1,0:T(8,128)S(1)} collective-permute-done((f32[2,136,128]{2,1,0:T(8,128)S(1)}, f32[2,136,128]{2,1,0:T(8,128)S(1)}, u32[]{:S(2)}, u32[]{:S(2)}) %collective-permute-start.6) | collective-permute-done | bytes 139296 | tf_op jit(solution)/shard_map/ppermute | solution.py:318
  38.7 2.7 %weights.1 = (f32[256,256]{1,0:T(8,128)S(1)}, f32[256,256]{1,0:T(8,128)S(1)}, f32[256,256]{1,0:T(8,128)S(1)}, f32[256,256]{1,0:T(8,128)S(1)}, s32[16]{0:T(128)S(1)}) custom-call(s32[2]{0:T(128)S(1)} %pad_add_fusion.ids, f32[2,136,128]{2,1,0:T(8,128)S(1)} %get-tuple-element.24.own, f32[2,136,128]{2,1,0:T(8,128)} %copy-done.11, f32[2,136,128]{2,1,0:T(8,128)} %copy-done.12, ...), custom_call_target="tpu_custom_call" | custom-call | tf_op jit(solution)/shard_map/weights/pallas_call | solution.py:349
  42.3 2.3 %collective-permute-start.7 = (f32[8,64,128]{2,1,0:T(8,128)S(1)}, f32[8,64,128]{2,1,0:T(8,128)S(1)}, u32[]{:S(2)}, u32[]{:S(2)}) collective-permute-start(f32[8,64,128]{2,1,0:T(8,128)S(1)} %get-tuple-element.41), channel_id=1, source_target_pairs={{0,1},{1,2},{2,3},{3,4},{4,5},{5,6},{6,7},{8,9},{9,10},{10,11},{11... | collective-permute-start | bytes 786440 | tf_op jit(solution)/shard_map/ppermute | solution.py:374
  44.7 4.3 %collective-permute-start.8 = (f32[8,64,128]{2,1,0:T(8,128)S(1)}, f32[8,64,128]{2,1,0:T(8,128)S(1)}, u32[]{:S(2)}, u32[]{:S(2)}) collective-permute-start(f32[8,64,128]{2,1,0:T(8,128)S(1)} %get-tuple-element.43), channel_id=1, source_target_pairs={{1,0},{2,1},{3,2},{4,3},{5,4},{6,5},{7,6},{9,8},{10,9},{11,10},{12... | collective-permute-start | bytes 786440 | tf_op jit(solution)/shard_map/ppermute | solution.py:375
  49.0 3.5 %collective-permute-start.14 = (f32[256,256]{1,0:T(8,128)S(1)}, f32[256,256]{1,0:T(8,128)S(1)}, u32[]{:S(2)}, u32[]{:S(2)}) collective-permute-start(f32[256,256]{1,0:T(8,128)S(1)} %get-tuple-element.37.rest_0_), channel_id=1, source_target_pairs={{0,8},{24,16},{1,9},{25,17},{2,10},{26,18},{3,11},{27,19},{4,12},{... | collective-permute-start | bytes 786440 | tf_op jit(solution)/shard_map/ppermute | solution.py:270
  52.5 1.1 %spectrum.1.spec = f32[2,192,256]{2,1,0:T(8,128)S(1)} custom-call(f32[1,4]{1,0:T(1,128)S(1)} %copy-done.9, f32[4,128,128]{2,1,0:T(8,128)S(1)} %copy-done.4, bf16[2,384,128]{2,1,0:T(8,128)(2,1)S(1)} %copy-done.5, bf16[2,2,256,256]{3,2,1,0:T(8,128)(2,1)S(1)} %copy-done), custom_call_target="tpu_custom_call" | custom-call | tf_op jit(solution)/shard_map/spectrum/pallas_call | solution.py:340
  53.7 2.9 %shard_map.150 = f32[256,256]{1,0:T(8,128)S(1)} custom-call(s32[2]{0:T(128)S(1)} %pad_add_fusion.ids, f32[8,64,128]{2,1,0:T(8,128)S(1)} %collective-permute-done.7.above, f32[8,256,128]{2,1,0:T(8,128)S(1)} %get-tuple-element.42.image, f32[8,64,128]{2,1,0:T(8,128)S(1)} %collective-permute-done.8.below, f32[2,192,256]{2,1,0:T(8,128)S(1)} %spectrum.1.spec, ...), custom_call_target="tpu_custom_call" | custom-call | tf_op jit(solution)/shard_map/pallas_call | solution.py:379
  56.6 2.7 %collective-permute-start.10 = (f32[256,256]{1,0:T(8,128)S(1)}, f32[256,256]{1,0:T(8,128)S(1)}, u32[]{:S(2)}, u32[]{:S(2)}) collective-permute-start(f32[256,256]{1,0:T(8,128)S(1)} %shard_map.150), channel_id=1, source_target_pairs={{0,8},{24,16},{1,9},{25,17},{2,10},{26,18},{3,11},{27,19},{4,12},{... | collective-permute-start | bytes 786440 | tf_op jit(solution)/shard_map/ppermute | solution.py:270
  60.0 2.2 %collective-permute-start.16 = (f32[256,256]{1,0:T(8,128)S(1)}, f32[256,256]{1,0:T(8,128)S(1)}, u32[]{:S(2)}, u32[]{:S(2)}) collective-permute-start(f32[256,256]{1,0:T(8,128)S(1)} %get-tuple-element.39.rest_2_.rest_1_), channel_id=1, source_target_pairs={{0,8},{8,0},{16,24},{24,16},{1,9},{9,1},{17,25},{25,17},{2,10},{10... | collective-permute-start | bytes 786440 | tf_op jit(solution)/shard_map/ppermute | solution.py:270
  62.3 0.9 collective-permute-start.15
  63.9 5.0 %shard_map.151 = (f32[256,256]{1,0:T(8,128)S(1)}, f32[256,256]{1,0:T(8,128)S(1)}) custom-call(s32[2]{0:T(128)S(1)} %pad_add_fusion.ids, f32[8,64,128]{2,1,0:T(8,128)S(1)} %collective-permute-done.7.above, f32[8,256,128]{2,1,0:T(8,128)S(1)} %get-tuple-element.42.image, f32[8,64,128]{2,1,0:T(8,128)S(1)} %collective-permute-done.8.below, ...), custom_call_target="tpu_custom_call" | custom-call | tf_op jit(solution)/shard_map/pallas_call | solution.py:379
  68.9 3.9 %collective-permute-start.12 = (f32[256,256]{1,0:T(8,128)S(1)}, f32[256,256]{1,0:T(8,128)S(1)}, u32[]{:S(2)}, u32[]{:S(2)}) collective-permute-start(f32[256,256]{1,0:T(8,128)S(1)} %get-tuple-element.45), channel_id=1, source_target_pairs={{0,8},{8,0},{16,24},{24,16},{1,9},{9,1},{17,25},{25,17},{2,10},{10... | collective-permute-start | bytes 786440 | tf_op jit(solution)/shard_map/ppermute | solution.py:270
  73.4 7.0 %collective-permute-done.15 = f32[256,256]{1,0:T(8,128)S(1)} collective-permute-done((f32[256,256]{1,0:T(8,128)S(1)}, f32[256,256]{1,0:T(8,128)S(1)}, u32[]{:S(2)}, u32[]{:S(2)}) %collective-permute-start.15) | collective-permute-done | bytes 262176 | tf_op jit(solution)/shard_map/ppermute | solution.py:270
  80.5 2.9 %shard_map.149 = f32[256,256]{1,0:T(8,128)S(1)} custom-call(s32[2]{0:T(128)S(1)} %pad_add_fusion.ids, f32[8,64,128]{2,1,0:T(8,128)S(1)} %collective-permute-done.7.above, f32[8,256,128]{2,1,0:T(8,128)S(1)} %get-tuple-element.42.image, f32[8,64,128]{2,1,0:T(8,128)S(1)} %collective-permute-done.8.below, f32[2,192,256]{2,1,0:T(8,128)S(1)} %spectrum.1.spec, ...), custom_call_target="tpu_custom_call" | custom-call | tf_op jit(solution)/shard_map/pallas_call | solution.py:379
  83.5 13.0 %collective-permute-done.11 = f32[256,256]{1,0:T(8,128)S(1)} collective-permute-done((f32[256,256]{1,0:T(8,128)S(1)}, f32[256,256]{1,0:T(8,128)S(1)}, u32[]{:S(2)}, u32[]{:S(2)}) %collective-permute-start.11) | collective-permute-done | bytes 262176 | tf_op jit(solution)/shard_map/ppermute | solution.py:270
  (61 shorter events, 5.9 us)
Async XLA Ops:
  8.5 32.9 %all-to-all-start = ((f32[16,128,128]{2,1,0:T(8,128)}), f32[16,128,128]{2,1,0:T(8,128)S(1)}, u32[]{:S(2)}, u32[]{:S(2)}) async-start(f32[16,128,128]{2,1,0:T(8,128)} %warp_flux.1), calls=%async_computation | async-start | bytes 2097152 | tf_op jit(solution)/shard_map/all_to_all | solution.py:339
  12.7 3.6 %collective-permute-start = (f32[2,136,128]{2,1,0:T(8,128)S(1)}, f32[2,136,128]{2,1,0:T(8,128)S(1)}, u32[]{:S(2)}, u32[]{:S(2)}) collective-permute-start(f32[2,136,128]{2,1,0:T(8,128)S(1)} %get-tuple-element.25), channel_id=1, source_target_pairs={{0,1},{1,0},{2,3},{3,2},{4,5},{5,4},{6,7},{7,6},{8,9},{9,8},{10,11... | collective-permute-start | bytes 417800 | tf_op jit(solution)/shard_map/ppermute | solution.py:318
  12.8 17.4 %collective-permute-start.1 = (f32[2,136,128]{2,1,0:T(8,128)S(1)}, f32[2,136,128]{2,1,0:T(8,128)S(1)}, u32[]{:S(2)}, u32[]{:S(2)}) collective-permute-start(f32[2,136,128]{2,1,0:T(8,128)S(1)} %get-tuple-element.26), channel_id=1, source_target_pairs={{0,2},{1,3},{2,0},{3,1},{4,6},{5,7},{6,4},{7,5},{8,10},{9,11},{10,... | collective-permute-start | bytes 417800 | tf_op jit(solution)/shard_map/ppermute | solution.py:318
  14.3 17.8 %collective-permute-start.2 = (f32[2,136,128]{2,1,0:T(8,128)S(1)}, f32[2,136,128]{2,1,0:T(8,128)S(1)}, u32[]{:S(2)}, u32[]{:S(2)}) collective-permute-start(f32[2,136,128]{2,1,0:T(8,128)S(1)} %get-tuple-element.27), channel_id=1, source_target_pairs={{0,3},{1,2},{2,1},{3,0},{4,7},{5,6},{6,5},{7,4},{8,11},{9,10},{10,... | collective-permute-start | bytes 417800 | tf_op jit(solution)/shard_map/ppermute | solution.py:318
  14.6 17.5 %collective-permute-start.3 = (f32[2,136,128]{2,1,0:T(8,128)S(1)}, f32[2,136,128]{2,1,0:T(8,128)S(1)}, u32[]{:S(2)}, u32[]{:S(2)}) collective-permute-start(f32[2,136,128]{2,1,0:T(8,128)S(1)} %get-tuple-element.28), channel_id=1, source_target_pairs={{0,4},{1,5},{2,6},{3,7},{4,0},{5,1},{6,2},{7,3},{8,12},{9,13},{10,... | collective-permute-start | bytes 417800 | tf_op jit(solution)/shard_map/ppermute | solution.py:318
  14.9 17.2 %collective-permute-start.4 = (f32[2,136,128]{2,1,0:T(8,128)S(1)}, f32[2,136,128]{2,1,0:T(8,128)S(1)}, u32[]{:S(2)}, u32[]{:S(2)}) collective-permute-start(f32[2,136,128]{2,1,0:T(8,128)S(1)} %get-tuple-element.29), channel_id=1, source_target_pairs={{0,5},{1,4},{2,7},{3,6},{4,1},{5,0},{6,3},{7,2},{8,13},{9,12},{10,... | collective-permute-start | bytes 417800 | tf_op jit(solution)/shard_map/ppermute | solution.py:318
  16.3 21.7 %copy-start.11 = (f32[2,136,128]{2,1,0:T(8,128)}, f32[2,136,128]{2,1,0:T(8,128)S(1)}, u32[]{:S(2)}) copy-start(f32[2,136,128]{2,1,0:T(8,128)S(1)} %collective-permute-done.rest_0_) | copy-start | bytes 417796
  16.3 19.9 %collective-permute-start.5 = (f32[2,136,128]{2,1,0:T(8,128)S(1)}, f32[2,136,128]{2,1,0:T(8,128)S(1)}, u32[]{:S(2)}, u32[]{:S(2)}) collective-permute-start(f32[2,136,128]{2,1,0:T(8,128)S(1)} %get-tuple-element.30), channel_id=1, source_target_pairs={{0,6},{1,7},{2,4},{3,5},{4,2},{5,3},{6,0},{7,1},{8,14},{9,15},{10,... | collective-permute-start | bytes 417800 | tf_op jit(solution)/shard_map/ppermute | solution.py:318
  30.2 7.8 %collective-permute-start.6 = (f32[2,136,128]{2,1,0:T(8,128)S(1)}, f32[2,136,128]{2,1,0:T(8,128)S(1)}, u32[]{:S(2)}, u32[]{:S(2)}) collective-permute-start(f32[2,136,128]{2,1,0:T(8,128)S(1)} %get-tuple-element.31), channel_id=1, source_target_pairs={{0,7},{1,6},{2,5},{3,4},{4,3},{5,2},{6,1},{7,0},{8,15},{9,14},{10,... | collective-permute-start | bytes 417800 | tf_op jit(solution)/shard_map/ppermute | solution.py:318
  41.4 11.1 %copy-start = (bf16[2,2,256,256]{3,2,1,0:T(8,128)(2,1)S(1)}, bf16[2,2,256,256]{3,2,1,0:T(8,128)(2,1)}, u32[]{:S(2)}) copy-start(bf16[2,2,256,256]{3,2,1,0:T(8,128)(2,1)} %constant.22.clone.col_fwd) | copy-start | bytes 1572868
  41.4 11.1 %copy-start.4 = (f32[4,128,128]{2,1,0:T(8,128)S(1)}, f32[4,128,128]{2,1,0:T(8,128)}, u32[]{:S(2)}) copy-start(f32[4,128,128]{2,1,0:T(8,128)} %basis.1) | copy-start | bytes 786436
  41.4 11.1 %copy-start.5 = (bf16[2,384,128]{2,1,0:T(8,128)(2,1)S(1)}, bf16[2,384,128]{2,1,0:T(8,128)(2,1)}, u32[]{:S(2)}) copy-start(bf16[2,384,128]{2,1,0:T(8,128)(2,1)} %constant.21.clone.row_ker) | copy-start | bytes 589828
  41.4 12.2 %copy-start.3 = (bf16[2,256,384]{2,1,0:T(8,128)(2,1)S(1)}, bf16[2,256,384]{2,1,0:T(8,128)(2,1)}, u32[]{:S(2)}) copy-start(bf16[2,256,384]{2,1,0:T(8,128)(2,1)} %constant.24.clone.row_inv) | copy-start | bytes 1179652
  42.3 11.3 %collective-permute-start.7 = (f32[8,64,128]{2,1,0:T(8,128)S(1)}, f32[8,64,128]{2,1,0:T(8,128)S(1)}, u32[]{:S(2)}, u32[]{:S(2)}) collective-permute-start(f32[8,64,128]{2,1,0:T(8,128)S(1)} %get-tuple-element.41), channel_id=1, source_target_pairs={{0,1},{1,2},{2,3},{3,4},{4,5},{5,6},{6,7},{8,9},{9,10},{10,11},{11... | collective-permute-start | bytes 786440 | tf_op jit(solution)/shard_map/ppermute | solution.py:374
  44.7 9.0 %collective-permute-start.8 = (f32[8,64,128]{2,1,0:T(8,128)S(1)}, f32[8,64,128]{2,1,0:T(8,128)S(1)}, u32[]{:S(2)}, u32[]{:S(2)}) collective-permute-start(f32[8,64,128]{2,1,0:T(8,128)S(1)} %get-tuple-element.43), channel_id=1, source_target_pairs={{1,0},{2,1},{3,2},{4,3},{5,4},{6,5},{7,6},{9,8},{10,9},{11,10},{12... | collective-permute-start | bytes 786440 | tf_op jit(solution)/shard_map/ppermute | solution.py:375
  49.0 13.2 %collective-permute-start.14 = (f32[256,256]{1,0:T(8,128)S(1)}, f32[256,256]{1,0:T(8,128)S(1)}, u32[]{:S(2)}, u32[]{:S(2)}) collective-permute-start(f32[256,256]{1,0:T(8,128)S(1)} %get-tuple-element.37.rest_0_), channel_id=1, source_target_pairs={{0,8},{24,16},{1,9},{25,17},{2,10},{26,18},{3,11},{27,19},{4,12},{... | collective-permute-start | bytes 786440 | tf_op jit(solution)/shard_map/ppermute | solution.py:270
  56.6 12.3 %collective-permute-start.10 = (f32[256,256]{1,0:T(8,128)S(1)}, f32[256,256]{1,0:T(8,128)S(1)}, u32[]{:S(2)}, u32[]{:S(2)}) collective-permute-start(f32[256,256]{1,0:T(8,128)S(1)} %shard_map.150), channel_id=1, source_target_pairs={{0,8},{24,16},{1,9},{25,17},{2,10},{26,18},{3,11},{27,19},{4,12},{... | collective-permute-start | bytes 786440 | tf_op jit(solution)/shard_map/ppermute | solution.py:270
  59.3 13.6 %collective-permute-start.13 = (f32[256,256]{1,0:T(8,128)S(1)}, f32[256,256]{1,0:T(8,128)S(1)}, u32[]{:S(2)}, u32[]{:S(2)}) collective-permute-start(f32[256,256]{1,0:T(8,128)S(1)} %get-tuple-element.37.rest_0_), channel_id=1, source_target_pairs={{8,16},{16,8},{9,17},{17,9},{10,18},{18,10},{11,19},{19,11},{12,20... | collective-permute-start | bytes 786440 | tf_op jit(solution)/shard_map/ppermute | solution.py:270
  60.0 13.4 %collective-permute-start.16 = (f32[256,256]{1,0:T(8,128)S(1)}, f32[256,256]{1,0:T(8,128)S(1)}, u32[]{:S(2)}, u32[]{:S(2)}) collective-permute-start(f32[256,256]{1,0:T(8,128)S(1)} %get-tuple-element.39.rest_2_.rest_1_), channel_id=1, source_target_pairs={{0,8},{8,0},{16,24},{24,16},{1,9},{9,1},{17,25},{25,17},{2,10},{10... | collective-permute-start | bytes 786440 | tf_op jit(solution)/shard_map/ppermute | solution.py:270
  62.3 18.2 %collective-permute-start.15 = (f32[256,256]{1,0:T(8,128)S(1)}, f32[256,256]{1,0:T(8,128)S(1)}, u32[]{:S(2)}, u32[]{:S(2)}) collective-permute-start(f32[256,256]{1,0:T(8,128)S(1)} %add.29), channel_id=1, source_target_pairs={{0,16},{8,24},{16,0},{24,8},{1,17},{9,25},{17,1},{25,9},{2,18},{10... | collective-permute-start | bytes 786440 | tf_op jit(solution)/shard_map/ppermute | solution.py:270
  63.2 20.3 %collective-permute-start.9 = (f32[256,256]{1,0:T(8,128)S(1)}, f32[256,256]{1,0:T(8,128)S(1)}, u32[]{:S(2)}, u32[]{:S(2)}) collective-permute-start(f32[256,256]{1,0:T(8,128)S(1)} %shard_map.150), channel_id=1, source_target_pairs={{8,16},{16,8},{9,17},{17,9},{10,18},{18,10},{11,19},{19,11},{12,20... | collective-permute-start | bytes 786440 | tf_op jit(solution)/shard_map/ppermute | solution.py:270
  68.9 14.6 %collective-permute-start.12 = (f32[256,256]{1,0:T(8,128)S(1)}, f32[256,256]{1,0:T(8,128)S(1)}, u32[]{:S(2)}, u32[]{:S(2)}) collective-permute-start(f32[256,256]{1,0:T(8,128)S(1)} %get-tuple-element.45), channel_id=1, source_target_pairs={{0,8},{8,0},{16,24},{24,16},{1,9},{9,1},{17,25},{25,17},{2,10},{10... | collective-permute-start | bytes 786440 | tf_op jit(solution)/shard_map/ppermute | solution.py:270
  72.9 23.6 %collective-permute-start.11 = (f32[256,256]{1,0:T(8,128)S(1)}, f32[256,256]{1,0:T(8,128)S(1)}, u32[]{:S(2)}, u32[]{:S(2)}) collective-permute-start(f32[256,256]{1,0:T(8,128)S(1)} %add.25), channel_id=1, source_target_pairs={{0,16},{8,24},{16,0},{24,8},{1,17},{9,25},{17,1},{25,9},{2,18},{10... | collective-permute-start | bytes 786440 | tf_op jit(solution)/shard_map/ppermute | solution.py:270
  80.5 16.0 %copy-start.10 = (f32[256,256]{1,0:T(8,128)}, f32[256,256]{1,0:T(8,128)S(1)}, u32[]{:S(2)}) copy-start(f32[256,256]{1,0:T(8,128)S(1)} %add_add_fusion) | copy-start | bytes 786436
  (12 other events, 58.5 us)

commit v6 on v5

--- a/solution.py
+++ b/solution.py
@@ -109,12 +109,7 @@
 
 
 def tile_at(ids, k, tiles):
-    if tiles != 4:
-        return jnp.int32(k)
-    mine = jnp.int32(LINE[-1][k])
-    for v in range(tiles - 1):
-        mine = jnp.where(ids[1] == v, LINE[v][k], mine)
-    return mine
+    return jnp.bitwise_xor(ids[1], tiles - 1 - k)
 
 
 def masked(extent, ivar, q):
@@ -190,7 +185,8 @@
 
 
 def image_body(ids, slot, got, *rest):
-    *tiles, image, top, bottom, acc = rest
+    *tiles, image, near, far, acc = rest
+    odd_strip = ids[0] % 2 == 1
     side = acc.shape[1]
     per_tile = tiles[0].shape[1] // side
     acc[...] = jnp.zeros(acc.shape, F32)
@@ -203,8 +199,9 @@
                 rows = slice(r * side, (r + 1) * side)
                 weight = tile[rows, c * side : (c + 1) * side]
                 image[to, rows, :] = acc[r * BC + to] / jnp.maximum(weight, 1.0)
-            top[to] = image[to, :HALO, :]
-            bottom[to] = image[to, -HALO:, :]
+            top, bottom = image[to, :HALO, :], image[to, -HALO:, :]
+            near[to] = jnp.where(odd_strip, top, bottom)
+            far[to] = jnp.where(odd_strip, bottom, top)
 
 
 def beside(stacked):
@@ -221,16 +218,19 @@
         out[odd] = dot(lines, fixed(col_fwd.at[odd], 0))
 
 
-def conv_body(first, tiles, ids, above, image, below, spec, row_fwd, col_fwd, col_inv, row_inv, *rest):
+def conv_body(first, tiles, ids, near, image, far, spec, row_fwd, col_fwd, col_inv, row_inv, *rest):
     *rest, lines = rest
     count = len(rest) // 2
     weight, out = rest[:count], rest[count:]
     taps = image.shape[2]
     per_tile = out[0].shape[1] // taps
     freqs = spec.shape[1]
+    odd_strip = ids[0] % 2 == 1
 
     def column(c):
-        return jnp.concatenate([above[c], image[c], below[c]], 0)
+        above = jnp.where(odd_strip, near[c], far[c])
+        below = jnp.where(odd_strip, far[c], near[c])
+        return jnp.concatenate([above, image[c], below], 0)
 
     lead = fixed(row_fwd, 1)
     last = fixed(row_inv, 1)
@@ -257,36 +257,9 @@
         out[k][...] = dot(last, data(jnp.concatenate(cols, 1), 0)) * weight[k][...]
 
 
-LINE = ((3, 2, 1, 0), (2, 3, 0, 1), (1, 0, 3, 2), (0, 1, 2, 3))
-
-
-class VisitSum:
-    def __init__(self, count):
-        self.count = count
-        self.sent = []
-        self.tiles = []
-
-    def send(self, tile, *routes):
-        self.sent += [lax.ppermute(tile, "visit", route) for route in routes]
-
-    def push(self, *tiles):
-        for tile in tiles:
-            k = len(self.tiles)
-            self.tiles.append(tile)
-            if self.count != 4:
-                continue
-            if k == 0:
-                self.send(tile, [(0, 1), (3, 2)])
-                self.send(tile, [(1, 2), (2, 1)])
-            elif k == 1:
-                self.send(tile + self.sent[0], [(0, 2), (1, 3), (2, 0), (3, 1)])
-            elif k == 2:
-                self.send(tile, [(0, 1), (1, 0), (2, 3), (3, 2)])
-
-    def parts(self):
-        if self.count != 4:
-            return [lax.psum_scatter(jnp.stack(self.tiles), "visit", scatter_dimension=0, tiled=False)]
-        return [self.tiles[3], *self.sent[1:]]
+def send_tile(tile, k):
+    visits = lax.axis_size("visit")
+    return lax.ppermute(tile, "visit", [(v, v ^ (visits - 1 - k)) for v in range(visits)])
 
 
 def coadd_patches(piece_flux, piece_ivar, warp_rows, warp_cols, piece_owner, piece_slot, piece_extent, basis, coeffs):
@@ -359,9 +332,9 @@
         compiler_params=params,
         name="weights",
     )(ids, got_weight[0], *in_hbm(*got_weight[1:]))
-    weight_sum = VisitSum(visits)
-    weight_sum.push(*ivar)
-    image, top, bottom = pl.pallas_call(
+    got_tiles = [send_tile(t, k) for k, t in enumerate(ivar[:-1])]
+    weight_map = lax.optimization_barrier(functools.reduce(jnp.add, got_tiles, ivar[-1]))
+    image, near, far = pl.pallas_call(
         image_body,
         out_shape=[arr(BC, rows_dev, side)] + [arr(BC, HALO, side)] * 2,
         in_specs=[SMEM] * 2 + [VMEM] * (1 + visits),
@@ -370,10 +343,9 @@
         compiler_params=params,
         name="image",
     )(ids, slots, got_flux, *ivar)
-    ends = owners - 1
-    above = lax.ppermute(bottom, "bulk", [(i, i + 1) for i in range(ends)])
-    below = lax.ppermute(top, "bulk", [(i + 1, i) for i in range(ends)])
-    weight_map = lax.optimization_barrier(functools.reduce(jnp.add, weight_sum.parts()))
+    pairs = [(i + 1, i + 2) for i in range(0, owners - 2, 2)]
+    far = lax.ppermute(far, "bulk", pairs + [(j, i) for i, j in pairs])
+    near = lax.ppermute(near, "bulk", [(i, i ^ 1) for i in range(owners)])
 
     def convolve(first, count):
         return pl.pallas_call(
@@ -383,13 +355,14 @@
             out_specs=[VMEM] * count,
             scratch_shapes=[pltpu.VMEM((2 * freqs, (per_tile + 1) * side), F32)],
             compiler_params=params,
-        )(ids, above, image, below, spec, row_fwd, col_fwd, col_inv, row_inv, *ivar[first : first + count])
-
-    image_sum = VisitSum(visits)
-    image_sum.push(*convolve(0, 1))
-    image_sum.push(*convolve(1, visits - 2))
-    image_sum.push(*convolve(visits - 1, 1))
-    numerator = functools.reduce(jnp.add, image_sum.parts())
+        )(ids, near, image, far, spec, row_fwd, col_fwd, col_inv, row_inv, *ivar[first : first + count])
+
+    last = visits - 1
+    parts = convolve(0, 1)
+    got = [send_tile(parts[0], 0)]
+    parts = convolve(1, visits - 2)
+    got += [send_tile(part, k + 1) for k, part in enumerate(parts)]
+    numerator = functools.reduce(jnp.add, got, convolve(last, 1)[0])
     return (numerator / jnp.maximum(weight_map, 1.0), weight_map)
 
 

time: 97.7 us -> 96.1 us (0.984)
  the two profiles are of different devices: /device:TPU:4 before, /device:TPU:0 now
where the time goes in v6:
time: 96.1 us; the launch traced here: 95.5 us
  waiting for transfers between devices  44.7 us (47%)
  starting transfers between devices  25 us (26%)
  Pallas kernels  22.6 us (24%)
  local copies, waits for them, and re-layouts  1.37 us (1%)
    ppermute x6, waiting for transfers between devices, send_tile(): lax.ppermute(tile, 'visit', [(v, v ^ visits - 1 - k) for v in range(visit...  24.5 us
    ppermute x7, waiting for transfers between devices, exchange(): lax.ppermute(sent[d], 'bulk', [(i, i ^ d) for i in range(owners)])  20.2 us
    ppermute x6, starting transfers between devices, send_tile(): lax.ppermute(tile, 'visit', [(v, v ^ visits - 1 - k) for v in range(visit...  12 us
    pallas_call x3, Pallas kernels, convolve(): pl.pallas_call(functools.partial(conv_body, first, visits), out_shape=[ti...  10.9 us
    ppermute x7, starting transfers between devices, exchange(): lax.ppermute(sent[d], 'bulk', [(i, i ^ d) for i in range(owners)])  6.57 us
    all_to_all x1, starting transfers between devices, coadd_patches(): lax.all_to_all(sent_flux, 'bulk', split_axis=0, concat_axis=0, tiled=True)  5.2 us
    pallas_call x1, Pallas kernels, coadd_patches(): pl.pallas_call(warp_weight_body, out_shape=[arr(CAP, side + META, side)]...  3.78 us
    pallas_call x1, Pallas kernels, coadd_patches(): pl.pallas_call(warp_flux_body, out_shape=arr(cap, side, side), in_specs=[...  3.28 us
  transfers between devices with their start and end apart: 16, of which 6 were waited for; matrix products, arithmetic and copies ran while one was open for 0% of the time, Pallas kernels for 15%

profile of v6, /device:TPU:0, one launch (start us, length us, event | category | flops | bytes accessed | tf_op | source)
XLA Modules:
  0.0 95.5 jit_solution(5275545818242241924)
XLA Ops:
  1.4 3.8 %warp_weight.1 = (f32[2,136,128]{2,1,0:T(8,128)S(1)}, f32[2,136,128]{2,1,0:T(8,128)S(1)}, f32[2,136,128]{2,1,0:T(8,128)S(1)}, f32[2,136,128]{2,1,0:T(8,128)S(1)}...) custom-call(s32[2]{0:T(128)S(1)} %pad_add_fusion.ids, ...), custom_call_target="tpu_custom_call" | custom-call | tf_op jit(solution)/shard_map/warp_weight/pallas_call | solution.py:294
  5.2 3.3 %warp_flux.1 = f32[16,128,128]{2,1,0:T(8,128)} custom-call(s32[2]{0:T(128)S(1)} %pad_add_fusion.ids, s32[1,1,1,8]{3,2,1,0:T(1,128)S(1)} %bitcast.7, s32[1,1,8]{2,1,0:T(1,128)S(1)} %copy-done.8, s32[1,1,2,8]{3,2,1,0:T(2,128)S(1)} %bitcast.5, f32[1,1,8,128,128]{4,3,2,1,0:T(8,128)S(1)} %get-tuple-element.33.ivar, ...), custom_call_target="tpu_custom_call" | custom-call | tf_op jit(solution)/shard_map/warp_flux/pallas_call | solution.py:304
  8.5 5.2 %all-to-all-start = ((f32[16,128,128]{2,1,0:T(8,128)}), f32[16,128,128]{2,1,0:T(8,128)S(1)}, u32[]{:S(2)}, u32[]{:S(2)}) async-start(f32[16,128,128]{2,1,0:T(8,128)} %warp_flux.1), calls=%async_computation | async-start | bytes 2097152 | tf_op jit(solution)/shard_map/all_to_all | solution.py:312
  14.2 1.6 %collective-permute-start.1 = (f32[2,136,128]{2,1,0:T(8,128)S(1)}, f32[2,136,128]{2,1,0:T(8,128)S(1)}, u32[]{:S(2)}, u32[]{:S(2)}) collective-permute-start(f32[2,136,128]{2,1,0:T(8,128)S(1)} %get-tuple-element.26), channel_id=1, source_target_pairs={{0,2},{1,3},{2,0},{3,1},{4,6},{5,7},{6,4},{7,5},{8,10},{9,11},{10,... | collective-permute-start | bytes 417800 | tf_op jit(solution)/shard_map/ppermute | solution.py:291
  15.8 1.7 %collective-permute-start.3 = (f32[2,136,128]{2,1,0:T(8,128)S(1)}, f32[2,136,128]{2,1,0:T(8,128)S(1)}, u32[]{:S(2)}, u32[]{:S(2)}) collective-permute-start(f32[2,136,128]{2,1,0:T(8,128)S(1)} %get-tuple-element.28), channel_id=1, source_target_pairs={{0,4},{1,5},{2,6},{3,7},{4,0},{5,1},{6,2},{7,3},{8,12},{9,13},{10,... | collective-permute-start | bytes 417800 | tf_op jit(solution)/shard_map/ppermute | solution.py:291
  17.7 2.5 %collective-permute-start.5 = (f32[2,136,128]{2,1,0:T(8,128)S(1)}, f32[2,136,128]{2,1,0:T(8,128)S(1)}, u32[]{:S(2)}, u32[]{:S(2)}) collective-permute-start(f32[2,136,128]{2,1,0:T(8,128)S(1)} %get-tuple-element.30), channel_id=1, source_target_pairs={{0,6},{1,7},{2,4},{3,5},{4,2},{5,3},{6,0},{7,1},{8,14},{9,15},{10,... | collective-permute-start | bytes 417800 | tf_op jit(solution)/shard_map/ppermute | solution.py:291
  20.2 11.5 %collective-permute-done.1.rest_1_ = f32[2,136,128]{2,1,0:T(8,128)S(1)} collective-permute-done((f32[2,136,128]{2,1,0:T(8,128)S(1)}, f32[2,136,128]{2,1,0:T(8,128)S(1)}, u32[]{:S(2)}, u32[]{:S(2)}) %collective-permute-start.1) | collective-permute-done | bytes 139296 | tf_op jit(solution)/shard_map/ppermute | solution.py:291
  31.8 1.8 %collective-permute-done.2.rest_2_ = f32[2,136,128]{2,1,0:T(8,128)S(1)} collective-permute-done((f32[2,136,128]{2,1,0:T(8,128)S(1)}, f32[2,136,128]{2,1,0:T(8,128)S(1)}, u32[]{:S(2)}, u32[]{:S(2)}) %collective-permute-start.2) | collective-permute-done | bytes 139296 | tf_op jit(solution)/shard_map/ppermute | solution.py:291
  33.6 5.0 %collective-permute-done.5.rest_5_ = f32[2,136,128]{2,1,0:T(8,128)S(1)} collective-permute-done((f32[2,136,128]{2,1,0:T(8,128)S(1)}, f32[2,136,128]{2,1,0:T(8,128)S(1)}, u32[]{:S(2)}, u32[]{:S(2)}) %collective-permute-start.5) | collective-permute-done | bytes 139296 | tf_op jit(solution)/shard_map/ppermute | solution.py:291
  38.6 1.8 %collective-permute-done.6.rest_6_ = f32[2,136,128]{2,1,0:T(8,128)S(1)} collective-permute-done((f32[2,136,128]{2,1,0:T(8,128)S(1)}, f32[2,136,128]{2,1,0:T(8,128)S(1)}, u32[]{:S(2)}, u32[]{:S(2)}) %collective-permute-start.6) | collective-permute-done | bytes 139296 | tf_op jit(solution)/shard_map/ppermute | solution.py:291
  41.1 2.7 %weights.1 = (f32[256,256]{1,0:T(8,128)S(1)}, f32[256,256]{1,0:T(8,128)S(1)}, f32[256,256]{1,0:T(8,128)S(1)}, f32[256,256]{1,0:T(8,128)S(1)}, s32[16]{0:T(128)S(1)}) custom-call(s32[2]{0:T(128)S(1)} %pad_add_fusion.ids, f32[2,136,128]{2,1,0:T(8,128)S(1)} %get-tuple-element.24.own, f32[2,136,128]{2,1,0:T(8,128)} %copy-done.11, f32[2,136,128]{2,1,0:T(8,128)} %copy-done.12, ...), custom_call_target="tpu_custom_call" | custom-call | tf_op jit(solution)/shard_map/weights/pallas_call | solution.py:322
  43.8 0.9 image.1
  45.2 0.8 collective-permute-start.8
  46.0 3.7 %collective-permute-start.12 = (f32[256,256]{1,0:T(8,128)S(1)}, f32[256,256]{1,0:T(8,128)S(1)}, u32[]{:S(2)}, u32[]{:S(2)}) collective-permute-start(f32[256,256]{1,0:T(8,128)S(1)} %get-tuple-element.37.rest_0_), channel_id=1, source_target_pairs={{0,24},{8,16},{16,8},{24,0},{1,25},{9,17},{17,9},{25,1},{2,26},{10... | collective-permute-start | bytes 786440 | tf_op jit(solution)/shard_map/ppermute | solution.py:262
  49.7 0.8 collective-permute-start.14
  50.5 1.1 %spectrum.1.spec = f32[2,192,256]{2,1,0:T(8,128)S(1)} custom-call(f32[1,4]{1,0:T(1,128)S(1)} %copy-done.9, f32[4,128,128]{2,1,0:T(8,128)S(1)} %copy-done.4, bf16[2,384,128]{2,1,0:T(8,128)(2,1)S(1)} %copy-done.5, bf16[2,2,256,256]{3,2,1,0:T(8,128)(2,1)S(1)} %copy-done), custom_call_target="tpu_custom_call" | custom-call | tf_op jit(solution)/shard_map/spectrum/pallas_call | solution.py:313
  51.6 2.9 %shard_map.150 = f32[256,256]{1,0:T(8,128)S(1)} custom-call(s32[2]{0:T(128)S(1)} %pad_add_fusion.ids, f32[8,64,128]{2,1,0:T(8,128)S(1)} %collective-permute-done.7.near, f32[8,256,128]{2,1,0:T(8,128)S(1)} %get-tuple-element.42.image, f32[8,64,128]{2,1,0:T(8,128)S(1)} %collective-permute-done.8.far, f32[2,192,256]{2,1,0:T(8,128)S(1)} %spectrum.1.spec, ...), custom_call_target="tpu_custom_call" | custom-call | tf_op jit(solution)/shard_map/pallas_call | solution.py:351
  54.6 3.7 %collective-permute-start.9 = (f32[256,256]{1,0:T(8,128)S(1)}, f32[256,256]{1,0:T(8,128)S(1)}, u32[]{:S(2)}, u32[]{:S(2)}) collective-permute-start(f32[256,256]{1,0:T(8,128)S(1)} %shard_map.150), channel_id=1, source_target_pairs={{0,24},{8,16},{16,8},{24,0},{1,25},{9,17},{17,9},{25,1},{2,26},{10... | collective-permute-start | bytes 786440 | tf_op jit(solution)/shard_map/ppermute | solution.py:262
  58.2 5.0 %shard_map.151 = (f32[256,256]{1,0:T(8,128)S(1)}, f32[256,256]{1,0:T(8,128)S(1)}) custom-call(s32[2]{0:T(128)S(1)} %pad_add_fusion.ids, f32[8,64,128]{2,1,0:T(8,128)S(1)} %collective-permute-done.7.near, f32[8,256,128]{2,1,0:T(8,128)S(1)} %get-tuple-element.42.image, f32[8,64,128]{2,1,0:T(8,128)S(1)} %collective-permute-done.8.far, ...), custom_call_target="tpu_custom_call" | custom-call | tf_op jit(solution)/shard_map/pallas_call | solution.py:351
  63.4 3.8 %collective-permute-start.11 = (f32[256,256]{1,0:T(8,128)S(1)}, f32[256,256]{1,0:T(8,128)S(1)}, u32[]{:S(2)}, u32[]{:S(2)}) collective-permute-start(f32[256,256]{1,0:T(8,128)S(1)} %get-tuple-element.45), channel_id=1, source_target_pairs={{0,8},{8,0},{16,24},{24,16},{1,9},{9,1},{17,25},{25,17},{2,10},{10... | collective-permute-start | bytes 786440 | tf_op jit(solution)/shard_map/ppermute | solution.py:262
  67.2 16.3 %collective-permute-done.13 = f32[256,256]{1,0:T(8,128)S(1)} collective-permute-done((f32[256,256]{1,0:T(8,128)S(1)}, f32[256,256]{1,0:T(8,128)S(1)}, u32[]{:S(2)}, u32[]{:S(2)}) %collective-permute-start.13) | collective-permute-done | bytes 262176 | tf_op jit(solution)/shard_map/ppermute | solution.py:262
  83.6 2.9 %shard_map.149 = f32[256,256]{1,0:T(8,128)S(1)} custom-call(s32[2]{0:T(128)S(1)} %pad_add_fusion.ids, f32[8,64,128]{2,1,0:T(8,128)S(1)} %collective-permute-done.7.near, f32[8,256,128]{2,1,0:T(8,128)S(1)} %get-tuple-element.42.image, f32[8,64,128]{2,1,0:T(8,128)S(1)} %collective-permute-done.8.far, f32[2,192,256]{2,1,0:T(8,128)S(1)} %spectrum.1.spec, ...), custom_call_target="tpu_custom_call" | custom-call | tf_op jit(solution)/shard_map/pallas_call | solution.py:351
  86.5 8.2 %collective-permute-done.10 = f32[256,256]{1,0:T(8,128)S(1)} collective-permute-done((f32[256,256]{1,0:T(8,128)S(1)}, f32[256,256]{1,0:T(8,128)S(1)}, u32[]{:S(2)}, u32[]{:S(2)}) %collective-permute-start.10) | collective-permute-done | bytes 262176 | tf_op jit(solution)/shard_map/ppermute | solution.py:262
  94.7 0.8 maximum_divide_fusion
  (55 shorter events, 2.7 us)
Async XLA Ops:
  8.5 35.3 %all-to-all-start = ((f32[16,128,128]{2,1,0:T(8,128)}), f32[16,128,128]{2,1,0:T(8,128)S(1)}, u32[]{:S(2)}, u32[]{:S(2)}) async-start(f32[16,128,128]{2,1,0:T(8,128)} %warp_flux.1), calls=%async_computation | async-start | bytes 2097152 | tf_op jit(solution)/shard_map/all_to_all | solution.py:312
  13.7 4.0 %collective-permute-start = (f32[2,136,128]{2,1,0:T(8,128)S(1)}, f32[2,136,128]{2,1,0:T(8,128)S(1)}, u32[]{:S(2)}, u32[]{:S(2)}) collective-permute-start(f32[2,136,128]{2,1,0:T(8,128)S(1)} %get-tuple-element.25), channel_id=1, source_target_pairs={{0,1},{1,0},{2,3},{3,2},{4,5},{5,4},{6,7},{7,6},{8,9},{9,8},{10,11... | collective-permute-start | bytes 417800 | tf_op jit(solution)/shard_map/ppermute | solution.py:291
  14.2 17.6 %collective-permute-start.1 = (f32[2,136,128]{2,1,0:T(8,128)S(1)}, f32[2,136,128]{2,1,0:T(8,128)S(1)}, u32[]{:S(2)}, u32[]{:S(2)}) collective-permute-start(f32[2,136,128]{2,1,0:T(8,128)S(1)} %get-tuple-element.26), channel_id=1, source_target_pairs={{0,2},{1,3},{2,0},{3,1},{4,6},{5,7},{6,4},{7,5},{8,10},{9,11},{10,... | collective-permute-start | bytes 417800 | tf_op jit(solution)/shard_map/ppermute | solution.py:291
  15.8 17.8 %collective-permute-start.2 = (f32[2,136,128]{2,1,0:T(8,128)S(1)}, f32[2,136,128]{2,1,0:T(8,128)S(1)}, u32[]{:S(2)}, u32[]{:S(2)}) collective-permute-start(f32[2,136,128]{2,1,0:T(8,128)S(1)} %get-tuple-element.27), channel_id=1, source_target_pairs={{0,3},{1,2},{2,1},{3,0},{4,7},{5,6},{6,5},{7,4},{8,11},{9,10},{10,... | collective-permute-start | bytes 417800 | tf_op jit(solution)/shard_map/ppermute | solution.py:291
  15.8 17.8 %collective-permute-start.3 = (f32[2,136,128]{2,1,0:T(8,128)S(1)}, f32[2,136,128]{2,1,0:T(8,128)S(1)}, u32[]{:S(2)}, u32[]{:S(2)}) collective-permute-start(f32[2,136,128]{2,1,0:T(8,128)S(1)} %get-tuple-element.28), channel_id=1, source_target_pairs={{0,4},{1,5},{2,6},{3,7},{4,0},{5,1},{6,2},{7,3},{8,12},{9,13},{10,... | collective-permute-start | bytes 417800 | tf_op jit(solution)/shard_map/ppermute | solution.py:291
  17.6 16.0 %collective-permute-start.4 = (f32[2,136,128]{2,1,0:T(8,128)S(1)}, f32[2,136,128]{2,1,0:T(8,128)S(1)}, u32[]{:S(2)}, u32[]{:S(2)}) collective-permute-start(f32[2,136,128]{2,1,0:T(8,128)S(1)} %get-tuple-element.29), channel_id=1, source_target_pairs={{0,5},{1,4},{2,7},{3,6},{4,1},{5,0},{6,3},{7,2},{8,13},{9,12},{10,... | collective-permute-start | bytes 417800 | tf_op jit(solution)/shard_map/ppermute | solution.py:291
  17.7 22.8 %copy-start.11 = (f32[2,136,128]{2,1,0:T(8,128)}, f32[2,136,128]{2,1,0:T(8,128)S(1)}, u32[]{:S(2)}) copy-start(f32[2,136,128]{2,1,0:T(8,128)S(1)} %collective-permute-done.rest_0_) | copy-start | bytes 417796
  17.7 20.9 %collective-permute-start.5 = (f32[2,136,128]{2,1,0:T(8,128)S(1)}, f32[2,136,128]{2,1,0:T(8,128)S(1)}, u32[]{:S(2)}, u32[]{:S(2)}) collective-permute-start(f32[2,136,128]{2,1,0:T(8,128)S(1)} %get-tuple-element.30), channel_id=1, source_target_pairs={{0,6},{1,7},{2,4},{3,5},{4,2},{5,3},{6,0},{7,1},{8,14},{9,15},{10,... | collective-permute-start | bytes 417800 | tf_op jit(solution)/shard_map/ppermute | solution.py:291
  31.8 8.7 %copy-start.12 = (f32[2,136,128]{2,1,0:T(8,128)}, f32[2,136,128]{2,1,0:T(8,128)S(1)}, u32[]{:S(2)}) copy-start(f32[2,136,128]{2,1,0:T(8,128)S(1)} %collective-permute-done.1.rest_1_) | copy-start | bytes 417796
  31.8 8.7 %collective-permute-start.6 = (f32[2,136,128]{2,1,0:T(8,128)S(1)}, f32[2,136,128]{2,1,0:T(8,128)S(1)}, u32[]{:S(2)}, u32[]{:S(2)}) collective-permute-start(f32[2,136,128]{2,1,0:T(8,128)S(1)} %get-tuple-element.31), channel_id=1, source_target_pairs={{0,7},{1,6},{2,5},{3,4},{4,3},{5,2},{6,1},{7,0},{8,15},{9,14},{10,... | collective-permute-start | bytes 417800 | tf_op jit(solution)/shard_map/ppermute | solution.py:291
  33.6 6.9 %copy-start.13 = (f32[2,136,128]{2,1,0:T(8,128)}, f32[2,136,128]{2,1,0:T(8,128)S(1)}, u32[]{:S(2)}) copy-start(f32[2,136,128]{2,1,0:T(8,128)S(1)} %collective-permute-done.2.rest_2_) | copy-start | bytes 417796
  33.6 6.9 %copy-start.14 = (f32[2,136,128]{2,1,0:T(8,128)}, f32[2,136,128]{2,1,0:T(8,128)S(1)}, u32[]{:S(2)}) copy-start(f32[2,136,128]{2,1,0:T(8,128)S(1)} %collective-permute-done.3.rest_3_) | copy-start | bytes 417796
  33.6 6.9 %copy-start.15 = (f32[2,136,128]{2,1,0:T(8,128)}, f32[2,136,128]{2,1,0:T(8,128)S(1)}, u32[]{:S(2)}) copy-start(f32[2,136,128]{2,1,0:T(8,128)S(1)} %collective-permute-done.4.rest_4_) | copy-start | bytes 417796
  43.8 6.7 %copy-start = (bf16[2,2,256,256]{3,2,1,0:T(8,128)(2,1)S(1)}, bf16[2,2,256,256]{3,2,1,0:T(8,128)(2,1)}, u32[]{:S(2)}) copy-start(bf16[2,2,256,256]{3,2,1,0:T(8,128)(2,1)} %constant.22.clone.col_fwd) | copy-start | bytes 1572868
  43.8 7.8 %copy-start.3 = (bf16[2,256,384]{2,1,0:T(8,128)(2,1)S(1)}, bf16[2,256,384]{2,1,0:T(8,128)(2,1)}, u32[]{:S(2)}) copy-start(bf16[2,256,384]{2,1,0:T(8,128)(2,1)} %constant.24.clone.row_inv) | copy-start | bytes 1179652
  44.8 6.8 %collective-permute-start.7 = (f32[8,64,128]{2,1,0:T(8,128)S(1)}, f32[8,64,128]{2,1,0:T(8,128)S(1)}, u32[]{:S(2)}, u32[]{:S(2)}) collective-permute-start(f32[8,64,128]{2,1,0:T(8,128)S(1)} %get-tuple-element.41), channel_id=1, source_target_pairs={{0,1},{1,0},{2,3},{3,2},{4,5},{5,4},{6,7},{7,6},{8,9},{9,8},{10,11... | collective-permute-start | bytes 786440 | tf_op jit(solution)/shard_map/ppermute | solution.py:348
  45.2 6.4 %collective-permute-start.8 = (f32[8,64,128]{2,1,0:T(8,128)S(1)}, f32[8,64,128]{2,1,0:T(8,128)S(1)}, u32[]{:S(2)}, u32[]{:S(2)}) collective-permute-start(f32[8,64,128]{2,1,0:T(8,128)S(1)} %get-tuple-element.43), channel_id=1, source_target_pairs={{1,2},{3,4},{5,6},{2,1},{4,3},{6,5},{9,10},{11,12},{13,14},{10,9},... | collective-permute-start | bytes 786440 | tf_op jit(solution)/shard_map/ppermute | solution.py:347
  46.0 17.3 %collective-permute-start.12 = (f32[256,256]{1,0:T(8,128)S(1)}, f32[256,256]{1,0:T(8,128)S(1)}, u32[]{:S(2)}, u32[]{:S(2)}) collective-permute-start(f32[256,256]{1,0:T(8,128)S(1)} %get-tuple-element.37.rest_0_), channel_id=1, source_target_pairs={{0,24},{8,16},{16,8},{24,0},{1,25},{9,17},{17,9},{25,1},{2,26},{10... | collective-permute-start | bytes 786440 | tf_op jit(solution)/shard_map/ppermute | solution.py:262
  49.7 33.8 %collective-permute-start.13 = (f32[256,256]{1,0:T(8,128)S(1)}, f32[256,256]{1,0:T(8,128)S(1)}, u32[]{:S(2)}, u32[]{:S(2)}) collective-permute-start(f32[256,256]{1,0:T(8,128)S(1)} %get-tuple-element.38.rest_1_.rest_0_), channel_id=1, source_target_pairs={{0,16},{8,24},{16,0},{24,8},{1,17},{9,25},{17,1},{25,9},{2,18},{10... | collective-permute-start | bytes 786440 | tf_op jit(solution)/shard_map/ppermute | solution.py:262
  49.7 33.8 %collective-permute-start.14 = (f32[256,256]{1,0:T(8,128)S(1)}, f32[256,256]{1,0:T(8,128)S(1)}, u32[]{:S(2)}, u32[]{:S(2)}) collective-permute-start(f32[256,256]{1,0:T(8,128)S(1)} %get-tuple-element.39.rest_2_.rest_1_), channel_id=1, source_target_pairs={{0,8},{8,0},{16,24},{24,16},{1,9},{9,1},{17,25},{25,17},{2,10},{10... | collective-permute-start | bytes 786440 | tf_op jit(solution)/shard_map/ppermute | solution.py:262
  54.6 31.9 %collective-permute-start.9 = (f32[256,256]{1,0:T(8,128)S(1)}, f32[256,256]{1,0:T(8,128)S(1)}, u32[]{:S(2)}, u32[]{:S(2)}) collective-permute-start(f32[256,256]{1,0:T(8,128)S(1)} %shard_map.150), channel_id=1, source_target_pairs={{0,24},{8,16},{16,8},{24,0},{1,25},{9,17},{17,9},{25,1},{2,26},{10... | collective-permute-start | bytes 786440 | tf_op jit(solution)/shard_map/ppermute | solution.py:262
  63.3 31.4 %collective-permute-start.10 = (f32[256,256]{1,0:T(8,128)S(1)}, f32[256,256]{1,0:T(8,128)S(1)}, u32[]{:S(2)}, u32[]{:S(2)}) collective-permute-start(f32[256,256]{1,0:T(8,128)S(1)} %get-tuple-element.44), channel_id=1, source_target_pairs={{0,16},{8,24},{16,0},{24,8},{1,17},{9,25},{17,1},{25,9},{2,18},{10... | collective-permute-start | bytes 786440 | tf_op jit(solution)/shard_map/ppermute | solution.py:262
  63.4 31.4 %collective-permute-start.11 = (f32[256,256]{1,0:T(8,128)S(1)}, f32[256,256]{1,0:T(8,128)S(1)}, u32[]{:S(2)}, u32[]{:S(2)}) collective-permute-start(f32[256,256]{1,0:T(8,128)S(1)} %get-tuple-element.45), channel_id=1, source_target_pairs={{0,8},{8,0},{16,24},{24,16},{1,9},{9,1},{17,25},{25,17},{2,10},{10... | collective-permute-start | bytes 786440 | tf_op jit(solution)/shard_map/ppermute | solution.py:262
  83.6 11.2 %copy-start.10 = (f32[256,256]{1,0:T(8,128)}, f32[256,256]{1,0:T(8,128)S(1)}, u32[]{:S(2)}) copy-start(f32[256,256]{1,0:T(8,128)S(1)} %add_add_fusion) | copy-start | bytes 786436
  (10 other events, 36.5 us)

commit v7 on v6

--- a/solution.py
+++ b/solution.py
@@ -15,7 +15,7 @@
 BC = 8
 CAP = 2
 LANES = 128
-VMEM_BYTES = 12 * 2**20
+VMEM_BYTES = 8 * 2**20
 META = 8
 
 
@@ -119,11 +119,6 @@
     return jnp.where(valid, ivar, 0.0)
 
 
-def warp(plane, rows, cols):
-    mid = dot(data(plane, 1), weights(cols, 1), ((1,), (1,)))
-    return dot(weights(rows, 1), data(mid, 0))
-
-
 def run(copies):
     for copy in copies:
         copy.start()
@@ -131,31 +126,30 @@
         copy.wait()
 
 
-def warp_weight_body(ids, owner, slot, extent, ivar_far, rows_far, cols_far, flux_far, *rest):
-    *outs, ivar, rows, cols, flux, send, sems = rest
+def warp_body(ids, owner, slot, extent, ivar_far, rows_far, cols_far, flux_far, *rest):
+    *outs, flux_out, ivar, rows, cols, flux, send, sems = rest
     side = ivar.shape[3]
-    later = pltpu.make_async_copy(flux_far, flux, sems.at[3])
-    far = (ivar_far, rows_far, cols_far)
-    copies = [pltpu.make_async_copy(a, b, sems.at[n]) for n, (a, b) in enumerate(zip(far, (ivar, rows, cols)))]
-    for copy in [*copies, later]:
+    far = (ivar_far, rows_far, cols_far, flux_far)
+    near = (ivar, rows, cols, flux)
+    copies = [pltpu.make_async_copy(a, b, sems.at[n]) for n, (a, b) in enumerate(zip(far, near))]
+    for copy in copies:
         copy.start()
     for d in range(len(outs)):
         for rank in range(CAP):
             send[d, rank, side:, :] = jnp.full((META, side), -1.0, F32)
     for copy in copies:
         copy.wait()
-    for q, to, _, rank, at in places(ids, owner, slot):
-        send[to, rank, :side, :] = warp(masked(extent, ivar[0, 0, q], q), rows[0, 0, q], cols[0, 0, q])
+    for q, to, own, rank, at in places(ids, owner, slot):
+        weighted = masked(extent, ivar[0, 0, q], q)
+        planes = jnp.concatenate([weighted * flux[0, 0, q], weighted], 0)
+        mid = dot(data(planes, 1), weights(cols[0, 0, q], 1), ((1,), (1,)))
+        mid = jnp.concatenate([mid[:side], mid[side:]], 1)
+        done = dot(weights(rows[0, 0, q], 1), data(mid, 0))
+        flux_out[own * CAP + rank] = done[:, :side]
+        send[to, rank, :side, :] = done[:, side:]
         send[to, rank, side:, :] = jnp.full((META, side), at.astype(F32), F32)
     for d, out in enumerate(outs):
         out[...] = send[d]
-    later.wait()
-
-
-def warp_flux_body(ids, owner, slot, extent, ivar, rows, cols, flux, out):
-    for q, _, own, rank, _ in places(ids, owner, slot):
-        plane = masked(extent, ivar[0, 0, q], q) * flux[0, 0, q]
-        out[own * CAP + rank] = warp(plane, rows[0, 0, q], cols[0, 0, q])
 
 
 def weight_body(ids, own, *rest):
@@ -262,6 +256,10 @@
     return lax.ppermute(tile, "visit", [(v, v ^ (visits - 1 - k)) for v in range(visits)])
 
 
+def send_part(tile, route):
+    return lax.ppermute(tile, "visit", route)
+
+
 def coadd_patches(piece_flux, piece_ivar, warp_rows, warp_cols, piece_owner, piece_slot, piece_extent, basis, coeffs):
     owners = lax.axis_size("bulk")
     visits = lax.axis_size("visit")
@@ -275,7 +273,7 @@
     ids = jnp.stack([lax.axis_index("bulk"), lax.axis_index("visit")]).astype(jnp.int32)
     facts = (ids, piece_owner.transpose(0, 1, 3, 2), piece_slot, piece_extent.transpose(0, 1, 3, 2))
 
-    params = pltpu.CompilerParams(vmem_limit_bytes=VMEM_BYTES)
+    params = pltpu.CompilerParams(vmem_limit_bytes=VMEM_BYTES + 12 * 4 * piece_flux.size)
 
     def arr(*shape):
         return jax.ShapeDtypeStruct(shape, F32)
@@ -291,24 +289,17 @@
             got.append(lax.ppermute(sent[d], "bulk", [(i, i ^ d) for i in range(owners)]))
         return got
 
-    *sent_weight, ivar_near, rows_near, cols_near, flux_near = pl.pallas_call(
-        warp_weight_body,
-        out_shape=[arr(CAP, side + META, side)] * owners + [arr(*piece_flux.shape)] * 4,
+    *sent_weight, sent_flux = pl.pallas_call(
+        warp_body,
+        out_shape=[arr(CAP, side + META, side)] * owners + [arr(cap, side, side)],
         in_specs=[SMEM] * 4 + [hbm] * 4,
-        out_specs=[VMEM] * (owners + 4),
-        scratch_shapes=[pltpu.VMEM((owners, CAP, side + META, side), F32), pltpu.SemaphoreType.DMA((4,))],
+        out_specs=[VMEM] * (owners + 1),
+        scratch_shapes=[pltpu.VMEM(piece_flux.shape, F32)] * 4
+        + [pltpu.VMEM((owners, CAP, side + META, side), F32), pltpu.SemaphoreType.DMA((4,))],
         compiler_params=params,
-        name="warp_weight",
+        name="warp",
     )(*facts, *in_hbm(piece_ivar, warp_rows, warp_cols, piece_flux))
     got_weight = exchange(sent_weight)
-    sent_flux = pl.pallas_call(
-        warp_flux_body,
-        out_shape=arr(cap, side, side),
-        in_specs=[SMEM] * 4 + [VMEM] * 4,
-        out_specs=VMEM,
-        compiler_params=params,
-        name="warp_flux",
-    )(*facts, ivar_near, rows_near, cols_near, flux_near)
     got_flux = lax.all_to_all(sent_flux, "bulk", split_axis=0, concat_axis=0, tiled=True)
     spec = pl.pallas_call(
         spectrum_body,
@@ -357,12 +348,18 @@
             compiler_params=params,
         )(ids, near, image, far, spec, row_fwd, col_fwd, col_inv, row_inv, *ivar[first : first + count])
 
-    last = visits - 1
-    parts = convolve(0, 1)
-    got = [send_tile(parts[0], 0)]
-    parts = convolve(1, visits - 2)
-    got += [send_tile(part, k + 1) for k, part in enumerate(parts)]
-    numerator = functools.reduce(jnp.add, got, convolve(last, 1)[0])
+    first, *_ = convolve(0, 1)
+    if visits == 4:
+        joining = send_part(first, [(0, 1), (3, 2)])
+        got = [send_part(first, [(1, 2), (2, 1)])]
+        second, third = convolve(1, 2)
+        got.append(send_part(third, [(0, 1), (1, 0), (2, 3), (3, 2)]))
+        got.append(send_part(second + joining, [(0, 2), (1, 3), (2, 0), (3, 1)]))
+    else:
+        got = [send_tile(first, 0)]
+        middle = convolve(1, visits - 2)
+        got += [send_tile(part, k + 1) for k, part in enumerate(middle)]
+    numerator = functools.reduce(jnp.add, got, convolve(visits - 1, 1)[0])
     return (numerator / jnp.maximum(weight_map, 1.0), weight_map)
 
 

time: 96.1 us -> 102 us (1.061)
  the two profiles are of different devices: /device:TPU:0 before, /device:TPU:2 now
where the time goes in v7:
time: 102 us; the launch traced here: 101 us
  waiting for transfers between devices  51.3 us (50%)
  starting transfers between devices  26.1 us (26%)
  Pallas kernels  20.8 us (20%)
  local copies, waits for them, and re-layouts  1.37 us (1%)
    ppermute x7, waiting for transfers between devices, exchange(): lax.ppermute(sent[d], 'bulk', [(i, i ^ d) for i in range(owners)])  18.7 us
    ppermute x4, waiting for transfers between devices, send_part(): return lax.ppermute(tile, 'visit', route)  14 us
    ppermute x3, waiting for transfers between devices, send_tile(): lax.ppermute(tile, 'visit', [(v, v ^ visits - 1 - k) for v in range(visit...  13.3 us
    pallas_call x3, Pallas kernels, convolve(): pl.pallas_call(functools.partial(conv_body, first, visits), out_shape=[ti...  10.9 us
    ppermute x4, starting transfers between devices, send_part(): return lax.ppermute(tile, 'visit', route)  7.12 us
    ppermute x7, starting transfers between devices, exchange(): lax.ppermute(sent[d], 'bulk', [(i, i ^ d) for i in range(owners)])  6.57 us
    ppermute x1, waiting for transfers between devices, coadd_patches(): far = lax.ppermute(far, 'bulk', pairs + [(j, i) for i, j in pairs])  5.23 us
    pallas_call x1, Pallas kernels, coadd_patches(): pl.pallas_call(warp_body, out_shape=[arr(CAP, side + META, side)] * owner...  5.22 us
  transfers between devices with their start and end apart: 17, of which 10 were waited for; matrix products, arithmetic and copies ran while one was open for 0% of the time, Pallas kernels for 12%

profile of v7, /device:TPU:2, one launch (start us, length us, event | category | flops | bytes accessed | tf_op | source)
XLA Modules:
  0.0 101.4 jit_solution(1277890099938711152)
XLA Ops:
  1.4 5.2 %warp.1 = (f32[2,136,128]{2,1,0:T(8,128)S(1)}, f32[2,136,128]{2,1,0:T(8,128)S(1)}, f32[2,136,128]{2,1,0:T(8,128)S(1)}, f32[2,136,128]{2,1,0:T(8,128)S(1)}, f32[2...) custom-call(s32[2]{0:T(128)S(1)} %pad_add_fusion.ids, ...), custom_call_target="tpu_custom_call" | custom-call | tf_op jit(solution)/shard_map/warp/pallas_call | solution.py:292
  6.6 4.3 %all-to-all-start = ((f32[16,128,128]{2,1,0:T(8,128)}), f32[16,128,128]{2,1,0:T(8,128)S(1)}, u32[]{:S(2)}, u32[]{:S(2)}) async-start(f32[16,128,128]{2,1,0:T(8,128)} %get-tuple-element.30), calls=%async_computation | async-start | bytes 2097152 | tf_op jit(solution)/shard_map/all_to_all | solution.py:303
  11.4 1.4 %collective-permute-start.2 = (f32[2,136,128]{2,1,0:T(8,128)S(1)}, f32[2,136,128]{2,1,0:T(8,128)S(1)}, u32[]{:S(2)}, u32[]{:S(2)}) collective-permute-start(f32[2,136,128]{2,1,0:T(8,128)S(1)} %get-tuple-element.24), channel_id=1, source_target_pairs={{0,3},{1,2},{2,1},{3,0},{4,7},{5,6},{6,5},{7,4},{8,11},{9,10},{10,... | collective-permute-start | bytes 417800 | tf_op jit(solution)/shard_map/ppermute | solution.py:289
  12.8 1.5 %collective-permute-start.3 = (f32[2,136,128]{2,1,0:T(8,128)S(1)}, f32[2,136,128]{2,1,0:T(8,128)S(1)}, u32[]{:S(2)}, u32[]{:S(2)}) collective-permute-start(f32[2,136,128]{2,1,0:T(8,128)S(1)} %get-tuple-element.25), channel_id=1, source_target_pairs={{0,4},{1,5},{2,6},{3,7},{4,0},{5,1},{6,2},{7,3},{8,12},{9,13},{10,... | collective-permute-start | bytes 417800 | tf_op jit(solution)/shard_map/ppermute | solution.py:289
  14.5 1.5 %collective-permute-start.5 = (f32[2,136,128]{2,1,0:T(8,128)S(1)}, f32[2,136,128]{2,1,0:T(8,128)S(1)}, u32[]{:S(2)}, u32[]{:S(2)}) collective-permute-start(f32[2,136,128]{2,1,0:T(8,128)S(1)} %get-tuple-element.27), channel_id=1, source_target_pairs={{0,6},{1,7},{2,4},{3,5},{4,2},{5,3},{6,0},{7,1},{8,14},{9,15},{10,... | collective-permute-start | bytes 417800 | tf_op jit(solution)/shard_map/ppermute | solution.py:289
  16.0 11.0 %collective-permute-done.1.rest_1_ = f32[2,136,128]{2,1,0:T(8,128)S(1)} collective-permute-done((f32[2,136,128]{2,1,0:T(8,128)S(1)}, f32[2,136,128]{2,1,0:T(8,128)S(1)}, u32[]{:S(2)}, u32[]{:S(2)}) %collective-permute-start.1) | collective-permute-done | bytes 139296 | tf_op jit(solution)/shard_map/ppermute | solution.py:289
  27.0 1.5 %collective-permute-start.6 = (f32[2,136,128]{2,1,0:T(8,128)S(1)}, f32[2,136,128]{2,1,0:T(8,128)S(1)}, u32[]{:S(2)}, u32[]{:S(2)}) collective-permute-start(f32[2,136,128]{2,1,0:T(8,128)S(1)} %get-tuple-element.28), channel_id=1, source_target_pairs={{0,7},{1,6},{2,5},{3,4},{4,3},{5,2},{6,1},{7,0},{8,15},{9,14},{10,... | collective-permute-start | bytes 417800 | tf_op jit(solution)/shard_map/ppermute | solution.py:289
  29.6 1.5 %collective-permute-done.4.rest_4_ = f32[2,136,128]{2,1,0:T(8,128)S(1)} collective-permute-done((f32[2,136,128]{2,1,0:T(8,128)S(1)}, f32[2,136,128]{2,1,0:T(8,128)S(1)}, u32[]{:S(2)}, u32[]{:S(2)}) %collective-permute-start.4) | collective-permute-done | bytes 139296 | tf_op jit(solution)/shard_map/ppermute | solution.py:289
  31.1 3.3 %collective-permute-done.5.rest_5_ = f32[2,136,128]{2,1,0:T(8,128)S(1)} collective-permute-done((f32[2,136,128]{2,1,0:T(8,128)S(1)}, f32[2,136,128]{2,1,0:T(8,128)S(1)}, u32[]{:S(2)}, u32[]{:S(2)}) %collective-permute-start.5) | collective-permute-done | bytes 139296 | tf_op jit(solution)/shard_map/ppermute | solution.py:289
  34.4 1.8 %collective-permute-done.6.rest_6_ = f32[2,136,128]{2,1,0:T(8,128)S(1)} collective-permute-done((f32[2,136,128]{2,1,0:T(8,128)S(1)}, f32[2,136,128]{2,1,0:T(8,128)S(1)}, u32[]{:S(2)}, u32[]{:S(2)}) %collective-permute-start.6) | collective-permute-done | bytes 139296 | tf_op jit(solution)/shard_map/ppermute | solution.py:289
  36.9 2.7 %weights.1 = (f32[256,256]{1,0:T(8,128)S(1)}, f32[256,256]{1,0:T(8,128)S(1)}, f32[256,256]{1,0:T(8,128)S(1)}, f32[256,256]{1,0:T(8,128)S(1)}, s32[16]{0:T(128)S(1)}) custom-call(s32[2]{0:T(128)S(1)} %pad_add_fusion.ids, f32[2,136,128]{2,1,0:T(8,128)S(1)} %get-tuple-element.21.own, f32[2,136,128]{2,1,0:T(8,128)} %copy-done.11, f32[2,136,128]{2,1,0:T(8,128)} %copy-done.12, ...), custom_call_target="tpu_custom_call" | custom-call | tf_op jit(solution)/shard_map/weights/pallas_call | solution.py:313
  41.0 3.2 %collective-permute-start.8 = (f32[8,64,128]{2,1,0:T(8,128)S(1)}, f32[8,64,128]{2,1,0:T(8,128)S(1)}, u32[]{:S(2)}, u32[]{:S(2)}) collective-permute-start(f32[8,64,128]{2,1,0:T(8,128)S(1)} %get-tuple-element.37), channel_id=1, source_target_pairs={{1,2},{3,4},{5,6},{2,1},{4,3},{6,5},{9,10},{11,12},{13,14},{10,9},... | collective-permute-start | bytes 786440 | tf_op jit(solution)/shard_map/ppermute | solution.py:338
  45.3 5.2 %collective-permute-done.8.far = f32[8,64,128]{2,1,0:T(8,128)S(1)} collective-permute-done((f32[8,64,128]{2,1,0:T(8,128)S(1)}, f32[8,64,128]{2,1,0:T(8,128)S(1)}, u32[]{:S(2)}, u32[]{:S(2)}) %collective-permute-start.8) | collective-permute-done | bytes 262176 | tf_op jit(solution)/shard_map/ppermute | solution.py:338
  50.6 2.9 %shard_map.150 = f32[256,256]{1,0:T(8,128)S(1)} custom-call(s32[2]{0:T(128)S(1)} %pad_add_fusion.ids, f32[8,64,128]{2,1,0:T(8,128)S(1)} %collective-permute-done.7.near, f32[8,256,128]{2,1,0:T(8,128)S(1)} %get-tuple-element.36.image, f32[8,64,128]{2,1,0:T(8,128)S(1)} %collective-permute-done.8.far, f32[2,192,256]{2,1,0:T(8,128)S(1)} %spectrum.1.spec, ...), custom_call_target="tpu_custom_call" | custom-call | tf_op jit(solution)/shard_map/pallas_call | solution.py:342
  53.5 3.5 %collective-permute-start.11 = (f32[256,256]{1,0:T(8,128)S(1)}, f32[256,256]{1,0:T(8,128)S(1)}, u32[]{:S(2)}, u32[]{:S(2)}) collective-permute-start(f32[256,256]{1,0:T(8,128)S(1)} %shard_map.150), channel_id=1, source_target_pairs={{0,8},{24,16},{1,9},{25,17},{2,10},{26,18},{3,11},{27,19},{4,12},{... | collective-permute-start | bytes 786440 | tf_op jit(solution)/shard_map/ppermute | solution.py:260
  57.1 3.0 %collective-permute-start.14 = (f32[256,256]{1,0:T(8,128)S(1)}, f32[256,256]{1,0:T(8,128)S(1)}, u32[]{:S(2)}, u32[]{:S(2)}) collective-permute-start(f32[256,256]{1,0:T(8,128)S(1)} %get-tuple-element.32.rest_1_.rest_0_), channel_id=1, source_target_pairs={{0,16},{8,24},{16,0},{24,8},{1,17},{9,25},{17,1},{25,9},{2,18},{10... | collective-permute-start | bytes 786440 | tf_op jit(solution)/shard_map/ppermute | solution.py:256
  60.1 1.4 %collective-permute-start.13 = (f32[256,256]{1,0:T(8,128)S(1)}, f32[256,256]{1,0:T(8,128)S(1)}, u32[]{:S(2)}, u32[]{:S(2)}) collective-permute-start(f32[256,256]{1,0:T(8,128)S(1)} %get-tuple-element.31.rest_0_), channel_id=1, source_target_pairs={{0,24},{8,16},{16,8},{24,0},{1,25},{9,17},{17,9},{25,1},{2,26},{10... | collective-permute-start | bytes 786440 | tf_op jit(solution)/shard_map/ppermute | solution.py:256
  62.2 5.0 %shard_map.151 = (f32[256,256]{1,0:T(8,128)S(1)}, f32[256,256]{1,0:T(8,128)S(1)}) custom-call(s32[2]{0:T(128)S(1)} %pad_add_fusion.ids, f32[8,64,128]{2,1,0:T(8,128)S(1)} %collective-permute-done.7.near, f32[8,256,128]{2,1,0:T(8,128)S(1)} %get-tuple-element.36.image, f32[8,64,128]{2,1,0:T(8,128)S(1)} %collective-permute-done.8.far, ...), custom_call_target="tpu_custom_call" | custom-call | tf_op jit(solution)/shard_map/pallas_call | solution.py:342
  67.2 2.0 %collective-permute-start.10 = (f32[256,256]{1,0:T(8,128)S(1)}, f32[256,256]{1,0:T(8,128)S(1)}, u32[]{:S(2)}, u32[]{:S(2)}) collective-permute-start(f32[256,256]{1,0:T(8,128)S(1)} %get-tuple-element.38), channel_id=1, source_target_pairs={{0,8},{8,0},{16,24},{24,16},{1,9},{9,1},{17,25},{25,17},{2,10},{10... | collective-permute-start | bytes 786440 | tf_op jit(solution)/shard_map/ppermute | solution.py:260
  69.3 2.6 %collective-permute-done.15 = f32[256,256]{1,0:T(8,128)S(1)} collective-permute-done((f32[256,256]{1,0:T(8,128)S(1)}, f32[256,256]{1,0:T(8,128)S(1)}, u32[]{:S(2)}, u32[]{:S(2)}) %collective-permute-start.15) | collective-permute-done | bytes 262176 | tf_op jit(solution)/shard_map/ppermute | solution.py:256
  72.8 2.2 %collective-permute-done.14 = f32[256,256]{1,0:T(8,128)S(1)} collective-permute-done((f32[256,256]{1,0:T(8,128)S(1)}, f32[256,256]{1,0:T(8,128)S(1)}, u32[]{:S(2)}, u32[]{:S(2)}) %collective-permute-start.14) | collective-permute-done | bytes 262176 | tf_op jit(solution)/shard_map/ppermute | solution.py:256
  75.0 8.5 %collective-permute-done.13 = f32[256,256]{1,0:T(8,128)S(1)} collective-permute-done((f32[256,256]{1,0:T(8,128)S(1)}, f32[256,256]{1,0:T(8,128)S(1)}, u32[]{:S(2)}, u32[]{:S(2)}) %collective-permute-start.13) | collective-permute-done | bytes 262176 | tf_op jit(solution)/shard_map/ppermute | solution.py:256
  83.6 2.9 %shard_map.149 = f32[256,256]{1,0:T(8,128)S(1)} custom-call(s32[2]{0:T(128)S(1)} %pad_add_fusion.ids, f32[8,64,128]{2,1,0:T(8,128)S(1)} %collective-permute-done.7.near, f32[8,256,128]{2,1,0:T(8,128)S(1)} %get-tuple-element.36.image, f32[8,64,128]{2,1,0:T(8,128)S(1)} %collective-permute-done.8.far, f32[2,192,256]{2,1,0:T(8,128)S(1)} %spectrum.1.spec, ...), custom_call_target="tpu_custom_call" | custom-call | tf_op jit(solution)/shard_map/pallas_call | solution.py:342
  86.6 14.0 %collective-permute-done.12 = f32[256,256]{1,0:T(8,128)S(1)} collective-permute-done((f32[256,256]{1,0:T(8,128)S(1)}, f32[256,256]{1,0:T(8,128)S(1)}, u32[]{:S(2)}, u32[]{:S(2)}) %collective-permute-start.12) | collective-permute-done | bytes 262176 | tf_op jit(solution)/shard_map/ppermute | solution.py:260
  (57 shorter events, 8.4 us)
Async XLA Ops:
  6.6 32.9 %all-to-all-start = ((f32[16,128,128]{2,1,0:T(8,128)}), f32[16,128,128]{2,1,0:T(8,128)S(1)}, u32[]{:S(2)}, u32[]{:S(2)}) async-start(f32[16,128,128]{2,1,0:T(8,128)} %get-tuple-element.30), calls=%async_computation | async-start | bytes 2097152 | tf_op jit(solution)/shard_map/all_to_all | solution.py:303
  10.9 3.6 %collective-permute-start = (f32[2,136,128]{2,1,0:T(8,128)S(1)}, f32[2,136,128]{2,1,0:T(8,128)S(1)}, u32[]{:S(2)}, u32[]{:S(2)}) collective-permute-start(f32[2,136,128]{2,1,0:T(8,128)S(1)} %get-tuple-element.22), channel_id=1, source_target_pairs={{0,1},{1,0},{2,3},{3,2},{4,5},{5,4},{6,7},{7,6},{8,9},{9,8},{10,11... | collective-permute-start | bytes 417800 | tf_op jit(solution)/shard_map/ppermute | solution.py:289
  11.0 15.9 %collective-permute-start.1 = (f32[2,136,128]{2,1,0:T(8,128)S(1)}, f32[2,136,128]{2,1,0:T(8,128)S(1)}, u32[]{:S(2)}, u32[]{:S(2)}) collective-permute-start(f32[2,136,128]{2,1,0:T(8,128)S(1)} %get-tuple-element.23), channel_id=1, source_target_pairs={{0,2},{1,3},{2,0},{3,1},{4,6},{5,7},{6,4},{7,5},{8,10},{9,11},{10,... | collective-permute-start | bytes 417800 | tf_op jit(solution)/shard_map/ppermute | solution.py:289
  11.4 18.2 %collective-permute-start.2 = (f32[2,136,128]{2,1,0:T(8,128)S(1)}, f32[2,136,128]{2,1,0:T(8,128)S(1)}, u32[]{:S(2)}, u32[]{:S(2)}) collective-permute-start(f32[2,136,128]{2,1,0:T(8,128)S(1)} %get-tuple-element.24), channel_id=1, source_target_pairs={{0,3},{1,2},{2,1},{3,0},{4,7},{5,6},{6,5},{7,4},{8,11},{9,10},{10,... | collective-permute-start | bytes 417800 | tf_op jit(solution)/shard_map/ppermute | solution.py:289
  12.8 16.8 %collective-permute-start.3 = (f32[2,136,128]{2,1,0:T(8,128)S(1)}, f32[2,136,128]{2,1,0:T(8,128)S(1)}, u32[]{:S(2)}, u32[]{:S(2)}) collective-permute-start(f32[2,136,128]{2,1,0:T(8,128)S(1)} %get-tuple-element.25), channel_id=1, source_target_pairs={{0,4},{1,5},{2,6},{3,7},{4,0},{5,1},{6,2},{7,3},{8,12},{9,13},{10,... | collective-permute-start | bytes 417800 | tf_op jit(solution)/shard_map/ppermute | solution.py:289
  14.2 16.9 %collective-permute-start.4 = (f32[2,136,128]{2,1,0:T(8,128)S(1)}, f32[2,136,128]{2,1,0:T(8,128)S(1)}, u32[]{:S(2)}, u32[]{:S(2)}) collective-permute-start(f32[2,136,128]{2,1,0:T(8,128)S(1)} %get-tuple-element.26), channel_id=1, source_target_pairs={{0,5},{1,4},{2,7},{3,6},{4,1},{5,0},{6,3},{7,2},{8,13},{9,12},{10,... | collective-permute-start | bytes 417800 | tf_op jit(solution)/shard_map/ppermute | solution.py:289
  14.5 21.7 %copy-start.11 = (f32[2,136,128]{2,1,0:T(8,128)}, f32[2,136,128]{2,1,0:T(8,128)S(1)}, u32[]{:S(2)}) copy-start(f32[2,136,128]{2,1,0:T(8,128)S(1)} %collective-permute-done.rest_0_) | copy-start | bytes 417796
  14.5 19.9 %collective-permute-start.5 = (f32[2,136,128]{2,1,0:T(8,128)S(1)}, f32[2,136,128]{2,1,0:T(8,128)S(1)}, u32[]{:S(2)}, u32[]{:S(2)}) collective-permute-start(f32[2,136,128]{2,1,0:T(8,128)S(1)} %get-tuple-element.27), channel_id=1, source_target_pairs={{0,6},{1,7},{2,4},{3,5},{4,2},{5,3},{6,0},{7,1},{8,14},{9,15},{10,... | collective-permute-start | bytes 417800 | tf_op jit(solution)/shard_map/ppermute | solution.py:289
  27.0 9.3 %copy-start.12 = (f32[2,136,128]{2,1,0:T(8,128)}, f32[2,136,128]{2,1,0:T(8,128)S(1)}, u32[]{:S(2)}) copy-start(f32[2,136,128]{2,1,0:T(8,128)S(1)} %collective-permute-done.1.rest_1_) | copy-start | bytes 417796
  27.0 9.3 %collective-permute-start.6 = (f32[2,136,128]{2,1,0:T(8,128)S(1)}, f32[2,136,128]{2,1,0:T(8,128)S(1)}, u32[]{:S(2)}, u32[]{:S(2)}) collective-permute-start(f32[2,136,128]{2,1,0:T(8,128)S(1)} %get-tuple-element.28), channel_id=1, source_target_pairs={{0,7},{1,6},{2,5},{3,4},{4,3},{5,2},{6,1},{7,0},{8,15},{9,14},{10,... | collective-permute-start | bytes 417800 | tf_op jit(solution)/shard_map/ppermute | solution.py:289
  29.6 6.7 %copy-start.14 = (f32[2,136,128]{2,1,0:T(8,128)}, f32[2,136,128]{2,1,0:T(8,128)S(1)}, u32[]{:S(2)}) copy-start(f32[2,136,128]{2,1,0:T(8,128)S(1)} %collective-permute-done.3.rest_3_) | copy-start | bytes 417796
  39.6 11.0 %copy-start.3 = (bf16[2,256,384]{2,1,0:T(8,128)(2,1)S(1)}, bf16[2,256,384]{2,1,0:T(8,128)(2,1)}, u32[]{:S(2)}) copy-start(bf16[2,256,384]{2,1,0:T(8,128)(2,1)} %constant.24.clone.row_inv) | copy-start | bytes 1179652
  40.5 4.8 %collective-permute-start.7 = (f32[8,64,128]{2,1,0:T(8,128)S(1)}, f32[8,64,128]{2,1,0:T(8,128)S(1)}, u32[]{:S(2)}, u32[]{:S(2)}) collective-permute-start(f32[8,64,128]{2,1,0:T(8,128)S(1)} %get-tuple-element.35), channel_id=1, source_target_pairs={{0,1},{1,0},{2,3},{3,2},{4,5},{5,4},{6,7},{7,6},{8,9},{9,8},{10,11... | collective-permute-start | bytes 786440 | tf_op jit(solution)/shard_map/ppermute | solution.py:339
  41.0 9.6 %copy-start.1 = (bf16[2,384,384]{2,1,0:T(8,128)(2,1)S(1)}, bf16[2,384,384]{2,1,0:T(8,128)(2,1)}, u32[]{:S(2)}) copy-start(bf16[2,384,384]{2,1,0:T(8,128)(2,1)} %constant.20.clone.row_fwd) | copy-start | bytes 1769476
  41.0 9.6 %copy-start.2 = (bf16[2,2,256,256]{3,2,1,0:T(8,128)(2,1)S(1)}, bf16[2,2,256,256]{3,2,1,0:T(8,128)(2,1)}, u32[]{:S(2)}) copy-start(bf16[2,2,256,256]{3,2,1,0:T(8,128)(2,1)} %constant.23.clone.col_inv) | copy-start | bytes 1572868
  41.0 9.6 %collective-permute-start.8 = (f32[8,64,128]{2,1,0:T(8,128)S(1)}, f32[8,64,128]{2,1,0:T(8,128)S(1)}, u32[]{:S(2)}, u32[]{:S(2)}) collective-permute-start(f32[8,64,128]{2,1,0:T(8,128)S(1)} %get-tuple-element.37), channel_id=1, source_target_pairs={{1,2},{3,4},{5,6},{2,1},{4,3},{6,5},{9,10},{11,12},{13,14},{10,9},... | collective-permute-start | bytes 786440 | tf_op jit(solution)/shard_map/ppermute | solution.py:338
  53.5 13.7 %collective-permute-start.11 = (f32[256,256]{1,0:T(8,128)S(1)}, f32[256,256]{1,0:T(8,128)S(1)}, u32[]{:S(2)}, u32[]{:S(2)}) collective-permute-start(f32[256,256]{1,0:T(8,128)S(1)} %shard_map.150), channel_id=1, source_target_pairs={{0,8},{24,16},{1,9},{25,17},{2,10},{26,18},{3,11},{27,19},{4,12},{... | collective-permute-start | bytes 786440 | tf_op jit(solution)/shard_map/ppermute | solution.py:260
  57.0 14.9 %collective-permute-start.15 = (f32[256,256]{1,0:T(8,128)S(1)}, f32[256,256]{1,0:T(8,128)S(1)}, u32[]{:S(2)}, u32[]{:S(2)}) collective-permute-start(f32[256,256]{1,0:T(8,128)S(1)} %get-tuple-element.33.rest_2_.rest_1_), channel_id=1, source_target_pairs={{0,8},{8,0},{16,24},{24,16},{1,9},{9,1},{17,25},{25,17},{2,10},{10... | collective-permute-start | bytes 786440 | tf_op jit(solution)/shard_map/ppermute | solution.py:256
  57.1 17.9 %collective-permute-start.14 = (f32[256,256]{1,0:T(8,128)S(1)}, f32[256,256]{1,0:T(8,128)S(1)}, u32[]{:S(2)}, u32[]{:S(2)}) collective-permute-start(f32[256,256]{1,0:T(8,128)S(1)} %get-tuple-element.32.rest_1_.rest_0_), channel_id=1, source_target_pairs={{0,16},{8,24},{16,0},{24,8},{1,17},{9,25},{17,1},{25,9},{2,18},{10... | collective-permute-start | bytes 786440 | tf_op jit(solution)/shard_map/ppermute | solution.py:256
  60.1 23.4 %collective-permute-start.13 = (f32[256,256]{1,0:T(8,128)S(1)}, f32[256,256]{1,0:T(8,128)S(1)}, u32[]{:S(2)}, u32[]{:S(2)}) collective-permute-start(f32[256,256]{1,0:T(8,128)S(1)} %get-tuple-element.31.rest_0_), channel_id=1, source_target_pairs={{0,24},{8,16},{16,8},{24,0},{1,25},{9,17},{17,9},{25,1},{2,26},{10... | collective-permute-start | bytes 786440 | tf_op jit(solution)/shard_map/ppermute | solution.py:256
  61.5 25.1 %collective-permute-start.9 = (f32[256,256]{1,0:T(8,128)S(1)}, f32[256,256]{1,0:T(8,128)S(1)}, u32[]{:S(2)}, u32[]{:S(2)}) collective-permute-start(f32[256,256]{1,0:T(8,128)S(1)} %shard_map.150), channel_id=1, source_target_pairs={{8,16},{16,8},{9,17},{17,9},{10,18},{18,10},{11,19},{19,11},{12,20... | collective-permute-start | bytes 786440 | tf_op jit(solution)/shard_map/ppermute | solution.py:260
  67.2 19.3 %collective-permute-start.10 = (f32[256,256]{1,0:T(8,128)S(1)}, f32[256,256]{1,0:T(8,128)S(1)}, u32[]{:S(2)}, u32[]{:S(2)}) collective-permute-start(f32[256,256]{1,0:T(8,128)S(1)} %get-tuple-element.38), channel_id=1, source_target_pairs={{0,8},{8,0},{16,24},{24,16},{1,9},{9,1},{17,25},{25,17},{2,10},{10... | collective-permute-start | bytes 786440 | tf_op jit(solution)/shard_map/ppermute | solution.py:260
  71.9 28.7 %collective-permute-start.12 = (f32[256,256]{1,0:T(8,128)S(1)}, f32[256,256]{1,0:T(8,128)S(1)}, u32[]{:S(2)}, u32[]{:S(2)}) collective-permute-start(f32[256,256]{1,0:T(8,128)S(1)} %add.23), channel_id=1, source_target_pairs={{0,16},{8,24},{16,0},{24,8},{1,17},{9,25},{17,1},{25,9},{2,18},{10... | collective-permute-start | bytes 786440 | tf_op jit(solution)/shard_map/ppermute | solution.py:260
  83.6 17.0 %copy-start.10 = (f32[256,256]{1,0:T(8,128)}, f32[256,256]{1,0:T(8,128)S(1)}, u32[]{:S(2)}) copy-start(f32[256,256]{1,0:T(8,128)S(1)} %add_add_fusion) | copy-start | bytes 786436
  (11 other events, 34.1 us)
